TPU v7x, 256 devices: a whole 4x4x8 slice. The times are simulated.
256 devices in a mesh: row: 16 (over y_hi, x, core), col: 16 (over y_lo, z).
Axes of the slice: x: 4, y: 4 (y_hi: 2, y_lo: 2; y = y_hi * 2 + y_lo), z: 8, core: 2. Of those that a mesh axis runs over, the one named last changes fastest.
Arguments:
- grad_x: float32 [8192, 8192], P('row', 'col'), may hold values from -6 to 6
- grad_y: float32 [8192, 8192], P('row', 'col'), may hold values from -6 to 6
Outputs:
- field: float32 [8192, 8192], P('row', 'col')
All inputs are finite; a program needn't handle non-finite values.
Results may differ from a plain program's by a relative error of at most 0.0003.
Values sent between devices are 32-bit elements; how exact they have to be, the bound alone decides.
No kernel may reach another device: no remote copies, remote signals or barrier semaphores. Data moves between devices by JAX's collectives and lax.ppermute only.
A program may use at most 64 MiB of HBM per device.

v0:
```python
import math

import jax
import jax.numpy as jnp
from jax import lax
from jax.sharding import PartitionSpec as P

highest = lax.Precision.HIGHEST


def passed_along(block, axis, distance):
    devices = range(lax.axis_size(axis))
    route = [(i - distance, i) for i in devices if i - distance in devices]
    return lax.ppermute(block, axis, route)


def trig_table(numer, modulus, span):
    reduced = (numer % modulus).astype(jnp.float32) * (math.pi / span)
    return (jnp.cos(reduced), jnp.sin(reduced))


def mixing_tables(members):
    target = jnp.arange(members, dtype=jnp.int32)[:, None]
    source = jnp.arange(members, dtype=jnp.int32)[None, :]
    cos_low, sin_low = trig_table(target * source, 2 * members, members)
    cos_high, sin_high = trig_table((target + members) * source, 2 * members, members)
    leading = target == 0
    forward = jnp.stack([cos_low, jnp.where(leading, cos_high, sin_low)], axis=1)
    inverse = jnp.stack([cos_low, jnp.where(leading, cos_high, -sin_low)], axis=0)
    return (forward, inverse)


def class_grids(members, length, index):
    total = members * length
    second = jnp.where(index == 0, members, 2 * members - index)
    levels = jnp.arange(length // 2, dtype=jnp.int32)
    odd_cells = 2 * jnp.arange(length, dtype=jnp.int32) + 1
    grids = []
    frequencies = []
    for start_freq in (index, second):
        freq_rows = start_freq + 2 * members * levels
        cos_grid, sin_grid = trig_table(
            freq_rows[:, None] * odd_cells[None, :], 4 * total, 2 * total
        )
        grids.append(jnp.concatenate([cos_grid, sin_grid], axis=1))
        frequencies.append(freq_rows)
    return (grids, jnp.concatenate(frequencies))


def axis_tables(members, length, index):
    grids, frequencies = class_grids(members, length, index)
    forward, inverse = mixing_tables(members)
    return (grids, frequencies, forward, inverse)


def forward_axis(block, tables, index, spread, mixing):
    grids, frequencies, forward, inverse = tables
    length, breadth = block.shape
    pieces = spread(block.reshape(1, length, breadth))
    partial_sums = jnp.einsum("dcp,pbm->dcbm", forward, pieces, precision=highest)
    channels = mixing(partial_sums)[0]
    leading = index == 0
    real_part = channels[0]
    imag_part = channels[1]
    zeros_like = jnp.zeros_like(real_part)
    inputs = [
        jnp.concatenate([real_part, jnp.where(leading, zeros_like, -imag_part)], 0),
        jnp.concatenate(
            [jnp.where(leading, imag_part, real_part), jnp.where(leading, zeros_like, imag_part)], 0
        ),
    ]
    results = [
        jnp.dot(grid_table, operand, precision=highest)
        for grid_table, operand in zip(grids, inputs)
    ]
    return jnp.concatenate(results, 0)


def inverse_axis(spec, tables, index, spread, mixing):
    grids, frequencies, forward, inverse = tables
    members = inverse.shape[1]
    length, breadth = spec.shape
    halfway = length // 2
    halves = []
    for which, grid_table in enumerate(grids):
        stacked_pair = jnp.dot(
            grid_table.T, spec[which * halfway : (which + 1) * halfway], precision=highest
        )
        halves.append((stacked_pair[:length], stacked_pair[length:]))
    (real_low, imag_low), (real_high, imag_high) = halves
    leading = index == 0
    channels = [
        jnp.where(leading, real_low, real_low + real_high),
        jnp.where(leading, real_high, imag_low - imag_high),
    ]
    stacked = jnp.stack(
        [channel.reshape(members, length // members, breadth) for channel in channels], axis=1
    )
    received = mixing(stacked)
    grouped = received.reshape(len(channels), members, length // members, breadth)
    pieces = jnp.einsum("cdp,cdbm->pbm", inverse, grouped, precision=highest)
    return spread(pieces.reshape(1, length, breadth)).reshape(length, breadth)


def body(grad_x, grad_y):
    above = passed_along(grad_x[-1:, :], "row", 1)
    before = passed_along(grad_y[:, -1:], "col", 1)
    diverge = (
        grad_x
        - jnp.concatenate([above, grad_x[:-1]], 0)
        + (grad_y - jnp.concatenate([before, grad_y[:, :-1]], 1))
    )
    row_members = lax.axis_size("row")
    col_members = lax.axis_size("col")
    row_index = lax.axis_index("row")
    col_index = lax.axis_index("col")
    rows_local, cols_local = diverge.shape

    def row_spread(values):
        return lax.all_to_all(values, "row", split_axis=1, concat_axis=0, tiled=True)

    def col_spread(values):
        return lax.all_to_all(values, "col", split_axis=1, concat_axis=0, tiled=True)

    def row_mixing(values):
        return lax.all_to_all(values, "row", split_axis=0, concat_axis=2, tiled=True)

    def col_mixing(values):
        return lax.all_to_all(values, "col", split_axis=0, concat_axis=2, tiled=True)

    row_tables = axis_tables(row_members, rows_local, row_index)
    col_tables = axis_tables(col_members, cols_local, col_index)
    freq_x = row_tables[1]
    freq_y = col_tables[1]
    spectrum_x = forward_axis(diverge, row_tables, row_index, row_spread, row_mixing)
    spectrum = forward_axis(spectrum_x.T, col_tables, col_index, col_spread, col_mixing)
    total_x = row_members * rows_local
    total_y = col_members * cols_local
    sine_x = jnp.sin(freq_x.astype(jnp.float32) * (math.pi / (2 * total_x)))
    sine_y = jnp.sin(freq_y.astype(jnp.float32) * (math.pi / (2 * total_y)))
    eigen = -4.0 * sine_y[:, None] ** 2 - 4.0 * sine_x[None, :] ** 2
    weight_x = jnp.where(freq_x == 0, 1.0, 2.0) / total_x
    weight_y = jnp.where(freq_y == 0, 1.0, 2.0) / total_y
    anchor = (freq_y == 0)[:, None] & (freq_x == 0)[None, :]
    scaled = (
        jnp.where(anchor, 0.0, spectrum / jnp.where(anchor, 1.0, eigen))
        * weight_y[:, None]
        * weight_x[None, :]
    )
    back_cols = inverse_axis(scaled, col_tables, col_index, col_spread, col_mixing)
    return inverse_axis(back_cols.T, row_tables, row_index, row_spread, row_mixing)


def solution(mesh):
    placed = (P("row", "col"), P("row", "col"))
    return jax.shard_map(
        body, mesh=mesh, in_specs=placed, out_specs=P("row", "col"), check_vma=False
    )
```

profile of v0, /device:TPU:1, one launch (start us, length us, event | category | flops | bytes accessed | tf_op | source)
XLA Modules:
  0.0 370.3 jit_solution(7181798416318112276)
XLA Ops:
  1.1 4.4 %collective-permute-start.1 = (f32[512,1]{1,0:T(8,128)S(1)}, f32[512,1]{1,0:T(8,128)S(1)}, u32[]{:S(2)}, u32[]{:S(2)}) collective-permute-start(f32[512,1]{1,0:T(8,128)S(1)} %slice.66), channel_id=1, source_target_pairs={{0,1},{1,2},{2,3},{3,4},{4,5},{5,6},{6,7},{7,8},{8,9},{9,10},{10,1... | collective-permute-start | bytes 6152 | tf_op jit(solution)/shard_map/ppermute | solution.py:14
  6.2 3.9 %collective-permute-start = (f32[1,512]{1,0:T(1,128)S(1)}, f32[1,512]{1,0:T(1,128)S(1)}, u32[]{:S(2)}, u32[]{:S(2)}) collective-permute-start(f32[1,512]{1,0:T(1,128)S(1)} %slice.64), channel_id=1, source_target_pairs={{0,16},{16,32},{32,48},{48,64},{64,80},{80,96},{96,112},{112,128},... | collective-permute-start | bytes 6152 | tf_op jit(solution)/shard_map/ppermute | solution.py:14
  10.9 2.7 fusion.33
  15.3 9.3 %all-to-all-start = ((f32[1,512,512]{2,0,1:T(1,128)}), f32[1,512,512]{2,0,1:T(1,128)S(1)}, u32[]{:S(2)}, u32[]{:S(2)}) async-start(f32[1,512,512]{2,0,1:T(1,128)} %reshape.479), calls=%async_computation | async-start | bytes 2097152 | tf_op jit(solution)/shard_map/all_to_all | solution.py:120
  24.7 17.1 %all-to-all-done = f32[1,512,512]{2,0,1:T(1,128)S(1)} async-done(((f32[1,512,512]{2,0,1:T(1,128)}), f32[1,512,512]{2,0,1:T(1,128)S(1)}, u32[]{:S(2)}, u32[]{:S(2)}) %all-to-all-start) | async-done | bytes 1048608 | tf_op jit(solution)/shard_map/all_to_all | solution.py:120
  41.9 2.2 fusion.38
  44.1 2.6 copy.22
  46.6 4.3 %all-to-all-start.1 = ((f32[16,2,32,512]{3,2,1,0:T(8,128)}), f32[16,2,32,512]{3,2,1,0:T(8,128)S(1)}, u32[]{:S(2)}, u32[]{:S(2)}) async-start(f32[16,2,32,512]{3,2,1,0:T(8,128)} %copy.22), calls=%async_computation.1 | async-start | bytes 4194304 | tf_op jit(solution)/shard_map/all_to_all | solution.py:126
  50.9 9.7 %fusion.67 = (f32[256,512]{1,0:T(8,128)}, f32[256,512]{1,0:T(8,128)}, f32[256,512]{1,0:T(8,128)}, f32[256,512]{1,0:T(8,128)}, f32[256,512]{1,0:T(8,128)}, /*inde...) fusion(s32[512]{0:T(512)S(1)} %multiply_add_fusion, s32[256]{0:T(256)S(1)} %get-tuple-element.43, ...), kind=kLoop, calls=%fused_computation.108 | loop fusion | flops 7340032 | bytes 4200448 | tf_op jit(solution)/shard_map/cos | solution.py:19
  60.7 18.9 %all-to-all-done.1 = f32[16,2,32,512]{3,2,1,0:T(8,128)S(1)} async-done(((f32[16,2,32,512]{3,2,1,0:T(8,128)}), f32[16,2,32,512]{3,2,1,0:T(8,128)S(1)}, u32[]{:S(2)}, u32[]{:S(2)}) %all-to-all-start.1) | async-done | bytes 2097184 | tf_op jit(solution)/shard_map/all_to_all | solution.py:126
  85.2 33.4 %all_to_all.102 = f32[1,512,512]{2,0,1:T(1,128)S(1)} all-to-all(f32[1,512,512]{2,0,1:T(1,128)S(1)} %copy.24), channel_id=1, replica_groups=mesh['row'=16,'col'=16] {'col'}, dimensions={1} | all-to-all | bytes 2097152 | tf_op jit(solution)/shard_map/all_to_all | solution.py:123
  120.9 2.6 copy.26
  123.5 6.8 %all-to-all-start.3 = ((f32[16,2,32,512]{3,2,1,0:T(8,128)}), f32[16,2,32,512]{3,2,1,0:T(8,128)S(1)}, u32[]{:S(2)}, u32[]{:S(2)}) async-start(f32[16,2,32,512]{3,2,1,0:T(8,128)} %copy.26), calls=%async_computation.3 | async-start | bytes 4194304 | tf_op jit(solution)/shard_map/all_to_all | solution.py:129
  130.4 47.3 %all-to-all-done.3 = f32[16,2,32,512]{3,2,1,0:T(8,128)S(1)} async-done(((f32[16,2,32,512]{3,2,1,0:T(8,128)}), f32[16,2,32,512]{3,2,1,0:T(8,128)S(1)}, u32[]{:S(2)}, u32[]{:S(2)}) %all-to-all-start.3) | async-done | bytes 2097184 | tf_op jit(solution)/shard_map/all_to_all | solution.py:129
  190.1 15.4 %pad_maximum_fusion = f32[16,2,32,512]{3,1,2,0:T(2,128)} fusion(f32[16,1,32,512]{3,1,2,0:T(1,128)S(1)} %copy.29, f32[16,1,32,512]{3,1,2,0:T(1,128)S(1)} %copy.28), kind=kLoop, calls=%fused_computation.16 | loop fusion | flops 524288 | bytes 4194304 | tf_op jit(solution)/shard_map/stack | solution.py:96
  205.4 7.2 %all-to-all-start.4 = ((f32[16,2,32,512]{3,1,2,0:T(2,128)}), f32[16,2,32,512]{3,1,2,0:T(2,128)S(1)}, u32[]{:S(2)}, u32[]{:S(2)}) async-start(f32[16,2,32,512]{3,1,2,0:T(2,128)} %pad_maximum_fusion), calls=%async_computation.4 | async-start | bytes 4194304 | tf_op jit(solution)/shard_map/all_to_all | solution.py:129
  212.7 47.7 %all-to-all-done.4 = f32[16,2,32,512]{3,1,2,0:T(2,128)S(1)} async-done(((f32[16,2,32,512]{3,1,2,0:T(2,128)}), f32[16,2,32,512]{3,1,2,0:T(2,128)S(1)}, u32[]{:S(2)}, u32[]{:S(2)}) %all-to-all-start.4) | async-done | bytes 2097184 | tf_op jit(solution)/shard_map/all_to_all | solution.py:129
  260.4 2.2 fusion.22
  264.4 32.1 %all_to_all.103 = f32[1,512,512]{2,0,1:T(1,128)S(1)} all-to-all(f32[1,512,512]{2,0,1:T(1,128)S(1)} %copy.32), channel_id=1, replica_groups=mesh['row'=16,'col'=16] {'col'}, dimensions={1} | all-to-all | bytes 2097152 | tf_op jit(solution)/shard_map/all_to_all | solution.py:123
  296.6 3.5 fusion.43
  300.0 3.5 fusion.45
  308.0 36.5 %all_to_all.104 = f32[16,2,32,512]{3,1,2,0:T(2,128)S(1)} all-to-all(f32[16,2,32,512]{3,1,2,0:T(2,128)S(1)} %pad_maximum_fusion.1), channel_id=1, replica_groups=mesh['row'=16,'col'=16] {'row'}, dimensions={0} | all-to-all | bytes 4194304 | tf_op jit(solution)/shard_map/all_to_all | solution.py:126
  344.5 2.2 fusion.25
  348.5 20.6 %all_to_all.105 = f32[1,512,512]{2,0,1:T(1,128)S(1)} all-to-all(f32[1,512,512]{2,0,1:T(1,128)S(1)} %copy.37), channel_id=1, replica_groups=mesh['row'=16,'col'=16] {'row'}, dimensions={1} | all-to-all | bytes 2097152 | tf_op jit(solution)/shard_map/all_to_all | solution.py:120
  (61 shorter events, 33.8 us)
Async XLA Ops:
  1.1 9.3 %collective-permute-start.1 = (f32[512,1]{1,0:T(8,128)S(1)}, f32[512,1]{1,0:T(8,128)S(1)}, u32[]{:S(2)}, u32[]{:S(2)}) collective-permute-start(f32[512,1]{1,0:T(8,128)S(1)} %slice.66), channel_id=1, source_target_pairs={{0,1},{1,2},{2,3},{3,4},{4,5},{5,6},{6,7},{7,8},{8,9},{9,10},{10,1... | collective-permute-start | bytes 6152 | tf_op jit(solution)/shard_map/ppermute | solution.py:14
  6.2 4.7 %collective-permute-start = (f32[1,512]{1,0:T(1,128)S(1)}, f32[1,512]{1,0:T(1,128)S(1)}, u32[]{:S(2)}, u32[]{:S(2)}) collective-permute-start(f32[1,512]{1,0:T(1,128)S(1)} %slice.64), channel_id=1, source_target_pairs={{0,16},{16,32},{32,48},{48,64},{64,80},{80,96},{96,112},{112,128},... | collective-permute-start | bytes 6152 | tf_op jit(solution)/shard_map/ppermute | solution.py:14
  15.3 26.6 %all-to-all-start = ((f32[1,512,512]{2,0,1:T(1,128)}), f32[1,512,512]{2,0,1:T(1,128)S(1)}, u32[]{:S(2)}, u32[]{:S(2)}) async-start(f32[1,512,512]{2,0,1:T(1,128)} %reshape.479), calls=%async_computation | async-start | bytes 2097152 | tf_op jit(solution)/shard_map/all_to_all | solution.py:120
  46.6 32.9 %all-to-all-start.1 = ((f32[16,2,32,512]{3,2,1,0:T(8,128)}), f32[16,2,32,512]{3,2,1,0:T(8,128)S(1)}, u32[]{:S(2)}, u32[]{:S(2)}) async-start(f32[16,2,32,512]{3,2,1,0:T(8,128)} %copy.22), calls=%async_computation.1 | async-start | bytes 4194304 | tf_op jit(solution)/shard_map/all_to_all | solution.py:126
  80.4 2.0 copy-start
  80.4 2.0 copy-start.2
  123.5 54.2 %all-to-all-start.3 = ((f32[16,2,32,512]{3,2,1,0:T(8,128)}), f32[16,2,32,512]{3,2,1,0:T(8,128)S(1)}, u32[]{:S(2)}, u32[]{:S(2)}) async-start(f32[16,2,32,512]{3,2,1,0:T(8,128)} %copy.26), calls=%async_computation.3 | async-start | bytes 4194304 | tf_op jit(solution)/shard_map/all_to_all | solution.py:129
  178.1 1.0 copy-start.4
  178.1 1.2 copy-start.5
  178.6 2.7 copy-start.6
  178.6 2.7 copy-start.7
  205.4 55.0 %all-to-all-start.4 = ((f32[16,2,32,512]{3,1,2,0:T(2,128)}), f32[16,2,32,512]{3,1,2,0:T(2,128)S(1)}, u32[]{:S(2)}, u32[]{:S(2)}) async-start(f32[16,2,32,512]{3,1,2,0:T(2,128)} %pad_maximum_fusion), calls=%async_computation.4 | async-start | bytes 4194304 | tf_op jit(solution)/shard_map/all_to_all | solution.py:129
  264.4 32.2 %copy-start.1 = (f32[256,512]{1,0:T(8,128)S(1)}, f32[256,512]{1,0:T(8,128)}, u32[]{:S(2)}) copy-start(f32[256,512]{1,0:T(8,128)} %get-tuple-element.33) | copy-start | bytes 1572868
  264.4 32.2 %copy-start.3 = (f32[256,512]{1,0:T(8,128)S(1)}, f32[256,512]{1,0:T(8,128)}, u32[]{:S(2)}) copy-start(f32[256,512]{1,0:T(8,128)} %get-tuple-element.34) | copy-start | bytes 1572868
where the time goes:
time: 373 us; the launch traced here: 370 us
  waiting for transfers between devices  132 us (35%)
  blocking collectives  123 us (33%)
  starting transfers between devices  35.9 us (10%)
  other arithmetic  32.4 us (9%)
  matrix products  27.2 us (7%)
  local copies, waits for them, and re-layouts  20 us (5%)
    all_to_all x2, waiting for transfers between devices, col_mixing(): lax.all_to_all(values, 'col', split_axis=0, concat_axis=2, tiled=True)  94.9 us
    all_to_all x2, blocking collectives, col_spread(): lax.all_to_all(values, 'col', split_axis=1, concat_axis=0, tiled=True)  65.5 us
    all_to_all x1, blocking collectives, row_mixing(): lax.all_to_all(values, 'row', split_axis=0, concat_axis=2, tiled=True)  36.5 us
    all_to_all x1, blocking collectives, row_spread(): lax.all_to_all(values, 'row', split_axis=1, concat_axis=0, tiled=True)  20.6 us
    all_to_all x1, waiting for transfers between devices, row_mixing(): lax.all_to_all(values, 'row', split_axis=0, concat_axis=2, tiled=True)  18.9 us
    another operation x2, other arithmetic, inverse_axis(): jnp.stack([channel.reshape(members, length // members, breadth) for chann...  17.3 us
    all_to_all x1, waiting for transfers between devices, row_spread(): lax.all_to_all(values, 'row', split_axis=1, concat_axis=0, tiled=True)  17.1 us
    all_to_all x2, starting transfers between devices, col_mixing(): lax.all_to_all(values, 'col', split_axis=0, concat_axis=2, tiled=True)  14 us
  transfers between devices with their start and end apart: 6, of which 6 were waited for; matrix products, arithmetic and copies ran while one was open for 3% of the time, Pallas kernels for 0%

commit v1 on v0

v1 whole, which is shorter than its diff:
```python
import math

import jax
import jax.numpy as jnp
import numpy as np
from jax import lax
from jax.experimental import pallas as pl
from jax.experimental.pallas import tpu as pltpu
from jax.sharding import PartitionSpec as P

DIRECT = False
f32 = jnp.float32
bf16 = jnp.bfloat16


def cosine_basis(n):
    k, i = np.arange(n)[:, None], np.arange(n)[None]
    return np.sqrt(np.where(k == 0, 1, 2) / n) * np.cos(np.pi * k * (2 * i + 1) / (2 * n))


def edge_tables(n, members, freq):
    s = 2 * np.sin(freq)
    half = np.arcsinh(s / 2)
    e = np.exp(-2 * n * half)
    safe = np.where(s == 0, 1, s)
    e1 = np.where(s == 0, 0.5, e)
    th = np.tanh(np.arcsinh(safe / 2))
    one = np.where(s == 0, 0, 1)
    lead = one * th * (1 - e1 * e1)
    couple = one * e1 / (th * (1 - e1 * e1))
    return lead, e, couple


def build_tables(n, members):
    total = n * members
    half = n // 2
    q = cosine_basis(n)
    k = np.arange(n)
    s = 2 * np.sin(np.pi * k / (2 * n))
    den = s[:, None] ** 2 + s[None] ** 2
    den[0, 0] = 1
    r = 1 / den
    r[0, 0] = 0
    sp = np.zeros((n, n))
    i = np.arange(n)[None]
    sp = np.sqrt(2 / n) * s[:, None] * np.sin(np.pi * k[:, None] * (i + 1) / n)
    sp[:, n - 1] = 0
    sp[0] = 0
    q0, q1 = q[:, 0], q[:, -1]
    lead, e, couple = edge_tables(n, members, np.pi * k / (2 * n))
    vec = np.zeros((8, n))
    vec[0], vec[1], vec[2], vec[3], vec[4] = q0, q1, lead, e, couple
    m = np.arange(half)
    gvec = np.zeros((members, 8, n))
    for c in range(members):
        kap = np.concatenate([c + 2 * members * m, c + members + 2 * members * m])
        gvec[c, 2], gvec[c, 3], gvec[c, 4] = edge_tables(n, members, np.pi * kap / (2 * total))
    j = 2 * np.arange(n) + 1
    cb = np.concatenate(
        [np.cos(np.pi * m[:, None] * j[None] / n), np.sin(np.pi * m[:, None] * j[None] / n)], 1
    )
    cls = np.arange(2 * members)
    ang = np.pi * cls[:, None] * j[None] / (2 * total)
    acs = np.concatenate([np.cos(ang), np.sin(ang)], 0)
    p = np.arange(members)
    wang = np.pi * cls[:, None] * p[None] / members
    wc, ws = np.cos(wang), np.sin(wang)
    wfwd = np.zeros((members, 8, 2 * members))
    for c in range(members):
        for side in range(2):
            for h in range(2):
                cols = slice(side * members, (side + 1) * members)
                wfwd[c, 2 * side + h, cols] = wc[c + h * members]
                wfwd[c, 4 + 2 * side + h, cols] = ws[c + h * members]
    winv = np.concatenate([wc.T, -ws.T], 1)
    M = members
    t = np.arange(1, M)
    st = np.sqrt(2 / M) * np.sin(np.pi * np.outer(t, t) / M)
    sa, stt, s2 = np.zeros((M, M)), np.zeros((M, M)), np.zeros((M, M))
    sa[: M - 1, : M - 1] = st
    sa[: M - 1, M - 1] = st[:, M - 2]
    stt[: M - 1, 1:] = -st
    s2[: M - 1, : M - 1] = st
    a0 = (q1[1:] ** 2 / s[1:] ** 2).sum()
    b0 = (q0[1:] * q1[1:] / s[1:] ** 2).sum()
    qq = 1 / np.sqrt(n)
    pp = np.arange(M)
    frac = (pp[:, None] + 1) / M
    t1 = frac - (pp[None] <= pp[:, None])
    h15 = np.zeros((M, M))
    h15[:, M - 1] = frac[:, 0]
    hmat = np.concatenate([h15, t1], 1)
    acc = (pp[None] < pp[:, None]).astype(float)
    acc[:, M - 1] = 0
    acc = (acc - acc.mean(0)) / qq
    up = np.zeros((M, M))
    up[:-1, 1:] = np.eye(M - 1)
    keep = np.eye(M)
    keep[M - 1, M - 1] = 0
    ka = acc @ keep
    kt = -acc @ (keep @ up)
    kh = acc @ (keep @ (-(1 + 2 * a0) * np.eye(M) + b0 * up + b0 * up.T))
    mats = np.zeros((6 * M, 128))
    mats[0:M, : 2 * M] = np.concatenate([sa, stt], 1)
    mats[M : 2 * M, :M] = s2
    mats[2 * M : 3 * M, : 2 * M] = hmat
    mats[3 * M : 4 * M, : 3 * M] = np.concatenate([ka, kt, kh], 1)
    mats[4 * M : 5 * M, : 4 * M] = winv
    mats[5 * M : 5 * M + M - 1, :] = np.cos(np.pi * t / M)[:, None]
    wf = np.zeros((M, 8, 128))
    wf[:, :, : 2 * M] = wfwd
    out = dict(q=q, sp=sp, r=r, vec=vec, gvec=gvec, cb=cb, acs=acs, mats=mats, wf=wf)
    return {name: np.asarray(value, np.float32) for name, value in out.items()}


def split(a):
    high = a.astype(bf16)
    return high, (a - high.astype(f32)).astype(bf16)


def mm(a, b, ca, cb):
    return lax.dot_general(a, b, (((ca,), (cb,)), ((), ())), preferred_element_type=f32)


def dot3(a, b, ca=1, cb=0):
    ah, al = a if isinstance(a, tuple) else split(a)
    bh, bl = b if isinstance(b, tuple) else split(b)
    return mm(ah, bh, ca, cb) + (mm(ah, bl, ca, cb) + mm(al, bh, ca, cb))


def doth(a, b, ca=1, cb=0):
    return lax.dot_general(
        a, b, (((ca,), (cb,)), ((), ())), precision=lax.Precision.HIGHEST, preferred_element_type=f32
    )


def rows_of(shape):
    return lax.broadcasted_iota(jnp.int32, shape, 0)


def lanes_of(shape):
    return lax.broadcasted_iota(jnp.int32, shape, 1)


def pick(values, index):
    return jnp.sum(jnp.where(rows_of(values.shape) == index, values, 0.0), 0, keepdims=True)


def below(values):
    return jnp.concatenate([jnp.zeros_like(values[:1]), values[:-1]], 0)


def edge_solve(al, t0, lead, e, couple, source, mats, special):
    M, n = al.shape
    L = min(n, 128)
    last = rows_of((M, n)) == M - 1
    both = jnp.concatenate([jnp.where(last, al * couple, al), t0], 0)
    modes = doth(mats[0:M, : 2 * M], both)
    cosphi = mats[5 * M : 6 * M, :1]
    modes = modes * (lead / (1.0 + e * e - 2.0 * e * cosphi))
    H = jnp.where(last, al, doth(mats[M : 2 * M, :M], modes))
    Hz = doth(mats[2 * M : 3 * M, : 2 * M], jnp.concatenate([al[:, :L], source], 0))
    mean = doth(mats[3 * M : 4 * M, : 3 * M], jnp.concatenate([al[:, :L], t0[:, :L], Hz], 0))
    lane = lanes_of((M, L))
    first = jnp.where((lane == 0) & special, Hz, H[:, :L])
    H = first if n == L else jnp.concatenate([first, H[:, L:]], 1)
    return H, jnp.where(special, mean[:, :1], 0.0)


def to_peers(rows, members):
    one = jnp.concatenate(rows, 0)
    return jnp.broadcast_to(one[None], (members,) + one.shape)


def stage_local(r, c, M, gx, gy, q, sp, rr, vec):
    gx, gy, q, sp, rr, vec = gx[...], gy[...], q[...], sp[...], rr[...], vec[...]
    n = q.shape[0]
    L = min(n, 128)
    qs, ss = split(q), split(sp)
    gys = split(gy)
    m1 = dot3(gx, qs, 1, 1)
    m2 = dot3(gys, ss, 1, 1)
    u = -(dot3(ss, m1) + dot3(qs, m2)) * rr
    slab = (gys[0][:, n - L :], gys[1][:, n - L :])
    gyl = dot3(slab, qs, 0, 1)[L - 1 :]
    us = split(u)
    tk = dot3(vec, us, 1, 1)
    tl = dot3(vec, us, 1, 0)
    alpha = gyl + jnp.where(c < M - 1, tk[1:2], 0.0)
    beta = m1[n - 1 :] + jnp.where(r < M - 1, tl[1:2], 0.0)
    return u, to_peers([alpha, tk[0:1], beta, tl[0:1]], M)


def stage_strip(r, c, M, ag, q, rr, vec, cb, acs, mats, wf):
    al, t0, be, ta0 = (ag[:, a, :] for a in range(4))
    vec, mats = vec[...], mats[...]
    n = al.shape[1]
    q0, q1, lead, e, couple = (vec[a : a + 1] for a in range(5))
    L = min(n, 128)
    zero = jnp.zeros((M, L), f32)
    H, mean = edge_solve(al, t0, lead, e, couple, zero, mats, True)
    Z = doth(jnp.concatenate([H * q0, H * q1], 0), rr[...])
    add0 = q0 * below(Z[:M]) - q1 * Z[:M]
    add1 = q0 * below(Z[M:]) - q1 * Z[M:]
    flat = jnp.where(lanes_of((M, n)) == 0, mean * (1.0 / math.sqrt(n)), 0.0)
    tau0 = ta0 + add0 + flat
    tau1 = be + jnp.where(r < M - 1, add1 + flat, 0.0)
    y = doth(jnp.concatenate([tau0, tau1], 0), q[...])
    g = doth(wf[c][:, : 2 * M], y)
    C, S = g[:4], g[4:]
    ca0, ca1 = acs[pl.ds(c, 1), :], acs[pl.ds(c + M, 1), :]
    sa0, sa1 = acs[pl.ds(c + 2 * M, 1), :], acs[pl.ds(c + 3 * M, 1), :]
    ca = jnp.concatenate([ca0, ca1, ca0, ca1], 0)
    sa = jnp.concatenate([sa0, sa1, sa0, sa1], 0)
    xy = jnp.concatenate([C * ca - S * sa, -(C * sa + S * ca)], 1)
    T = doth(xy, cb[...], 1, 1) * math.sqrt(2.0 / (n * M))
    x0 = jnp.concatenate([T[0:1], T[1:2]], 1)
    x1 = jnp.concatenate([T[2:3], T[3:4]], 1)
    root = jnp.where((lanes_of((1, n)) == 0) & (c == 0), math.sqrt(0.5), 1.0)
    src = jnp.broadcast_to(al[M - 1 :, :1] * (1.0 / math.sqrt(M)), (1, n))
    return (to_peers([x1 * root, x0 * root, src, jnp.zeros((1, n), f32)], M),)


def stage_edges(r, c, M, ag, gvec, mats):
    al, t0 = ag[:, 0, :], ag[:, 1, :]
    n = al.shape[1]
    L = min(n, 128)
    src = ag[:, 2, :][:, :L]
    gv = gvec[c]
    H, mean = edge_solve(al, t0, gv[2:3], gv[3:4], gv[4:5], src, mats[...], c == 0)
    right = pick(H, r)
    left = pick(H, r - 1)
    lift = jnp.broadcast_to(pick(mean, r) * (1.0 / math.sqrt(M)), (1, n))
    return (to_peers([left, right, lift, jnp.zeros((1, n), f32)], M),)


def stage_field(r, c, M, ag3, ag1, u, q, rr, vec, cb, acs, mats):
    q, rr, vec, mats = q[...], rr[...], vec[...], mats[...]
    n = q.shape[0]
    half = n // 2
    L = min(n, 128)
    q0, q1, lead, e, couple = (vec[a : a + 1] for a in range(5))
    hl, hr = ag3[:, 0, :], ag3[:, 1, :]
    T = jnp.concatenate([hl[:, :half], hl[:, half:], hr[:, :half], hr[:, half:]], 0)
    root = jnp.where(
        (lanes_of(T.shape) == 0) & (rows_of(T.shape) % (2 * M) == 0), math.sqrt(0.5), 1.0
    )
    xx = doth(T * (root * math.sqrt(2.0 / (n * M))), cb[...])
    ca, sa = acs[0 : 2 * M, :], acs[2 * M : 4 * M, :]
    h = []
    for side in range(2):
        xc = xx[side * 2 * M : (side + 1) * 2 * M, :n]
        xs = xx[side * 2 * M : (side + 1) * 2 * M, n:]
        rot = jnp.concatenate([ca * xc - sa * xs, sa * xc + ca * xs], 0)
        h.append(doth(mats[4 * M : 5 * M, : 4 * M], rot))
    hx = doth(jnp.concatenate(h, 0), q, 1, 1)
    left, right = hx[:M], hx[M:]
    Y = doth(jnp.concatenate([left * q0, left * q1, right * q0, right * q1], 0), rr)
    t0b = q0 * Y[0:M] - q1 * Y[2 * M : 3 * M]
    t1b = q0 * Y[M : 2 * M] - q1 * Y[3 * M :]
    last = rows_of((M, n)) == M - 1
    al = ag1[:, 0, :] + jnp.where(last, 0.0, t1b)
    t0 = ag1[:, 1, :] + t0b
    src = right[:, :L] - left[:, :L]
    H, mean = edge_solve(al, t0, lead, e, couple, src, mats, True)
    here, before = pick(H, c), pick(H, c - 1)
    lhs = jnp.concatenate([q1, -q0, here, -before], 0)
    rhs = jnp.concatenate([pick(right, c), pick(left, c), q1, q0], 0)
    pad = jnp.zeros((4, n), f32)
    G = doth(jnp.concatenate([lhs, pad], 0), jnp.concatenate([rhs, pad], 0), 0, 0)
    level = pick(mean, c) + ag3[:, 2, :][:1, :1]
    un = u[...] - rr * G
    un = jnp.where((rows_of(un.shape) == 0) & (lanes_of(un.shape) == 0), level, un)
    qs = split(q)
    return (dot3(qs, dot3(un, qs), 0, 0),)


def run_stage(stage, members, outs, *args):
    r, c = lax.axis_index("row"), lax.axis_index("col")
    if DIRECT:
        return stage(r, c, members, *args)

    def kernel(place, *refs):
        results = stage(place[0], place[1], members, *refs[: len(args)])
        for ref, value in zip(refs[len(args) :], results):
            ref[...] = value

    place = jnp.stack([r, c]).astype(jnp.int32)
    vmem = pl.BlockSpec(memory_space=pltpu.VMEM)
    return pl.pallas_call(
        kernel,
        out_shape=[jax.ShapeDtypeStruct(shape, f32) for shape in outs],
        in_specs=[pl.BlockSpec(memory_space=pltpu.SMEM)] + [vmem] * len(args),
        out_specs=[vmem] * len(outs),
        compiler_params=pltpu.CompilerParams(vmem_limit_bytes=56 * 1024 * 1024),
        name=stage.__name__,
    )(place, *args)


def exchange(values, axis):
    return lax.all_to_all(values, axis, split_axis=0, concat_axis=0, tiled=True)


def make_body(members):
    def body(grad_x, grad_y):
        n = grad_x.shape[0]
        t = {k: jnp.asarray(v) for k, v in build_tables(n, members).items()}
        edge = (members, 4, n)
        u, edges = run_stage(
            stage_local, members, [(n, n), edge], grad_x, grad_y, t["q"], t["sp"], t["r"], t["vec"]
        )
        strip = exchange(edges, "col")
        (lines,) = run_stage(
            stage_strip, members, [edge],
            strip, t["q"], t["r"], t["vec"], t["cb"], t["acs"], t["mats"], t["wf"],
        )
        lines = exchange(lines, "row")
        (flux,) = run_stage(stage_edges, members, [edge], lines, t["gvec"], t["mats"])
        flux = exchange(flux, "col")
        (field,) = run_stage(
            stage_field, members, [(n, n)],
            flux, strip, u, t["q"], t["r"], t["vec"], t["cb"], t["acs"], t["mats"],
        )
        return field

    return body


def solution(mesh):
    members = mesh.shape["row"]
    placed = (P("row", "col"), P("row", "col"))
    return jax.shard_map(
        make_body(members), mesh=mesh, in_specs=placed, out_specs=P("row", "col"), check_vma=False
    )
```

time: 373 us -> 70.8 us (0.19)
  waiting for transfers between devices: 132 us -> 0 us
  blocking collectives: 123 us -> 45.6 us
  starting transfers between devices: 35.9 us -> 0 us
  other arithmetic: 32.4 us -> 0.6 us
  matrix products: 27.2 us -> 0 us
  Pallas kernels: 0 us -> 24.2 us
  local copies, waits for them, and re-layouts: 20 us -> 0 us
    all_to_all x4 -> x0, waiting for transfers between devices: 131 us -> none  [the longest x2 94.9 us: col_mixing(): lax.all_to_all(values, 'col', split_axis=0, concat_axis=2, tiled=True)]
    all_to_all x4 -> x3, blocking collectives: 123 us -> 45.6 us  [exchange(): return lax.all_to_all(values, axis, split_axis=0, concat_axis=0, tiled=True)]
    all_to_all x4 -> x0, starting transfers between devices: 27.6 us -> none  [the longest x2 14 us: col_mixing(): lax.all_to_all(values, 'col', split_axis=0, concat_axis=2, tiled=True)]
    dot_general x12 -> x0, matrix products: 27.2 us -> none  [the longest x4 10.6 us: inverse_axis(): jnp.dot(grid_table.T, spec[which * halfway:(which + 1) * halfway], precis...]
    pallas_call x0 -> x4, Pallas kernels: none -> 24.2 us  [run_stage(): pl.pallas_call(kernel, out_shape=[jax.ShapeDtypeStruct(shape, f32) for sh...]
    another operation x2 -> x1, other arithmetic: 17.3 us -> 0.6 us  [run_stage(): place = jnp.stack([r, c]).astype(jnp.int32)]
    cos x1 -> x0, other arithmetic: 9.71 us -> none  [trig_table(): return (jnp.cos(reduced), jnp.sin(reduced))]
    ppermute x2 -> x0, starting transfers between devices: 8.32 us -> none  [passed_along(): return lax.ppermute(block, axis, route)]
  transfers between devices with their start and end apart: 6 -> 0, of which waited for: 6 -> 0; matrix products, arithmetic and copies ran while one was open for 3% -> 0% of each run, Pallas kernels for 0% -> 0%
where the time goes in v1:
time: 70.8 us; the launch traced here: 70.5 us
  blocking collectives  45.6 us (64%)
  Pallas kernels  24.2 us (34%)
    all_to_all x3, blocking collectives, exchange(): return lax.all_to_all(values, axis, split_axis=0, concat_axis=0, tiled=True)  45.6 us
    pallas_call x4, Pallas kernels, run_stage(): pl.pallas_call(kernel, out_shape=[jax.ShapeDtypeStruct(shape, f32) for sh...  24.2 us

profile of v1, /device:TPU:1, one launch (start us, length us, event | category | flops | bytes accessed | tf_op | source)
XLA Modules:
  0.0 70.5 jit_solution(200625815376930438)
XLA Ops:
  0.0 0.6 pad_add_fusion.place
  0.6 7.7 %stage_local.1 = (f32[512,512]{1,0:T(8,128)}, f32[16,4,512]{2,1,0:T(4,128)}) custom-call(s32[2]{0:T(128)} %pad_add_fusion.place, f32[512,512]{1,0:T(8,128)} %refs_0_.1, f32[512,512]{1,0:T(8,128)} %refs_1_.3, f32[512,512]{1,0:T(8,128)} %constant.25.clone.refs_2_.refs_1_.refs_3_, f32[512,512]{1,0:T(8,128)} %constant.26.clone.refs_3_, ...), custom_call_target="tpu_custom_call" | custom-call | tf_op jit(solution)/shard_map/stage_local/pallas_call | solution.py:290
  8.3 17.7 %all_to_all.15.refs_0_.refs_1_ = f32[16,4,512]{2,1,0:T(4,128)} all-to-all(f32[16,4,512]{2,1,0:T(4,128)} %get-tuple-element.7), channel_id=1, replica_groups=mesh['row'=16,'col'=16] {'col'}, dimensions={0} | all-to-all | bytes 262144 | tf_op jit(solution)/shard_map/all_to_all | solution.py:301
  26.0 5.3 %stage_strip.1 = f32[16,4,512]{2,1,0:T(4,128)} custom-call(s32[2]{0:T(128)} %pad_add_fusion.place, f32[16,4,512]{2,1,0:T(4,128)} %all_to_all.15.refs_0_.refs_1_, f32[512,512]{1,0:T(8,128)} %constant.25.clone.refs_2_.refs_1_.refs_3_, f32[512,512]{1,0:T(8,128)} %constant.27.clone.refs_4_.refs_2_, f32[8,512]{1,0:T(8,128)} %constant.28.clone.refs_5_.refs_3_, ...), custom_call_target="tpu_custom_call" | custom-call | tf_op jit(solution)/shard_map/stage_strip/pallas_call | solution.py:290
  31.3 16.3 %all_to_all.16.refs_0_ = f32[16,4,512]{2,1,0:T(4,128)} all-to-all(f32[16,4,512]{2,1,0:T(4,128)} %stage_strip.1), channel_id=1, replica_groups=mesh['row'=16,'col'=16] {'row'}, dimensions={0} | all-to-all | bytes 262144 | tf_op jit(solution)/shard_map/all_to_all | solution.py:301
  47.6 2.3 %stage_edges.1 = f32[16,4,512]{2,1,0:T(4,128)} custom-call(s32[2]{0:T(128)} %pad_add_fusion.place, f32[16,4,512]{2,1,0:T(4,128)} %all_to_all.16.refs_0_, f32[16,8,512]{2,1,0:T(8,128)} %constant.29.clone.refs_1_, f32[96,128]{1,0:T(8,128)} %constant.32.clone.refs_6_.refs_2_.refs_8_), custom_call_target="tpu_custom_call" | custom-call | tf_op jit(solution)/shard_map/stage_edges/pallas_call | solution.py:290
  49.9 11.6 %all_to_all.17.refs_0_ = f32[16,4,512]{2,1,0:T(4,128)} all-to-all(f32[16,4,512]{2,1,0:T(4,128)} %stage_edges.1), channel_id=1, replica_groups=mesh['row'=16,'col'=16] {'col'}, dimensions={0} | all-to-all | bytes 262144 | tf_op jit(solution)/shard_map/all_to_all | solution.py:301
  61.4 9.0 %stage_field.1 = f32[512,512]{1,0:T(8,128)} custom-call(s32[2]{0:T(128)} %pad_add_fusion.place, f32[16,4,512]{2,1,0:T(4,128)} %all_to_all.17.refs_0_, f32[16,4,512]{2,1,0:T(4,128)} %all_to_all.15.refs_0_.refs_1_, f32[512,512]{1,0:T(8,128)} %get-tuple-element.8.refs_2_, f32[512,512]{1,0:T(8,128)} %constant.25.clone.refs_2_.refs_1_.refs_3_, ...), custom_call_target="tpu_custom_call" | custom-call | tf_op jit(solution)/shard_map/stage_field/pallas_call | solution.py:290

commit v2 on v1

--- a/solution.py
+++ b/solution.py
@@ -51,27 +51,19 @@
     vec = np.zeros((8, n))
     vec[0], vec[1], vec[2], vec[3], vec[4] = q0, q1, lead, e, couple
     m = np.arange(half)
-    gvec = np.zeros((members, 8, n))
-    for c in range(members):
-        kap = np.concatenate([c + 2 * members * m, c + members + 2 * members * m])
-        gvec[c, 2], gvec[c, 3], gvec[c, 4] = edge_tables(n, members, np.pi * kap / (2 * total))
+    cls = np.arange(2 * members)
+    kap = cls[:, None] + 2 * members * m[None]
+    glob = np.stack(edge_tables(n, members, np.pi * kap / (2 * total)))
     j = 2 * np.arange(n) + 1
     cb = np.concatenate(
         [np.cos(np.pi * m[:, None] * j[None] / n), np.sin(np.pi * m[:, None] * j[None] / n)], 1
     )
-    cls = np.arange(2 * members)
     ang = np.pi * cls[:, None] * j[None] / (2 * total)
     acs = np.concatenate([np.cos(ang), np.sin(ang)], 0)
     p = np.arange(members)
     wang = np.pi * cls[:, None] * p[None] / members
     wc, ws = np.cos(wang), np.sin(wang)
-    wfwd = np.zeros((members, 8, 2 * members))
-    for c in range(members):
-        for side in range(2):
-            for h in range(2):
-                cols = slice(side * members, (side + 1) * members)
-                wfwd[c, 2 * side + h, cols] = wc[c + h * members]
-                wfwd[c, 4 + 2 * side + h, cols] = ws[c + h * members]
+    wfwd = np.concatenate([wc, ws], 0)
     winv = np.concatenate([wc.T, -ws.T], 1)
     M = members
     t = np.arange(1, M)
@@ -100,16 +92,22 @@
     ka = acc @ keep
     kt = -acc @ (keep @ up)
     kh = acc @ (keep @ (-(1 + 2 * a0) * np.eye(M) + b0 * up + b0 * up.T))
-    mats = np.zeros((6 * M, 128))
+    s2x = s2.copy()
+    s2x[M - 1, M - 1] = 1
+    mats = np.zeros((15 * M, 128))
     mats[0:M, : 2 * M] = np.concatenate([sa, stt], 1)
     mats[M : 2 * M, :M] = s2
     mats[2 * M : 3 * M, : 2 * M] = hmat
     mats[3 * M : 4 * M, : 3 * M] = np.concatenate([ka, kt, kh], 1)
     mats[4 * M : 5 * M, : 4 * M] = winv
     mats[5 * M : 5 * M + M - 1, :] = np.cos(np.pi * t / M)[:, None]
-    wf = np.zeros((M, 8, 128))
-    wf[:, :, : 2 * M] = wfwd
-    out = dict(q=q, sp=sp, r=r, vec=vec, gvec=gvec, cb=cb, acs=acs, mats=mats, wf=wf)
+    mats[6 * M : 7 * M, :M] = s2x
+    mats[7 * M : 8 * M, :M] = t1.T
+    mats[8 * M : 9 * M, :M] = ka.T * qq
+    mats[9 * M : 10 * M, :M] = kt.T * qq
+    mats[10 * M : 11 * M, :M] = (kh @ t1).T
+    mats[11 * M : 15 * M, :M] = wfwd
+    out = dict(q=q, sp=sp, r=r, vec=vec, glob=glob, cb=cb, acs=acs, mats=mats)
     return {name: np.asarray(value, np.float32) for name, value in out.items()}
 
 
@@ -191,99 +189,146 @@
     return u, to_peers([alpha, tk[0:1], beta, tl[0:1]], M)
 
 
-def stage_strip(r, c, M, ag, q, rr, vec, cb, acs, mats, wf):
+def lane_pick(values, index):
+    return jnp.sum(jnp.where(lanes_of(values.shape) == index, values, 0.0), 1, keepdims=True)
+
+
+def stage_strip(r, c, M, ag, q, rr, vec, glob, cb, acs, mats):
     al, t0, be, ta0 = (ag[:, a, :] for a in range(4))
     vec, mats = vec[...], mats[...]
     n = al.shape[1]
+    half = n // 2
     q0, q1, lead, e, couple = (vec[a : a + 1] for a in range(5))
     L = min(n, 128)
+    qq = 1.0 / math.sqrt(n)
     zero = jnp.zeros((M, L), f32)
+    sa, stt, s2 = mats[:M, :M], mats[:M, M : 2 * M], mats[M : 2 * M, :M]
+    cosphi = mats[5 * M : 6 * M, :1]
+
     H, mean = edge_solve(al, t0, lead, e, couple, zero, mats, True)
     Z = doth(jnp.concatenate([H * q0, H * q1], 0), rr[...])
     add0 = q0 * below(Z[:M]) - q1 * Z[:M]
     add1 = q0 * below(Z[M:]) - q1 * Z[M:]
-    flat = jnp.where(lanes_of((M, n)) == 0, mean * (1.0 / math.sqrt(n)), 0.0)
+    flat = jnp.where(lanes_of((M, n)) == 0, mean * qq, 0.0)
     tau0 = ta0 + add0 + flat
     tau1 = be + jnp.where(r < M - 1, add1 + flat, 0.0)
-    y = doth(jnp.concatenate([tau0, tau1], 0), q[...])
-    g = doth(wf[c][:, : 2 * M], y)
-    C, S = g[:4], g[4:]
-    ca0, ca1 = acs[pl.ds(c, 1), :], acs[pl.ds(c + M, 1), :]
-    sa0, sa1 = acs[pl.ds(c + 2 * M, 1), :], acs[pl.ds(c + 3 * M, 1), :]
-    ca = jnp.concatenate([ca0, ca1, ca0, ca1], 0)
-    sa = jnp.concatenate([sa0, sa1, sa0, sa1], 0)
-    xy = jnp.concatenate([C * ca - S * sa, -(C * sa + S * ca)], 1)
-    T = doth(xy, cb[...], 1, 1) * math.sqrt(2.0 / (n * M))
-    x0 = jnp.concatenate([T[0:1], T[1:2]], 1)
-    x1 = jnp.concatenate([T[2:3], T[3:4]], 1)
-    root = jnp.where((lanes_of((1, n)) == 0) & (c == 0), math.sqrt(0.5), 1.0)
-    src = jnp.broadcast_to(al[M - 1 :, :1] * (1.0 / math.sqrt(M)), (1, n))
-    return (to_peers([x1 * root, x0 * root, src, jnp.zeros((1, n), f32)], M),)
-
-
-def stage_edges(r, c, M, ag, gvec, mats):
-    al, t0 = ag[:, 0, :], ag[:, 1, :]
-    n = al.shape[1]
-    L = min(n, 128)
-    src = ag[:, 2, :][:, :L]
-    gv = gvec[c]
-    H, mean = edge_solve(al, t0, gv[2:3], gv[3:4], gv[4:5], src, mats[...], c == 0)
-    right = pick(H, r)
-    left = pick(H, r - 1)
-    lift = jnp.broadcast_to(pick(mean, r) * (1.0 / math.sqrt(M)), (1, n))
-    return (to_peers([left, right, lift, jnp.zeros((1, n), f32)], M),)
-
-
-def stage_field(r, c, M, ag3, ag1, u, q, rr, vec, cb, acs, mats):
-    q, rr, vec, mats = q[...], rr[...], vec[...], mats[...]
+
+    y = doth(jnp.concatenate([tau1, tau0], 0), q[...])
+    wf = mats[11 * M : 15 * M, :M]
+    ca, sna = acs[0 : 2 * M, :], acs[2 * M : 4 * M, :]
+    turned = []
+    for side in range(2):
+        g = doth(wf, y[side * M : (side + 1) * M])
+        C, S = g[: 2 * M], g[2 * M :]
+        turned.append(jnp.concatenate([C * ca - S * sna, -(C * sna + S * ca)], 1))
+    T = doth(jnp.concatenate(turned, 0), cb[...], 1, 1)
+    shape = (2 * M, half)
+    origin = (rows_of(shape) == 0) & (lanes_of(shape) == 0)
+    scale = jnp.where(origin, math.sqrt(1.0 / (n * M)), math.sqrt(2.0 / (n * M)))
+    T1, T0 = T[: 2 * M] * scale, T[2 * M :] * scale
+
+    own = rows_of((M, L)) == r
+    alz = jnp.where(own, T1[:1, :1], 0.0)
+    t0z = jnp.where(own, T0[:1, :1], 0.0)
+    src = jnp.where(own, al[M - 1 :, :1] * (1.0 / math.sqrt(M)), 0.0)
+    Hz = doth(mats[2 * M : 3 * M, : 2 * M], jnp.concatenate([alz, src], 0))
+    lift = doth(mats[3 * M : 4 * M, : 3 * M], jnp.concatenate([alz, t0z, Hz], 0))
+    g0 = jnp.where(rows_of((M, L)) == M - 1, Hz, doth(s2, Hz))
+    ge = glob[1]
+    up, down = lane_pick(sa, r), lane_pick(stt, r)
+    T1c = jnp.where(r == M - 1, T1 * glob[2], T1)
+    top, bottom = glob[0] * T1c, glob[0] * T0
+    quad = 1.0 + ge * ge
+    modes = []
+    for m in range(M - 1):
+        value = (up[m : m + 1] * top + down[m : m + 1] * bottom) / (
+            quad - ge * (2.0 * cosphi[m : m + 1])
+        )
+        modes.append(jnp.where(origin, g0[m : m + 1, :1], value) * scale)
+    modes.append(jnp.where(r == M - 1, T1, 0.0) * scale)
+    XX = dot3(jnp.concatenate(modes, 0), cb[...])
+    wi = split(mats[4 * M : 5 * M, : 4 * M])
+    lines = []
+    for m in range(M):
+        xc, xs = XX[2 * M * m : 2 * M * (m + 1), :n], XX[2 * M * m : 2 * M * (m + 1), n:]
+        lines.append(dot3(wi, jnp.concatenate([ca * xc - sna * xs, sna * xc + ca * xs], 0)))
+    hx = dot3(jnp.concatenate(lines, 0), q[...], 1, 1)
+    rs = split(rr[...])
+    Y0, Y1 = dot3(hx * q0, rs), dot3(hx * q1, rs)
+
+    D = lead / (1.0 + e * e - 2.0 * e * cosphi)
+    inner = rows_of((M, n)) < M - 1
+    first = lanes_of((1, n)) == 0
+    cols = []
+    for cc in (c, c - 1):
+        KD = lane_pick(s2, cc) * D
+        k1 = jnp.where(inner, doth(sa, KD, 0, 0), 0.0)
+        k2 = doth(stt, KD, 0, 0)
+        ksrc = lane_pick(mats[7 * M : 8 * M, :M], cc) * (-1.0 / qq)
+        cols.append((k1, k2, ksrc))
+    ka, kt = lane_pick(mats[8 * M : 9 * M, :M], c), lane_pick(mats[9 * M : 10 * M, :M], c)
+    kth = lane_pick(mats[10 * M : 11 * M, :M], c)
+    here, side_c, side_b, level = [], [], [], []
+    for m in range(M):
+        rows = slice(M * m, M * (m + 1))
+        hm, y0, y1 = hx[rows], Y0[rows], Y1[rows]
+        here.append(pick(hm, c))
+        for (k1, k2, ksrc), sides in zip(cols, (side_c, side_b)):
+            phi = jnp.sum(k1 * y1 + k2 * y0, 0, keepdims=True)
+            z = jnp.sum(ksrc * hm, 0, keepdims=True)
+            sides.append(jnp.where(first, z, phi))
+        level.append(
+            jnp.sum(kth * hm[:, :L] - ka * y1[:, :L] - kt * y0[:, :L], 0, keepdims=True)
+        )
+    s2x = mats[6 * M : 7 * M, :M]
+    mixed = [doth(s2x, jnp.concatenate(v, 0)) for v in (here, side_c, side_b, level)]
+    right, fc, fb, lv = mixed
+    lv = (lv - below(lv) + lift * (1.0 / math.sqrt(M)))[:, :1]
+    share = [
+        below(right),
+        right,
+        q0 * below(fc) - q1 * fc,
+        q0 * below(fb) - q1 * fb,
+        jnp.broadcast_to(lv, (M, n)),
+    ]
+    keep = [pick(H, c), pick(H, c - 1), jnp.broadcast_to(pick(mean, c), (1, n))]
+    return share, jnp.concatenate(keep + [jnp.zeros((5, n), f32)], 0)
+
+
+def stage_field(r, c, M, share, keep, u, q, rr, vec):
+    keep, vec = keep[...], vec[...]
     n = q.shape[0]
-    half = n // 2
-    L = min(n, 128)
-    q0, q1, lead, e, couple = (vec[a : a + 1] for a in range(5))
-    hl, hr = ag3[:, 0, :], ag3[:, 1, :]
-    T = jnp.concatenate([hl[:, :half], hl[:, half:], hr[:, :half], hr[:, half:]], 0)
-    root = jnp.where(
-        (lanes_of(T.shape) == 0) & (rows_of(T.shape) % (2 * M) == 0), math.sqrt(0.5), 1.0
+    q0, q1 = vec[0:1], vec[1:2]
+    left, right, here, before, level = (
+        jnp.sum(share[:, a, :], 0, keepdims=True) for a in range(5)
     )
-    xx = doth(T * (root * math.sqrt(2.0 / (n * M))), cb[...])
-    ca, sa = acs[0 : 2 * M, :], acs[2 * M : 4 * M, :]
-    h = []
-    for side in range(2):
-        xc = xx[side * 2 * M : (side + 1) * 2 * M, :n]
-        xs = xx[side * 2 * M : (side + 1) * 2 * M, n:]
-        rot = jnp.concatenate([ca * xc - sa * xs, sa * xc + ca * xs], 0)
-        h.append(doth(mats[4 * M : 5 * M, : 4 * M], rot))
-    hx = doth(jnp.concatenate(h, 0), q, 1, 1)
-    left, right = hx[:M], hx[M:]
-    Y = doth(jnp.concatenate([left * q0, left * q1, right * q0, right * q1], 0), rr)
-    t0b = q0 * Y[0:M] - q1 * Y[2 * M : 3 * M]
-    t1b = q0 * Y[M : 2 * M] - q1 * Y[3 * M :]
-    last = rows_of((M, n)) == M - 1
-    al = ag1[:, 0, :] + jnp.where(last, 0.0, t1b)
-    t0 = ag1[:, 1, :] + t0b
-    src = right[:, :L] - left[:, :L]
-    H, mean = edge_solve(al, t0, lead, e, couple, src, mats, True)
-    here, before = pick(H, c), pick(H, c - 1)
-    lhs = jnp.concatenate([q1, -q0, here, -before], 0)
-    rhs = jnp.concatenate([pick(right, c), pick(left, c), q1, q0], 0)
+    here = here + keep[0:1]
+    before = before + keep[1:2]
+    level = (level + keep[2:3])[:, :1]
     pad = jnp.zeros((4, n), f32)
-    G = doth(jnp.concatenate([lhs, pad], 0), jnp.concatenate([rhs, pad], 0), 0, 0)
-    level = pick(mean, c) + ag3[:, 2, :][:1, :1]
-    un = u[...] - rr * G
+    lhs = jnp.concatenate([q1, -q0, here, -before, pad], 0)
+    rhs = jnp.concatenate([right, left, q1, q0, pad], 0)
+    G = doth(lhs, rhs, 0, 0)
+    un = u[...] - rr[...] * G
     un = jnp.where((rows_of(un.shape) == 0) & (lanes_of(un.shape) == 0), level, un)
-    qs = split(q)
+    qs = split(q[...])
     return (dot3(qs, dot3(un, qs), 0, 0),)
 
 
 def run_stage(stage, members, outs, *args):
     r, c = lax.axis_index("row"), lax.axis_index("col")
     if DIRECT:
-        return stage(r, c, members, *args)
+        results = stage(r, c, members, *args)
+        return [jnp.stack(v, 1) if isinstance(v, list) else v for v in results]
 
     def kernel(place, *refs):
         results = stage(place[0], place[1], members, *refs[: len(args)])
         for ref, value in zip(refs[len(args) :], results):
-            ref[...] = value
+            if isinstance(value, list):
+                for a, row in enumerate(value):
+                    ref[:, a, :] = row
+            else:
+                ref[...] = value
 
     place = jnp.stack([r, c]).astype(jnp.int32)
     vmem = pl.BlockSpec(memory_space=pltpu.VMEM)
@@ -310,16 +355,13 @@
             stage_local, members, [(n, n), edge], grad_x, grad_y, t["q"], t["sp"], t["r"], t["vec"]
         )
         strip = exchange(edges, "col")
-        (lines,) = run_stage(
-            stage_strip, members, [edge],
-            strip, t["q"], t["r"], t["vec"], t["cb"], t["acs"], t["mats"], t["wf"],
-        )
-        lines = exchange(lines, "row")
-        (flux,) = run_stage(stage_edges, members, [edge], lines, t["gvec"], t["mats"])
-        flux = exchange(flux, "col")
+        share, keep = run_stage(
+            stage_strip, members, [(members, 5, n), (8, n)],
+            strip, t["q"], t["r"], t["vec"], t["glob"], t["cb"], t["acs"], t["mats"],
+        )
+        share = exchange(share, "row")
         (field,) = run_stage(
-            stage_field, members, [(n, n)],
-            flux, strip, u, t["q"], t["r"], t["vec"], t["cb"], t["acs"], t["mats"],
+            stage_field, members, [(n, n)], share, keep, u, t["q"], t["r"], t["vec"]
         )
         return field
 

time: 70.8 us -> 60.6 us (0.86)
  blocking collectives: 45.6 us -> 35.2 us
    all_to_all x3 -> x2, blocking collectives: 45.6 us -> 35.2 us  [exchange(): return lax.all_to_all(values, axis, split_axis=0, concat_axis=0, tiled=True)]
    pallas_call x4 -> x3, Pallas kernels: 24.2 us -> 24.5 us  [run_stage(): pl.pallas_call(kernel, out_shape=[jax.ShapeDtypeStruct(shape, f32) for sh...]
where the time goes in v2:
time: 60.6 us; the launch traced here: 60.3 us
  blocking collectives  35.2 us (58%)
  Pallas kernels  24.5 us (40%)
    all_to_all x2, blocking collectives, exchange(): return lax.all_to_all(values, axis, split_axis=0, concat_axis=0, tiled=True)  35.2 us
    pallas_call x3, Pallas kernels, run_stage(): pl.pallas_call(kernel, out_shape=[jax.ShapeDtypeStruct(shape, f32) for sh...  24.5 us

profile of v2, /device:TPU:1, one launch (start us, length us, event | category | flops | bytes accessed | tf_op | source)
XLA Modules:
  0.0 60.3 jit_solution(227918446174326162)
XLA Ops:
  0.0 0.6 pad_add_fusion.place
  0.6 7.7 %stage_local.1 = (f32[512,512]{1,0:T(8,128)}, f32[16,4,512]{2,1,0:T(4,128)}) custom-call(s32[2]{0:T(128)} %pad_add_fusion.place, f32[512,512]{1,0:T(8,128)} %refs_0_.1, f32[512,512]{1,0:T(8,128)} %refs_1_.2, f32[512,512]{1,0:T(8,128)} %constant.23.clone.refs_2_.refs_1_.refs_3_, f32[512,512]{1,0:T(8,128)} %constant.24.clone.refs_3_, ...), custom_call_target="tpu_custom_call" | custom-call | tf_op jit(solution)/shard_map/stage_local/pallas_call | solution.py:335
  8.3 17.7 %all_to_all.10.refs_0_ = f32[16,4,512]{2,1,0:T(4,128)} all-to-all(f32[16,4,512]{2,1,0:T(4,128)} %get-tuple-element.9), channel_id=1, replica_groups=mesh['row'=16,'col'=16] {'col'}, dimensions={0} | all-to-all | bytes 262144 | tf_op jit(solution)/shard_map/all_to_all | solution.py:346
  26.0 11.1 %stage_strip.1 = (f32[16,5,512]{2,1,0:T(8,128)}, f32[8,512]{1,0:T(8,128)}) custom-call(s32[2]{0:T(128)} %pad_add_fusion.place, f32[16,4,512]{2,1,0:T(4,128)} %all_to_all.10.refs_0_, f32[512,512]{1,0:T(8,128)} %constant.23.clone.refs_2_.refs_1_.refs_3_, f32[512,512]{1,0:T(8,128)} %constant.25.clone.refs_4_.refs_2_, f32[8,512]{1,0:T(8,128)} %constant.26.clone.refs_5_.refs_3_, ...), custom_call_target="tpu_custom_call" | custom-call | tf_op jit(solution)/shard_map/stage_strip/pallas_call | solution.py:335
  37.1 17.5 %all_to_all.11.refs_0_ = f32[16,5,512]{2,1,0:T(8,128)} all-to-all(f32[16,5,512]{2,1,0:T(8,128)} %get-tuple-element.10), channel_id=1, replica_groups=mesh['row'=16,'col'=16] {'row'}, dimensions={0} | all-to-all | bytes 327680 | tf_op jit(solution)/shard_map/all_to_all | solution.py:346
  54.6 5.7 %stage_field.1 = f32[512,512]{1,0:T(8,128)} custom-call(s32[2]{0:T(128)} %pad_add_fusion.place, f32[16,5,512]{2,1,0:T(8,128)} %all_to_all.11.refs_0_, f32[8,512]{1,0:T(8,128)} %get-tuple-element.11.refs_1_, f32[512,512]{1,0:T(8,128)} %get-tuple-element.12.refs_2_, f32[512,512]{1,0:T(8,128)} %constant.23.clone.refs_2_.refs_1_.refs_3_, ...), custom_call_target="tpu_custom_call" | custom-call | tf_op jit(solution)/shard_map/stage_field/pallas_call | solution.py:335

commit v3 on v2

--- a/solution.py
+++ b/solution.py
@@ -34,30 +34,20 @@
 def build_tables(n, members):
     total = n * members
     half = n // 2
-    q = cosine_basis(n)
-    k = np.arange(n)
+    k = np.concatenate([np.arange(0, n, 2), np.arange(1, n, 2)])
+    q = cosine_basis(n)[k]
     s = 2 * np.sin(np.pi * k / (2 * n))
-    den = s[:, None] ** 2 + s[None] ** 2
-    den[0, 0] = 1
-    r = 1 / den
-    r[0, 0] = 0
-    sp = np.zeros((n, n))
-    i = np.arange(n)[None]
-    sp = np.sqrt(2 / n) * s[:, None] * np.sin(np.pi * k[:, None] * (i + 1) / n)
-    sp[:, n - 1] = 0
-    sp[0] = 0
     q0, q1 = q[:, 0], q[:, -1]
     lead, e, couple = edge_tables(n, members, np.pi * k / (2 * n))
     vec = np.zeros((8, n))
     vec[0], vec[1], vec[2], vec[3], vec[4] = q0, q1, lead, e, couple
+    vec[5], vec[6] = s * s, 1
     m = np.arange(half)
     cls = np.arange(2 * members)
     kap = cls[:, None] + 2 * members * m[None]
     glob = np.stack(edge_tables(n, members, np.pi * kap / (2 * total)))
     j = 2 * np.arange(n) + 1
-    cb = np.concatenate(
-        [np.cos(np.pi * m[:, None] * j[None] / n), np.sin(np.pi * m[:, None] * j[None] / n)], 1
-    )
+    sb = np.sqrt(2 / n) * np.sin(np.pi * m[:, None] * j[None] / n)
     ang = np.pi * cls[:, None] * j[None] / (2 * total)
     acs = np.concatenate([np.cos(ang), np.sin(ang)], 0)
     p = np.arange(members)
@@ -107,7 +97,7 @@
     mats[9 * M : 10 * M, :M] = kt.T * qq
     mats[10 * M : 11 * M, :M] = (kh @ t1).T
     mats[11 * M : 15 * M, :M] = wfwd
-    out = dict(q=q, sp=sp, r=r, vec=vec, glob=glob, cb=cb, acs=acs, mats=mats)
+    out = dict(q=q, vec=vec, glob=glob, sb=sb, acs=acs, mats=mats)
     return {name: np.asarray(value, np.float32) for name, value in out.items()}
 
 
@@ -170,13 +160,20 @@
     return jnp.broadcast_to(one[None], (members,) + one.shape)
 
 
-def stage_local(r, c, M, gx, gy, q, sp, rr, vec):
-    gx, gy, q, sp, rr, vec = gx[...], gy[...], q[...], sp[...], rr[...], vec[...]
+def stage_local(r, c, M, gx, gy, q, vec):
+    q, vec = q[...], vec[...]
     n = q.shape[0]
     L = min(n, 128)
+    one, two = vec[6:7], vec[5:6]
+    pad = jnp.zeros((6, n), f32)
+    den = doth(jnp.concatenate([two, one, pad], 0), jnp.concatenate([one, two, pad], 0), 0, 0)
+    origin = (rows_of(den.shape) == 0) & (lanes_of(den.shape) == 0)
+    rr = jnp.where(origin, 0.0, 1.0 / jnp.where(origin, 1.0, den))
+    after = jnp.concatenate([q[:, 1:], q[:, :1]], 1)
+    sp = jnp.where(lanes_of(q.shape) == n - 1, 0.0, q - after)
     qs, ss = split(q), split(sp)
-    gys = split(gy)
-    m1 = dot3(gx, qs, 1, 1)
+    m1 = dot3(gx[...], qs, 1, 1)
+    gys = split(gy[...])
     m2 = dot3(gys, ss, 1, 1)
     u = -(dot3(ss, m1) + dot3(qs, m2)) * rr
     slab = (gys[0][:, n - L :], gys[1][:, n - L :])
@@ -186,14 +183,14 @@
     tl = dot3(vec, us, 1, 0)
     alpha = gyl + jnp.where(c < M - 1, tk[1:2], 0.0)
     beta = m1[n - 1 :] + jnp.where(r < M - 1, tl[1:2], 0.0)
-    return u, to_peers([alpha, tk[0:1], beta, tl[0:1]], M)
+    return to_peers([alpha, tk[0:1], beta, tl[0:1]], M), u, q, qs[0], qs[1], rr
 
 
 def lane_pick(values, index):
     return jnp.sum(jnp.where(lanes_of(values.shape) == index, values, 0.0), 1, keepdims=True)
 
 
-def stage_strip(r, c, M, ag, q, rr, vec, glob, cb, acs, mats):
+def stage_strip(r, c, M, ag, q, qh, ql, rr, vec, glob, sb, acs, mats):
     al, t0, be, ta0 = (ag[:, a, :] for a in range(4))
     vec, mats = vec[...], mats[...]
     n = al.shape[1]
@@ -221,10 +218,13 @@
         g = doth(wf, y[side * M : (side + 1) * M])
         C, S = g[: 2 * M], g[2 * M :]
         turned.append(jnp.concatenate([C * ca - S * sna, -(C * sna + S * ca)], 1))
-    T = doth(jnp.concatenate(turned, 0), cb[...], 1, 1)
+    turned = jnp.concatenate(turned, 0)
+    T = doth(turned[:, :n], q[:half, :], 1, 1) + doth(turned[:, n:], sb[...], 1, 1)
     shape = (2 * M, half)
-    origin = (rows_of(shape) == 0) & (lanes_of(shape) == 0)
-    scale = jnp.where(origin, math.sqrt(1.0 / (n * M)), math.sqrt(2.0 / (n * M)))
+    zeroth = lanes_of(shape) == 0
+    origin = (rows_of(shape) == 0) & zeroth
+    root = 1.0 / math.sqrt(M)
+    scale = jnp.where(zeroth & (rows_of(shape) > 0), root * math.sqrt(2.0), root)
     T1, T0 = T[: 2 * M] * scale, T[2 * M :] * scale
 
     own = rows_of((M, L)) == r
@@ -246,13 +246,15 @@
         )
         modes.append(jnp.where(origin, g0[m : m + 1, :1], value) * scale)
     modes.append(jnp.where(r == M - 1, T1, 0.0) * scale)
-    XX = dot3(jnp.concatenate(modes, 0), cb[...])
+    modes = split(jnp.concatenate(modes, 0))
+    XC = dot3(modes, (qh[:half, :], ql[:half, :]))
+    XS = dot3(modes, sb[...])
     wi = split(mats[4 * M : 5 * M, : 4 * M])
     lines = []
     for m in range(M):
-        xc, xs = XX[2 * M * m : 2 * M * (m + 1), :n], XX[2 * M * m : 2 * M * (m + 1), n:]
+        xc, xs = XC[2 * M * m : 2 * M * (m + 1)], XS[2 * M * m : 2 * M * (m + 1)]
         lines.append(dot3(wi, jnp.concatenate([ca * xc - sna * xs, sna * xc + ca * xs], 0)))
-    hx = dot3(jnp.concatenate(lines, 0), q[...], 1, 1)
+    hx = dot3(jnp.concatenate(lines, 0), (qh[...], ql[...]), 1, 1)
     rs = split(rr[...])
     Y0, Y1 = dot3(hx * q0, rs), dot3(hx * q1, rs)
 
@@ -295,9 +297,9 @@
     return share, jnp.concatenate(keep + [jnp.zeros((5, n), f32)], 0)
 
 
-def stage_field(r, c, M, share, keep, u, q, rr, vec):
+def stage_field(r, c, M, share, keep, u, qh, ql, rr, vec):
     keep, vec = keep[...], vec[...]
-    n = q.shape[0]
+    n = vec.shape[1]
     q0, q1 = vec[0:1], vec[1:2]
     left, right, here, before, level = (
         jnp.sum(share[:, a, :], 0, keepdims=True) for a in range(5)
@@ -311,18 +313,18 @@
     G = doth(lhs, rhs, 0, 0)
     un = u[...] - rr[...] * G
     un = jnp.where((rows_of(un.shape) == 0) & (lanes_of(un.shape) == 0), level, un)
-    qs = split(q[...])
+    qs = (qh[...], ql[...])
     return (dot3(qs, dot3(un, qs), 0, 0),)
 
 
 def run_stage(stage, members, outs, *args):
-    r, c = lax.axis_index("row"), lax.axis_index("col")
     if DIRECT:
-        results = stage(r, c, members, *args)
+        results = stage(lax.axis_index("row"), lax.axis_index("col"), members, *args)
         return [jnp.stack(v, 1) if isinstance(v, list) else v for v in results]
 
-    def kernel(place, *refs):
-        results = stage(place[0], place[1], members, *refs[: len(args)])
+    def kernel(*refs):
+        r, c = lax.axis_index("row"), lax.axis_index("col")
+        results = stage(r, c, members, *refs[: len(args)])
         for ref, value in zip(refs[len(args) :], results):
             if isinstance(value, list):
                 for a, row in enumerate(value):
@@ -330,16 +332,15 @@
             else:
                 ref[...] = value
 
-    place = jnp.stack([r, c]).astype(jnp.int32)
     vmem = pl.BlockSpec(memory_space=pltpu.VMEM)
     return pl.pallas_call(
         kernel,
-        out_shape=[jax.ShapeDtypeStruct(shape, f32) for shape in outs],
-        in_specs=[pl.BlockSpec(memory_space=pltpu.SMEM)] + [vmem] * len(args),
+        out_shape=outs,
+        in_specs=[vmem] * len(args),
         out_specs=[vmem] * len(outs),
-        compiler_params=pltpu.CompilerParams(vmem_limit_bytes=56 * 1024 * 1024),
+        compiler_params=pltpu.CompilerParams(vmem_limit_bytes=40 * 1024 * 1024),
         name=stage.__name__,
-    )(place, *args)
+    )(*args)
 
 
 def exchange(values, axis):
@@ -350,18 +351,22 @@
     def body(grad_x, grad_y):
         n = grad_x.shape[0]
         t = {k: jnp.asarray(v) for k, v in build_tables(n, members).items()}
-        edge = (members, 4, n)
-        u, edges = run_stage(
-            stage_local, members, [(n, n), edge], grad_x, grad_y, t["q"], t["sp"], t["r"], t["vec"]
+        sent, near = jax.ShapeDtypeStruct, pltpu.VMEM
+        edges, u, q, qh, ql, rr = run_stage(
+            stage_local,
+            members,
+            [sent((members, 4, n), f32), near((n, n), f32), near((n, n), f32)]
+            + [near((n, n), bf16), near((n, n), bf16), near((n, n), f32)],
+            grad_x, grad_y, t["q"], t["vec"],
         )
         strip = exchange(edges, "col")
         share, keep = run_stage(
-            stage_strip, members, [(members, 5, n), (8, n)],
-            strip, t["q"], t["r"], t["vec"], t["glob"], t["cb"], t["acs"], t["mats"],
+            stage_strip, members, [sent((members, 5, n), f32), near((8, n), f32)],
+            strip, q, qh, ql, rr, t["vec"], t["glob"], t["sb"], t["acs"], t["mats"],
         )
         share = exchange(share, "row")
         (field,) = run_stage(
-            stage_field, members, [(n, n)], share, keep, u, t["q"], t["r"], t["vec"]
+            stage_field, members, [sent((n, n), f32)], share, keep, u, qh, ql, rr, t["vec"]
         )
         return field
 

time: 60.6 us -> 57 us (0.941)
  Pallas kernels: 24.5 us -> 17.5 us
  local copies, waits for them, and re-layouts: 0 us -> 4.41 us
    pallas_call x3, Pallas kernels: 24.5 us -> 17.5 us  [run_stage(): pl.pallas_call(kernel, out_shape=outs, in_specs=[vmem] * len(args), out_s...]
    unnamed x0 -> x16, local copies, waits for them, and re-layouts: none -> 4.41 us
where the time goes in v3:
time: 57 us; the launch traced here: 56.7 us
  blocking collectives  34.7 us (61%)
  Pallas kernels  17.5 us (31%)
  local copies, waits for them, and re-layouts  4.41 us (8%)
    all_to_all x2, blocking collectives, exchange(): return lax.all_to_all(values, axis, split_axis=0, concat_axis=0, tiled=True)  34.7 us
    pallas_call x3, Pallas kernels, run_stage(): pl.pallas_call(kernel, out_shape=outs, in_specs=[vmem] * len(args), out_s...  17.5 us
    unnamed x16, local copies, waits for them, and re-layouts  4.41 us

profile of v3, /device:TPU:1, one launch (start us, length us, event | category | flops | bytes accessed | tf_op | source)
XLA Modules:
  0.0 56.7 jit_solution(4597051984384767015)
XLA Ops:
  0.0 0.0 copy-start
  0.0 1.2 %copy-done = f32[512,512]{1,0:T(8,128)S(1)} copy-done((f32[512,512]{1,0:T(8,128)S(1)}, f32[512,512]{1,0:T(8,128)}, u32[]{:S(2)}) %copy-start) | copy-done | bytes 1048600
  1.2 0.0 copy-start.1
  1.2 1.2 %copy-done.1 = f32[512,512]{1,0:T(8,128)S(1)} copy-done((f32[512,512]{1,0:T(8,128)S(1)}, f32[512,512]{1,0:T(8,128)}, u32[]{:S(2)}) %copy-start.1) | copy-done | bytes 1048600
  2.5 0.0 copy-start.2
  2.5 1.2 %copy-done.2 = f32[512,512]{1,0:T(8,128)S(1)} copy-done((f32[512,512]{1,0:T(8,128)S(1)}, f32[512,512]{1,0:T(8,128)}, u32[]{:S(2)}) %copy-start.2) | copy-done | bytes 1048600
  3.7 0.0 copy-start.4
  3.7 0.7 %copy-done.4 = f32[8,512]{1,0:T(8,128)S(1)} copy-done((f32[8,512]{1,0:T(8,128)S(1)}, f32[8,512]{1,0:T(8,128)}, u32[]{:S(2)}) %copy-start.4) | copy-done | bytes 16408
  4.4 0.0 copy-start.3
  4.4 0.0 copy-start.7
  4.4 5.4 %stage_local.1 = (f32[16,4,512]{2,1,0:T(4,128)S(1)}, f32[512,512]{1,0:T(8,128)S(1)}, f32[512,512]{1,0:T(8,128)S(1)}, bf16[512,512]{1,0:T(8,128)(2,1)S(1)}, bf16[...) custom-call(f32[512,512]{1,0:T(8,128)S(1)} %copy-done, f32[512,512]{1,0:T(8,128)S(1)} %copy-done.1, ...), custom_call_target="tpu_custom_call" | custom-call | tf_op jit(solution)/shard_map/stage_local/pallas_call | solution.py:336
  9.8 0.0 copy-start.5
  9.8 0.0 copy-start.6
  9.8 17.5 %all_to_all.10.refs_0_ = f32[16,4,512]{2,1,0:T(4,128)S(1)} all-to-all(f32[16,4,512]{2,1,0:T(4,128)S(1)} %get-tuple-element.13), channel_id=1, replica_groups=mesh['row'=16,'col'=16] {'col'}, dimensions={0} | all-to-all | bytes 262144 | tf_op jit(solution)/shard_map/all_to_all | solution.py:347
  27.3 0.0 copy-done.3
  27.3 0.0 copy-done.7
  27.3 0.0 copy-done.5
  27.3 0.0 copy-done.6
  27.3 8.4 %stage_strip.1 = (f32[16,5,512]{2,1,0:T(8,128)S(1)}, f32[8,512]{1,0:T(8,128)S(1)}) custom-call(f32[16,4,512]{2,1,0:T(4,128)S(1)} %all_to_all.10.refs_0_, f32[512,512]{1,0:T(8,128)S(1)} %get-tuple-element.14.refs_1_, bf16[512,512]{1,0:T(8,128)(2,1)S(1)} %get-tuple-element.15.refs_2_.refs_3_, bf16[512,512]{1,0:T(8,128)(2,1)S(1)} %get-tuple-element.16.refs_3_.refs_4_, ...), custom_call_target="tpu_custom_call" | custom-call | tf_op jit(solution)/shard_map/stage_strip/pallas_call | solution.py:336
  35.7 17.2 %all_to_all.11.refs_0_ = f32[16,5,512]{2,1,0:T(8,128)S(1)} all-to-all(f32[16,5,512]{2,1,0:T(8,128)S(1)} %get-tuple-element.18), channel_id=1, replica_groups=mesh['row'=16,'col'=16] {'row'}, dimensions={0} | all-to-all | bytes 327680 | tf_op jit(solution)/shard_map/all_to_all | solution.py:347
  52.9 3.7 %stage_field.1 = f32[512,512]{1,0:T(8,128)} custom-call(f32[16,5,512]{2,1,0:T(8,128)S(1)} %all_to_all.11.refs_0_, f32[8,512]{1,0:T(8,128)S(1)} %get-tuple-element.19.refs_1_, f32[512,512]{1,0:T(8,128)S(1)} %get-tuple-element.20.refs_2_, bf16[512,512]{1,0:T(8,128)(2,1)S(1)} %get-tuple-element.15.refs_2_.refs_3_, ...), custom_call_target="tpu_custom_call" | custom-call | tf_op jit(solution)/shard_map/stage_field/pallas_call | solution.py:336
Async XLA Ops:
  0.0 1.2 %copy-start = (f32[512,512]{1,0:T(8,128)S(1)}, f32[512,512]{1,0:T(8,128)}, u32[]{:S(2)}) copy-start(f32[512,512]{1,0:T(8,128)} %refs_0_.1) | copy-start | bytes 3145732
  1.2 1.2 %copy-start.1 = (f32[512,512]{1,0:T(8,128)S(1)}, f32[512,512]{1,0:T(8,128)}, u32[]{:S(2)}) copy-start(f32[512,512]{1,0:T(8,128)} %refs_1_.1) | copy-start | bytes 3145732
  2.5 1.2 %copy-start.2 = (f32[512,512]{1,0:T(8,128)S(1)}, f32[512,512]{1,0:T(8,128)}, u32[]{:S(2)}) copy-start(f32[512,512]{1,0:T(8,128)} %constant.12.clone.refs_2_) | copy-start | bytes 3145732
  3.7 0.7 %copy-start.4 = (f32[8,512]{1,0:T(8,128)S(1)}, f32[8,512]{1,0:T(8,128)}, u32[]{:S(2)}) copy-start(f32[8,512]{1,0:T(8,128)} %constant.13.clone.refs_3_.refs_5_.refs_6_) | copy-start | bytes 49156
  4.4 22.9 %copy-start.3 = (f32[256,512]{1,0:T(8,128)S(1)}, f32[256,512]{1,0:T(8,128)}, u32[]{:S(2)}) copy-start(f32[256,512]{1,0:T(8,128)} %constant.15.clone.refs_7_) | copy-start | bytes 1572868
  4.4 22.9 %copy-start.7 = (f32[3,32,256]{2,1,0:T(8,128)S(1)}, f32[3,32,256]{2,1,0:T(8,128)}, u32[]{:S(2)}) copy-start(f32[3,32,256]{2,1,0:T(8,128)} %constant.14.clone.refs_6_) | copy-start | bytes 294916
  9.8 17.5 %copy-start.5 = (f32[64,512]{1,0:T(8,128)S(1)}, f32[64,512]{1,0:T(8,128)}, u32[]{:S(2)}) copy-start(f32[64,512]{1,0:T(8,128)} %constant.16.clone.refs_8_) | copy-start | bytes 393220
  9.8 17.5 %copy-start.6 = (f32[240,128]{1,0:T(8,128)S(1)}, f32[240,128]{1,0:T(8,128)}, u32[]{:S(2)}) copy-start(f32[240,128]{1,0:T(8,128)} %constant.17.clone.refs_9_) | copy-start | bytes 368644

commit v4 on v3

--- a/solution.py
+++ b/solution.py
@@ -8,6 +8,7 @@
 from jax.experimental.pallas import tpu as pltpu
 from jax.sharding import PartitionSpec as P
 
+VMEM_LIMIT = 32 * 1024 * 1024
 DIRECT = False
 f32 = jnp.float32
 bf16 = jnp.bfloat16
@@ -41,13 +42,24 @@
     lead, e, couple = edge_tables(n, members, np.pi * k / (2 * n))
     vec = np.zeros((8, n))
     vec[0], vec[1], vec[2], vec[3], vec[4] = q0, q1, lead, e, couple
-    vec[5], vec[6] = s * s, 1
     m = np.arange(half)
     cls = np.arange(2 * members)
     kap = cls[:, None] + 2 * members * m[None]
     glob = np.stack(edge_tables(n, members, np.pi * kap / (2 * total)))
+    bend = 1 + glob[1] ** 2 - 2 * glob[1] * np.cos(np.pi * np.arange(1, members) / members)[:, None, None]
+    size = np.full((2 * members, half), 1 / np.sqrt(members))
+    size[1:, 0] *= np.sqrt(2)
+    dens = (glob[0] * size / bend).reshape(-1, half)
     j = 2 * np.arange(n) + 1
     sb = np.sqrt(2 / n) * np.sin(np.pi * m[:, None] * j[None] / n)
+    turn = np.concatenate([q[:half].T, sb.T], 0)
+    sp = np.sqrt(2 / n) * s[:, None] * np.sin(np.pi * k[:, None] * (np.arange(n)[None] + 1) / n)
+    sp[:, n - 1] = 0
+    sp[0] = 0
+    den = s[:, None] ** 2 + s[None] ** 2
+    den[0, 0] = 1
+    r = 1 / den
+    r[0, 0] = 0
     ang = np.pi * cls[:, None] * j[None] / (2 * total)
     acs = np.concatenate([np.cos(ang), np.sin(ang)], 0)
     p = np.arange(members)
@@ -85,6 +97,8 @@
     s2x = s2.copy()
     s2x[M - 1, M - 1] = 1
     mats = np.zeros((15 * M, 128))
+    per = min(M, n // (2 * M), 256 // (4 * M))
+    wbd = np.kron(np.eye(per), winv)
     mats[0:M, : 2 * M] = np.concatenate([sa, stt], 1)
     mats[M : 2 * M, :M] = s2
     mats[2 * M : 3 * M, : 2 * M] = hmat
@@ -97,8 +111,15 @@
     mats[9 * M : 10 * M, :M] = kt.T * qq
     mats[10 * M : 11 * M, :M] = (kh @ t1).T
     mats[11 * M : 15 * M, :M] = wfwd
-    out = dict(q=q, vec=vec, glob=glob, sb=sb, acs=acs, mats=mats)
-    return {name: np.asarray(value, np.float32) for name, value in out.items()}
+    out = dict(r=r, vec=vec, couple=glob[2], dens=dens, acs=acs, mats=mats)
+    out = {name: np.asarray(value, np.float32) for name, value in out.items()}
+    for name, value, pieces in (
+        ("q", q, 3), ("s", sp, 2), ("r", r, 3), ("t", turn, 3), ("b", sb, 2), ("w", wbd, 3)
+    ):
+        for i in range(pieces):
+            out[f"{name}{i + 1}"] = np.asarray(value, jnp.bfloat16)
+            value = value - out[f"{name}{i + 1}"].astype(np.float64)
+    return out
 
 
 def split(a):
@@ -114,6 +135,38 @@
     ah, al = a if isinstance(a, tuple) else split(a)
     bh, bl = b if isinstance(b, tuple) else split(b)
     return mm(ah, bh, ca, cb) + (mm(ah, bl, ca, cb) + mm(al, bh, ca, cb))
+
+
+def split3(a):
+    high, rest = a.astype(bf16), None
+    rest = a - high.astype(f32)
+    mid = rest.astype(bf16)
+    return high, mid, (rest - mid.astype(f32)).astype(bf16)
+
+
+def dot6(a, b, cb=0):
+    m = a.shape[0]
+    a1, a2, a3 = split3(a)
+    b1, b2, b3 = b
+    p = mm(jnp.concatenate([a1, a2, a3], 0), b1, 1, cb)
+    q = mm(jnp.concatenate([a1, a2], 0), b2, 1, cb)
+    small = (p[2 * m :] + q[m:]) + mm(a1, b3, 1, cb)
+    return p[:m] + ((p[m : 2 * m] + q[:m]) + small)
+
+
+def dotl(a, b):
+    m = a[0].shape[0]
+    b1, b2, b3 = split3(b)
+    p = mm(jnp.concatenate(a, 0), b1, 1, 0)
+    q = mm(jnp.concatenate(a[:2], 0), b2, 1, 0)
+    small = (p[2 * m :] + q[m:]) + mm(a[0], b3, 1, 0)
+    return p[:m] + ((p[m : 2 * m] + q[:m]) + small)
+
+
+def doths(a, qs):
+    value = dot3(a, qs, 1, 1)
+    exact = jnp.sum(a, 1, keepdims=True) * (1.0 / math.sqrt(a.shape[1]))
+    return jnp.where(lanes_of(value.shape) == 0, exact, value)
 
 
 def doth(a, b, ca=1, cb=0):
@@ -160,42 +213,98 @@
     return jnp.broadcast_to(one[None], (members,) + one.shape)
 
 
-def stage_local(r, c, M, gx, gy, q, vec):
-    q, vec = q[...], vec[...]
-    n = q.shape[0]
+def stage_local(r, c, M, need, vec):
+    vec = vec[...]
+    n = vec.shape[1]
     L = min(n, 128)
-    one, two = vec[6:7], vec[5:6]
-    pad = jnp.zeros((6, n), f32)
-    den = doth(jnp.concatenate([two, one, pad], 0), jnp.concatenate([one, two, pad], 0), 0, 0)
-    origin = (rows_of(den.shape) == 0) & (lanes_of(den.shape) == 0)
-    rr = jnp.where(origin, 0.0, 1.0 / jnp.where(origin, 1.0, den))
-    after = jnp.concatenate([q[:, 1:], q[:, :1]], 1)
-    sp = jnp.where(lanes_of(q.shape) == n - 1, 0.0, q - after)
-    qs, ss = split(q), split(sp)
-    m1 = dot3(gx[...], qs, 1, 1)
-    gys = split(gy[...])
+    qs = (need("q1"), need("q2"))
+    m1 = dot3(need("x"), qs, 1, 1)
+    ss = (need("s1"), need("s2"))
+    gys = split(need("y"))
     m2 = dot3(gys, ss, 1, 1)
-    u = -(dot3(ss, m1) + dot3(qs, m2)) * rr
     slab = (gys[0][:, n - L :], gys[1][:, n - L :])
     gyl = dot3(slab, qs, 0, 1)[L - 1 :]
+    f = dot3(ss, m1) + dot3(qs, m2)
+    u = -f * need("r")
     us = split(u)
     tk = dot3(vec, us, 1, 1)
     tl = dot3(vec, us, 1, 0)
     alpha = gyl + jnp.where(c < M - 1, tk[1:2], 0.0)
     beta = m1[n - 1 :] + jnp.where(r < M - 1, tl[1:2], 0.0)
-    return to_peers([alpha, tk[0:1], beta, tl[0:1]], M), u, q, qs[0], qs[1], rr
+    return to_peers([alpha, tk[0:1], beta, tl[0:1]], M), u
+
+
+FIRST = ("q1", "q2", "x", "s1", "s2", "y", "r")
+LATER = ("q3", "r1", "r2", "r3", "t1", "t2", "t3", "b1", "b2", "w1", "w2", "w3")
+LATER += ("dens", "couple", "acs", "mats")
+KEPT = ("q1", "q2", "r") + LATER
+
+
+def run_local(members, arrays, vec):
+    n = vec.shape[1]
+    if DIRECT:
+        edges, u = stage_local(
+            lax.axis_index("row"), lax.axis_index("col"), members, arrays.__getitem__, vec
+        )
+        return edges, u, {name: arrays[name] for name in KEPT}
+
+    names = FIRST + LATER
+
+    def kernel(*refs):
+        count = len(names)
+        sources, vec = refs[:count], refs[count]
+        edges, u = refs[count + 1 : count + 3]
+        here = dict(zip(KEPT, refs[count + 3 :]))
+        here.update(zip((k for k in FIRST if k not in KEPT), refs[count + 3 + len(KEPT) :]))
+        sem = refs[-1]
+        copies = {
+            name: pltpu.make_async_copy(source, here[name], sem.at[i])
+            for i, (name, source) in enumerate(zip(names, sources))
+        }
+        for name in FIRST:
+            copies[name].start()
+
+        def need(name):
+            copies[name].wait()
+            if name == "y":
+                for later in LATER:
+                    copies[later].start()
+            return here[name][...]
+
+        edges[...], u[...] = stage_local(
+            lax.axis_index("row"), lax.axis_index("col"), members, need, vec
+        )
+        for name in LATER:
+            copies[name].wait()
+
+    far, vmem, near = pl.BlockSpec(memory_space=pltpu.HBM), pl.BlockSpec(memory_space=pltpu.VMEM), pltpu.VMEM
+    shape = {name: near(arrays[name].shape, arrays[name].dtype) for name in names}
+    edges, u, *tables = pl.pallas_call(
+        kernel,
+        out_shape=[jax.ShapeDtypeStruct((members, 4, n), f32), near((n, n), f32)]
+        + [shape[name] for name in KEPT],
+        in_specs=[far] * len(names) + [vmem],
+        out_specs=[vmem] * (2 + len(KEPT)),
+        scratch_shapes=[shape[name] for name in FIRST if name not in KEPT]
+        + [pltpu.SemaphoreType.DMA((len(names),))],
+        compiler_params=pltpu.CompilerParams(vmem_limit_bytes=VMEM_LIMIT),
+        name="stage_local",
+    )(*(pltpu.with_memory_space_constraint(arrays[name], pltpu.HBM) for name in names), vec)
+    return edges, u, dict(zip(KEPT, tables))
 
 
 def lane_pick(values, index):
     return jnp.sum(jnp.where(lanes_of(values.shape) == index, values, 0.0), 1, keepdims=True)
 
 
-def stage_strip(r, c, M, ag, q, qh, ql, rr, vec, glob, sb, acs, mats):
+def stage_strip(
+    r, c, M, ag, q1, q2, q3, r1, r2, r3, t1, t2, t3, b1, b2, w1, w2, w3, dens, gcouple, vec, acs, mats
+):
     al, t0, be, ta0 = (ag[:, a, :] for a in range(4))
     vec, mats = vec[...], mats[...]
     n = al.shape[1]
     half = n // 2
-    q0, q1, lead, e, couple = (vec[a : a + 1] for a in range(5))
+    v0, v1, lead, e, couple = (vec[a : a + 1] for a in range(5))
     L = min(n, 128)
     qq = 1.0 / math.sqrt(n)
     zero = jnp.zeros((M, L), f32)
@@ -203,14 +312,16 @@
     cosphi = mats[5 * M : 6 * M, :1]
 
     H, mean = edge_solve(al, t0, lead, e, couple, zero, mats, True)
-    Z = doth(jnp.concatenate([H * q0, H * q1], 0), rr[...])
-    add0 = q0 * below(Z[:M]) - q1 * Z[:M]
-    add1 = q0 * below(Z[M:]) - q1 * Z[M:]
+    rs = (r1[...], r2[...])
+    Z = dot6(jnp.concatenate([H * v0, H * v1], 0), rs + (r3[...],))
+    add0 = v0 * below(Z[:M]) - v1 * Z[:M]
+    add1 = v0 * below(Z[M:]) - v1 * Z[M:]
     flat = jnp.where(lanes_of((M, n)) == 0, mean * qq, 0.0)
     tau0 = ta0 + add0 + flat
     tau1 = be + jnp.where(r < M - 1, add1 + flat, 0.0)
 
-    y = doth(jnp.concatenate([tau1, tau0], 0), q[...])
+    qs = (q1[...], q2[...])
+    y = dot6(jnp.concatenate([tau1, tau0], 0), qs + (q3[...],))
     wf = mats[11 * M : 15 * M, :M]
     ca, sna = acs[0 : 2 * M, :], acs[2 * M : 4 * M, :]
     turned = []
@@ -218,8 +329,7 @@
         g = doth(wf, y[side * M : (side + 1) * M])
         C, S = g[: 2 * M], g[2 * M :]
         turned.append(jnp.concatenate([C * ca - S * sna, -(C * sna + S * ca)], 1))
-    turned = jnp.concatenate(turned, 0)
-    T = doth(turned[:, :n], q[:half, :], 1, 1) + doth(turned[:, n:], sb[...], 1, 1)
+    T = dot6(jnp.concatenate(turned, 0), (t1[...], t2[...], t3[...]))
     shape = (2 * M, half)
     zeroth = lanes_of(shape) == 0
     origin = (rows_of(shape) == 0) & zeroth
@@ -234,29 +344,27 @@
     Hz = doth(mats[2 * M : 3 * M, : 2 * M], jnp.concatenate([alz, src], 0))
     lift = doth(mats[3 * M : 4 * M, : 3 * M], jnp.concatenate([alz, t0z, Hz], 0))
     g0 = jnp.where(rows_of((M, L)) == M - 1, Hz, doth(s2, Hz))
-    ge = glob[1]
     up, down = lane_pick(sa, r), lane_pick(stt, r)
-    T1c = jnp.where(r == M - 1, T1 * glob[2], T1)
-    top, bottom = glob[0] * T1c, glob[0] * T0
-    quad = 1.0 + ge * ge
+    T1c = jnp.where(r == M - 1, T1 * gcouple[...], T1)
     modes = []
     for m in range(M - 1):
-        value = (up[m : m + 1] * top + down[m : m + 1] * bottom) / (
-            quad - ge * (2.0 * cosphi[m : m + 1])
-        )
-        modes.append(jnp.where(origin, g0[m : m + 1, :1], value) * scale)
+        value = (up[m : m + 1] * T1c + down[m : m + 1] * T0) * dens[2 * M * m : 2 * M * (m + 1), :]
+        modes.append(jnp.where(origin, g0[m : m + 1, :1] * root, value))
     modes.append(jnp.where(r == M - 1, T1, 0.0) * scale)
     modes = split(jnp.concatenate(modes, 0))
-    XC = dot3(modes, (qh[:half, :], ql[:half, :]))
-    XS = dot3(modes, sb[...])
-    wi = split(mats[4 * M : 5 * M, : 4 * M])
+    XC = dot3(modes, (qs[0][:half], qs[1][:half]))
+    XS = dot3(modes, (b1[...], b2[...]))
+    ws = (w1[...], w2[...], w3[...])
+    group = w1.shape[1] // (4 * M)
     lines = []
-    for m in range(M):
-        xc, xs = XC[2 * M * m : 2 * M * (m + 1)], XS[2 * M * m : 2 * M * (m + 1)]
-        lines.append(dot3(wi, jnp.concatenate([ca * xc - sna * xs, sna * xc + ca * xs], 0)))
-    hx = dot3(jnp.concatenate(lines, 0), (qh[...], ql[...]), 1, 1)
-    rs = split(rr[...])
-    Y0, Y1 = dot3(hx * q0, rs), dot3(hx * q1, rs)
+    for first in range(0, M, group):
+        rots = []
+        for m in range(first, first + group):
+            xc, xs = XC[2 * M * m : 2 * M * (m + 1)], XS[2 * M * m : 2 * M * (m + 1)]
+            rots += [ca * xc - sna * xs, sna * xc + ca * xs]
+        lines.append(dotl(ws, jnp.concatenate(rots, 0)))
+    hx = doths(jnp.concatenate(lines, 0), qs)
+    Y0, Y1 = dot3(hx * v0, rs), dot3(hx * v1, rs)
 
     D = lead / (1.0 + e * e - 2.0 * e * cosphi)
     inner = rows_of((M, n)) < M - 1
@@ -289,9 +397,9 @@
     share = [
         below(right),
         right,
-        q0 * below(fc) - q1 * fc,
-        q0 * below(fb) - q1 * fb,
-        jnp.broadcast_to(lv, (M, n)),
+        v0 * below(fc) - v1 * fc,
+        v0 * below(fb) - v1 * fb,
+        lv,
     ]
     keep = [pick(H, c), pick(H, c - 1), jnp.broadcast_to(pick(mean, c), (1, n))]
     return share, jnp.concatenate(keep + [jnp.zeros((5, n), f32)], 0)
@@ -302,11 +410,11 @@
     n = vec.shape[1]
     q0, q1 = vec[0:1], vec[1:2]
     left, right, here, before, level = (
-        jnp.sum(share[:, a, :], 0, keepdims=True) for a in range(5)
+        jnp.sum(share[:, a, :n] if a < 4 else share[:, 0, n:], 0, keepdims=True) for a in range(5)
     )
     here = here + keep[0:1]
     before = before + keep[1:2]
-    level = (level + keep[2:3])[:, :1]
+    level = level[:, :1] + keep[2:3, :1]
     pad = jnp.zeros((4, n), f32)
     lhs = jnp.concatenate([q1, -q0, here, -before, pad], 0)
     rhs = jnp.concatenate([right, left, q1, q0, pad], 0)
@@ -317,18 +425,25 @@
     return (dot3(qs, dot3(un, qs), 0, 0),)
 
 
+def packed(rows):
+    tail = jnp.broadcast_to(rows[4][:, :, None], rows[4].shape[:1] + (4, 128))
+    return jnp.concatenate([jnp.stack(rows[:4], 1), tail], 2)
+
+
 def run_stage(stage, members, outs, *args):
     if DIRECT:
         results = stage(lax.axis_index("row"), lax.axis_index("col"), members, *args)
-        return [jnp.stack(v, 1) if isinstance(v, list) else v for v in results]
+        return [packed(v) if isinstance(v, list) else v for v in results]
 
     def kernel(*refs):
         r, c = lax.axis_index("row"), lax.axis_index("col")
+        n = args[0].shape[-1]
         results = stage(r, c, members, *refs[: len(args)])
         for ref, value in zip(refs[len(args) :], results):
             if isinstance(value, list):
-                for a, row in enumerate(value):
-                    ref[:, a, :] = row
+                for a, row in enumerate(value[:4]):
+                    ref[:, a, :n] = row
+                ref[:, :, n:] = jnp.broadcast_to(value[4][:, :, None], (members, 4, 128))
             else:
                 ref[...] = value
 
@@ -338,7 +453,7 @@
         out_shape=outs,
         in_specs=[vmem] * len(args),
         out_specs=[vmem] * len(outs),
-        compiler_params=pltpu.CompilerParams(vmem_limit_bytes=40 * 1024 * 1024),
+        compiler_params=pltpu.CompilerParams(vmem_limit_bytes=VMEM_LIMIT),
         name=stage.__name__,
     )(*args)
 
@@ -352,21 +467,18 @@
         n = grad_x.shape[0]
         t = {k: jnp.asarray(v) for k, v in build_tables(n, members).items()}
         sent, near = jax.ShapeDtypeStruct, pltpu.VMEM
-        edges, u, q, qh, ql, rr = run_stage(
-            stage_local,
-            members,
-            [sent((members, 4, n), f32), near((n, n), f32), near((n, n), f32)]
-            + [near((n, n), bf16), near((n, n), bf16), near((n, n), f32)],
-            grad_x, grad_y, t["q"], t["vec"],
-        )
+        edges, u, kept = run_local(members, {**t, "x": grad_x, "y": grad_y}, t["vec"])
         strip = exchange(edges, "col")
+        names = LATER[:-2] + ("vec",) + LATER[-2:]
+        kept["vec"] = t["vec"]
         share, keep = run_stage(
-            stage_strip, members, [sent((members, 5, n), f32), near((8, n), f32)],
-            strip, q, qh, ql, rr, t["vec"], t["glob"], t["sb"], t["acs"], t["mats"],
+            stage_strip, members, [sent((members, 4, n + 128), f32), near((8, n), f32)],
+            strip, kept["q1"], kept["q2"], *(kept[name] for name in names),
         )
         share = exchange(share, "row")
         (field,) = run_stage(
-            stage_field, members, [sent((n, n), f32)], share, keep, u, qh, ql, rr, t["vec"]
+            stage_field, members, [sent((n, n), f32)],
+            share, keep, u, kept["q1"], kept["q2"], kept["r"], t["vec"],
         )
         return field
 

time: 57 us -> 51.6 us (0.905)
  local copies, waits for them, and re-layouts: 4.41 us -> 0.72 us
  blocking collectives: 34.7 us -> 33.7 us
  Pallas kernels: 17.5 us -> 16.9 us
    pallas_call x3 -> x2, Pallas kernels: 17.5 us -> 10 us  [run_stage(): pl.pallas_call(kernel, out_shape=outs, in_specs=[vmem] * len(args), out_s...]
    pallas_call x0 -> x1, Pallas kernels: none -> 6.84 us  [run_local(): pl.pallas_call(kernel, out_shape=[jax.ShapeDtypeStruct((members, 4, n), f...]
    unnamed x16 -> x2, local copies, waits for them, and re-layouts: 4.41 us -> 0.72 us
    all_to_all x2, blocking collectives: 34.7 us -> 33.7 us  [exchange(): return lax.all_to_all(values, axis, split_axis=0, concat_axis=0, tiled=True)]
where the time goes in v4:
time: 51.6 us; the launch traced here: 51.3 us
  blocking collectives  33.7 us (65%)
  Pallas kernels  16.9 us (33%)
  local copies, waits for them, and re-layouts  0.72 us (1%)
    all_to_all x2, blocking collectives, exchange(): return lax.all_to_all(values, axis, split_axis=0, concat_axis=0, tiled=True)  33.7 us
    pallas_call x2, Pallas kernels, run_stage(): pl.pallas_call(kernel, out_shape=outs, in_specs=[vmem] * len(args), out_s...  10 us
    pallas_call x1, Pallas kernels, run_local(): pl.pallas_call(kernel, out_shape=[jax.ShapeDtypeStruct((members, 4, n), f...  6.84 us

profile of v4, /device:TPU:1, one launch (start us, length us, event | category | flops | bytes accessed | tf_op | source)
XLA Modules:
  0.0 51.3 jit_solution(8513801802145305269)
XLA Ops:
  0.0 0.0 copy-start
  0.0 0.7 %copy-done = f32[8,512]{1,0:T(8,128)S(1)} copy-done((f32[8,512]{1,0:T(8,128)S(1)}, f32[8,512]{1,0:T(8,128)}, u32[]{:S(2)}) %copy-start) | copy-done | bytes 16408
  0.7 6.8 %stage_local.1 = (f32[16,4,512]{2,1,0:T(4,128)S(1)}, f32[512,512]{1,0:T(8,128)S(1)}, bf16[512,512]{1,0:T(8,128)(2,1)S(1)}, bf16[512,512]{1,0:T(8,128)(2,1)S(1)},...) custom-call(bf16[512,512]{1,0:T(8,128)(2,1)} %constant.50.clone.refs, ...), custom_call_target="tpu_custom_call" | custom-call | tf_op jit(solution)/shard_map/stage_local/pallas_call | solution.py:282
  7.6 17.3 %all_to_all.10.refs_0_ = f32[16,4,512]{2,1,0:T(4,128)S(1)} all-to-all(f32[16,4,512]{2,1,0:T(4,128)S(1)} %get-tuple-element.28), channel_id=1, replica_groups=mesh['row'=16,'col'=16] {'col'}, dimensions={0} | all-to-all | bytes 262144 | tf_op jit(solution)/shard_map/all_to_all | solution.py:462
  24.9 6.3 %stage_strip.1 = (f32[16,4,640]{2,1,0:T(4,128)S(1)}, f32[8,512]{1,0:T(8,128)S(1)}) custom-call(f32[16,4,512]{2,1,0:T(4,128)S(1)} %all_to_all.10.refs_0_, bf16[512,512]{1,0:T(8,128)(2,1)S(1)} %get-tuple-element.29.refs_1_.refs_3_, bf16[512,512]{1,0:T(8,128)(2,1)S(1)} %get-tuple-element.30.refs_2_.refs_4_, bf16[512,512]{1,0:T(8,128)(2,1)S(1)} %get-tuple-element.31.refs_3_, ...), custom_call_target="tpu_custom_call" | custom-call | tf_op jit(solution)/shard_map/stage_strip/pallas_call | solution.py:451
  31.2 16.4 %all_to_all.11.refs_0_ = f32[16,4,640]{2,1,0:T(4,128)S(1)} all-to-all(f32[16,4,640]{2,1,0:T(4,128)S(1)} %get-tuple-element.47), channel_id=1, replica_groups=mesh['row'=16,'col'=16] {'row'}, dimensions={0} | all-to-all | bytes 327680 | tf_op jit(solution)/shard_map/all_to_all | solution.py:462
  47.6 3.7 %stage_field.1 = f32[512,512]{1,0:T(8,128)} custom-call(f32[16,4,640]{2,1,0:T(4,128)S(1)} %all_to_all.11.refs_0_, f32[8,512]{1,0:T(8,128)S(1)} %get-tuple-element.48.refs_1_, f32[512,512]{1,0:T(8,128)S(1)} %get-tuple-element.49.refs_2_, bf16[512,512]{1,0:T(8,128)(2,1)S(1)} %get-tuple-element.29.refs_1_.refs_3_, ...), custom_call_target="tpu_custom_call" | custom-call | tf_op jit(solution)/shard_map/stage_field/pallas_call | solution.py:451
Async XLA Ops:
  0.0 0.7 %copy-start = (f32[8,512]{1,0:T(8,128)S(1)}, f32[8,512]{1,0:T(8,128)}, u32[]{:S(2)}) copy-start(f32[8,512]{1,0:T(8,128)} %constant.45.clone.refs_23_.refs_17_.refs_6_) | copy-start | bytes 49156

commit v5 on v4

--- a/solution.py
+++ b/solution.py
@@ -30,6 +30,19 @@
     lead = one * th * (1 - e1 * e1)
     couple = one * e1 / (th * (1 - e1 * e1))
     return lead, e, couple
+
+
+def pieces_of(value, count):
+    found = []
+    for _ in range(count):
+        found.append(np.asarray(value, jnp.bfloat16))
+        value = value - found[-1].astype(np.float64)
+    return found
+
+
+def stack_pieces(value):
+    a1, a2, a3 = pieces_of(value, 3)
+    return np.concatenate([a1, a1, a2, a2, a1, a3], 1)
 
 
 def build_tables(n, members):
@@ -96,29 +109,31 @@
     kh = acc @ (keep @ (-(1 + 2 * a0) * np.eye(M) + b0 * up + b0 * up.T))
     s2x = s2.copy()
     s2x[M - 1, M - 1] = 1
-    mats = np.zeros((15 * M, 128))
     per = min(M, n // (2 * M), 256 // (4 * M))
     wbd = np.kron(np.eye(per), winv)
+    minv = np.zeros((M, M, n))
+    lean = lead / (1 + e * e - 2 * e * np.cos(np.pi * t / M)[:, None])
+    minv[: M - 1, : M - 1] = np.einsum("pm,mk,mq->pqk", st, lean, st)
+    mats = np.zeros((8 * M, 128))
     mats[0:M, : 2 * M] = np.concatenate([sa, stt], 1)
-    mats[M : 2 * M, :M] = s2
-    mats[2 * M : 3 * M, : 2 * M] = hmat
-    mats[3 * M : 4 * M, : 3 * M] = np.concatenate([ka, kt, kh], 1)
-    mats[4 * M : 5 * M, : 4 * M] = winv
-    mats[5 * M : 5 * M + M - 1, :] = np.cos(np.pi * t / M)[:, None]
-    mats[6 * M : 7 * M, :M] = s2x
-    mats[7 * M : 8 * M, :M] = t1.T
-    mats[8 * M : 9 * M, :M] = ka.T * qq
-    mats[9 * M : 10 * M, :M] = kt.T * qq
-    mats[10 * M : 11 * M, :M] = (kh @ t1).T
-    mats[11 * M : 15 * M, :M] = wfwd
-    out = dict(r=r, vec=vec, couple=glob[2], dens=dens, acs=acs, mats=mats)
+    mats[M : 2 * M, :M] = t1.T
+    mats[2 * M : 3 * M, :M] = ka.T * qq
+    mats[3 * M : 4 * M, :M] = kt.T * qq
+    mats[4 * M : 5 * M, :M] = (kh @ t1).T
+    kmats = np.zeros((8 * M, 384), jnp.bfloat16)
+    row = 0
+    for small in (hmat, np.concatenate([ka, kt, kh], 1), s2, s2x, wfwd):
+        stacked = stack_pieces(small)
+        kmats[row : row + small.shape[0], : stacked.shape[1]] = stacked
+        row += small.shape[0]
+    out = dict(r=r, vec=vec, couple=glob[2], dens=dens, acs=acs, mats=mats, minv=minv)
     out = {name: np.asarray(value, np.float32) for name, value in out.items()}
-    for name, value, pieces in (
+    out["kmats"] = kmats
+    for name, value, count in (
         ("q", q, 3), ("s", sp, 2), ("r", r, 3), ("t", turn, 3), ("b", sb, 2), ("w", wbd, 3)
     ):
-        for i in range(pieces):
-            out[f"{name}{i + 1}"] = np.asarray(value, jnp.bfloat16)
-            value = value - out[f"{name}{i + 1}"].astype(np.float64)
+        for i, piece in enumerate(pieces_of(value, count)):
+            out[f"{name}{i + 1}"] = piece
     return out
 
 
@@ -191,17 +206,27 @@
     return jnp.concatenate([jnp.zeros_like(values[:1]), values[:-1]], 0)
 
 
-def edge_solve(al, t0, lead, e, couple, source, mats, special):
+def stacked(b):
+    b1, b2, b3 = (piece.astype(f32) for piece in split3(b))
+    return jnp.concatenate([b1, b2, b1, b2, b3, b1], 0).astype(bf16)
+
+
+def dotk(a, b):
+    return mm(a[:, : 6 * b.shape[0]], stacked(b), 1, 0)
+
+
+def edge_solve(al, t0, couple, source, minv, kmats, special):
     M, n = al.shape
     L = min(n, 128)
     last = rows_of((M, n)) == M - 1
-    both = jnp.concatenate([jnp.where(last, al * couple, al), t0], 0)
-    modes = doth(mats[0:M, : 2 * M], both)
-    cosphi = mats[5 * M : 6 * M, :1]
-    modes = modes * (lead / (1.0 + e * e - 2.0 * e * cosphi))
-    H = jnp.where(last, al, doth(mats[M : 2 * M, :M], modes))
-    Hz = doth(mats[2 * M : 3 * M, : 2 * M], jnp.concatenate([al[:, :L], source], 0))
-    mean = doth(mats[3 * M : 4 * M, : 3 * M], jnp.concatenate([al[:, :L], t0[:, :L], Hz], 0))
+    w = al - jnp.concatenate([t0[1:], t0[:1]], 0)
+    H = jnp.where(last, al, 0.0)
+    tail = couple * al[M - 1 :]
+    for p in range(M - 1):
+        wp = w[p : p + 1] + tail if p == M - 2 else w[p : p + 1]
+        H = H + minv[p] * wp
+    Hz = dotk(kmats[0:M, :], jnp.concatenate([al[:, :L], source], 0))
+    mean = dotk(kmats[M : 2 * M, :], jnp.concatenate([al[:, :L], t0[:, :L], Hz], 0))
     lane = lanes_of((M, L))
     first = jnp.where((lane == 0) & special, Hz, H[:, :L])
     H = first if n == L else jnp.concatenate([first, H[:, L:]], 1)
@@ -213,8 +238,8 @@
     return jnp.broadcast_to(one[None], (members,) + one.shape)
 
 
-def stage_local(r, c, M, need, vec):
-    vec = vec[...]
+def stage_local(r, c, M, need):
+    vec = need("vec")
     n = vec.shape[1]
     L = min(n, 128)
     qs = (need("q1"), need("q2"))
@@ -234,62 +259,61 @@
     return to_peers([alpha, tk[0:1], beta, tl[0:1]], M), u
 
 
-FIRST = ("q1", "q2", "x", "s1", "s2", "y", "r")
-LATER = ("q3", "r1", "r2", "r3", "t1", "t2", "t3", "b1", "b2", "w1", "w2", "w3")
-LATER += ("dens", "couple", "acs", "mats")
-KEPT = ("q1", "q2", "r") + LATER
-
-
-def run_local(members, arrays, vec):
-    n = vec.shape[1]
+WAVES = {None: ("vec", "q1", "x", "q2"), "x": ("s1", "s2", "y", "r")}
+WAVES["y"] = ("q3", "r1", "r2", "r3", "t1", "t2", "t3", "b1", "b2", "w1", "w2", "w3")
+WAVES["y"] += ("dens", "couple", "minv", "acs", "mats", "kmats")
+NAMES = WAVES[None] + WAVES["x"] + WAVES["y"]
+KEPT = ("vec", "q1", "q2", "r") + WAVES["y"]
+
+
+def run_local(members, arrays):
+    n = arrays["vec"].shape[1]
     if DIRECT:
         edges, u = stage_local(
-            lax.axis_index("row"), lax.axis_index("col"), members, arrays.__getitem__, vec
+            lax.axis_index("row"), lax.axis_index("col"), members, arrays.__getitem__
         )
         return edges, u, {name: arrays[name] for name in KEPT}
 
-    names = FIRST + LATER
-
     def kernel(*refs):
-        count = len(names)
-        sources, vec = refs[:count], refs[count]
-        edges, u = refs[count + 1 : count + 3]
-        here = dict(zip(KEPT, refs[count + 3 :]))
-        here.update(zip((k for k in FIRST if k not in KEPT), refs[count + 3 + len(KEPT) :]))
+        count = len(NAMES)
+        edges, u = refs[count : count + 2]
+        here = dict(zip(KEPT, refs[count + 2 :]))
+        here.update(zip((k for k in NAMES if k not in KEPT), refs[count + 2 + len(KEPT) :]))
         sem = refs[-1]
         copies = {
             name: pltpu.make_async_copy(source, here[name], sem.at[i])
-            for i, (name, source) in enumerate(zip(names, sources))
+            for i, (name, source) in enumerate(zip(NAMES, refs))
         }
-        for name in FIRST:
-            copies[name].start()
+
+        def release(wave):
+            for name in WAVES.get(wave, ()):
+                copies[name].start()
 
         def need(name):
             copies[name].wait()
-            if name == "y":
-                for later in LATER:
-                    copies[later].start()
+            release(name)
             return here[name][...]
 
+        release(None)
         edges[...], u[...] = stage_local(
-            lax.axis_index("row"), lax.axis_index("col"), members, need, vec
+            lax.axis_index("row"), lax.axis_index("col"), members, need
         )
-        for name in LATER:
+        for name in WAVES["y"]:
             copies[name].wait()
 
     far, vmem, near = pl.BlockSpec(memory_space=pltpu.HBM), pl.BlockSpec(memory_space=pltpu.VMEM), pltpu.VMEM
-    shape = {name: near(arrays[name].shape, arrays[name].dtype) for name in names}
+    shape = {name: near(arrays[name].shape, arrays[name].dtype) for name in NAMES}
     edges, u, *tables = pl.pallas_call(
         kernel,
         out_shape=[jax.ShapeDtypeStruct((members, 4, n), f32), near((n, n), f32)]
         + [shape[name] for name in KEPT],
-        in_specs=[far] * len(names) + [vmem],
+        in_specs=[far] * len(NAMES),
         out_specs=[vmem] * (2 + len(KEPT)),
-        scratch_shapes=[shape[name] for name in FIRST if name not in KEPT]
-        + [pltpu.SemaphoreType.DMA((len(names),))],
+        scratch_shapes=[shape[name] for name in NAMES if name not in KEPT]
+        + [pltpu.SemaphoreType.DMA((len(NAMES),))],
         compiler_params=pltpu.CompilerParams(vmem_limit_bytes=VMEM_LIMIT),
         name="stage_local",
-    )(*(pltpu.with_memory_space_constraint(arrays[name], pltpu.HBM) for name in names), vec)
+    )(*(pltpu.with_memory_space_constraint(arrays[name], pltpu.HBM) for name in NAMES))
     return edges, u, dict(zip(KEPT, tables))
 
 
@@ -298,20 +322,20 @@
 
 
 def stage_strip(
-    r, c, M, ag, q1, q2, q3, r1, r2, r3, t1, t2, t3, b1, b2, w1, w2, w3, dens, gcouple, vec, acs, mats
+    r, c, M, ag, vec, q1, q2, q3, r1, r2, r3, t1, t2, t3, b1, b2, w1, w2, w3,
+    dens, gcouple, minv, acs, mats, kmats,
 ):
     al, t0, be, ta0 = (ag[:, a, :] for a in range(4))
     vec, mats = vec[...], mats[...]
     n = al.shape[1]
     half = n // 2
-    v0, v1, lead, e, couple = (vec[a : a + 1] for a in range(5))
+    v0, v1, couple = vec[0:1], vec[1:2], vec[4:5]
     L = min(n, 128)
     qq = 1.0 / math.sqrt(n)
     zero = jnp.zeros((M, L), f32)
-    sa, stt, s2 = mats[:M, :M], mats[:M, M : 2 * M], mats[M : 2 * M, :M]
-    cosphi = mats[5 * M : 6 * M, :1]
-
-    H, mean = edge_solve(al, t0, lead, e, couple, zero, mats, True)
+    sa, stt = mats[:M, :M], mats[:M, M : 2 * M]
+
+    H, mean = edge_solve(al, t0, couple, zero, minv, kmats, True)
     rs = (r1[...], r2[...])
     Z = dot6(jnp.concatenate([H * v0, H * v1], 0), rs + (r3[...],))
     add0 = v0 * below(Z[:M]) - v1 * Z[:M]
@@ -322,12 +346,11 @@
 
     qs = (q1[...], q2[...])
     y = dot6(jnp.concatenate([tau1, tau0], 0), qs + (q3[...],))
-    wf = mats[11 * M : 15 * M, :M]
     ca, sna = acs[0 : 2 * M, :], acs[2 * M : 4 * M, :]
+    g = dotk(kmats[4 * M : 8 * M, :], jnp.concatenate([y[:M], y[M:]], 1))
     turned = []
     for side in range(2):
-        g = doth(wf, y[side * M : (side + 1) * M])
-        C, S = g[: 2 * M], g[2 * M :]
+        C, S = (g[k * 2 * M : (k + 1) * 2 * M, side * n : (side + 1) * n] for k in range(2))
         turned.append(jnp.concatenate([C * ca - S * sna, -(C * sna + S * ca)], 1))
     T = dot6(jnp.concatenate(turned, 0), (t1[...], t2[...], t3[...]))
     shape = (2 * M, half)
@@ -341,9 +364,9 @@
     alz = jnp.where(own, T1[:1, :1], 0.0)
     t0z = jnp.where(own, T0[:1, :1], 0.0)
     src = jnp.where(own, al[M - 1 :, :1] * (1.0 / math.sqrt(M)), 0.0)
-    Hz = doth(mats[2 * M : 3 * M, : 2 * M], jnp.concatenate([alz, src], 0))
-    lift = doth(mats[3 * M : 4 * M, : 3 * M], jnp.concatenate([alz, t0z, Hz], 0))
-    g0 = jnp.where(rows_of((M, L)) == M - 1, Hz, doth(s2, Hz))
+    Hz = dotk(kmats[0:M, :], jnp.concatenate([alz, src], 0))
+    lift = dotk(kmats[M : 2 * M, :], jnp.concatenate([alz, t0z, Hz], 0))
+    g0 = jnp.where(rows_of((M, L)) == M - 1, Hz, dotk(kmats[2 * M : 3 * M, :], Hz))
     up, down = lane_pick(sa, r), lane_pick(stt, r)
     T1c = jnp.where(r == M - 1, T1 * gcouple[...], T1)
     modes = []
@@ -366,18 +389,13 @@
     hx = doths(jnp.concatenate(lines, 0), qs)
     Y0, Y1 = dot3(hx * v0, rs), dot3(hx * v1, rs)
 
-    D = lead / (1.0 + e * e - 2.0 * e * cosphi)
-    inner = rows_of((M, n)) < M - 1
     first = lanes_of((1, n)) == 0
     cols = []
-    for cc in (c, c - 1):
-        KD = lane_pick(s2, cc) * D
-        k1 = jnp.where(inner, doth(sa, KD, 0, 0), 0.0)
-        k2 = doth(stt, KD, 0, 0)
-        ksrc = lane_pick(mats[7 * M : 8 * M, :M], cc) * (-1.0 / qq)
-        cols.append((k1, k2, ksrc))
-    ka, kt = lane_pick(mats[8 * M : 9 * M, :M], c), lane_pick(mats[9 * M : 10 * M, :M], c)
-    kth = lane_pick(mats[10 * M : 11 * M, :M], c)
+    for k1, cc in ((minv[c], c), (minv[jnp.maximum(c - 1, 0)], c - 1)):
+        k1 = jnp.where(cc < 0, 0.0, k1)
+        cols.append((k1, -below(k1), lane_pick(mats[M : 2 * M, :M], cc) * (-1.0 / qq)))
+    ka, kt = lane_pick(mats[2 * M : 3 * M, :M], c), lane_pick(mats[3 * M : 4 * M, :M], c)
+    kth = lane_pick(mats[4 * M : 5 * M, :M], c)
     here, side_c, side_b, level = [], [], [], []
     for m in range(M):
         rows = slice(M * m, M * (m + 1))
@@ -390,8 +408,9 @@
         level.append(
             jnp.sum(kth * hm[:, :L] - ka * y1[:, :L] - kt * y0[:, :L], 0, keepdims=True)
         )
-    s2x = mats[6 * M : 7 * M, :M]
-    mixed = [doth(s2x, jnp.concatenate(v, 0)) for v in (here, side_c, side_b, level)]
+    rows = [jnp.concatenate(v, 0) for v in (here, side_c, side_b, level)]
+    mixed = dotk(kmats[3 * M : 4 * M, :], jnp.concatenate(rows, 1))
+    mixed = [mixed[:, a * n : (a + 1) * n] for a in range(4)]
     right, fc, fb, lv = mixed
     lv = (lv - below(lv) + lift * (1.0 / math.sqrt(M)))[:, :1]
     share = [
@@ -416,13 +435,49 @@
     before = before + keep[1:2]
     level = level[:, :1] + keep[2:3, :1]
     pad = jnp.zeros((4, n), f32)
-    lhs = jnp.concatenate([q1, -q0, here, -before, pad], 0)
-    rhs = jnp.concatenate([right, left, q1, q0, pad], 0)
-    G = doth(lhs, rhs, 0, 0)
+    a1, a2, a3 = (
+        piece.astype(f32) for piece in split3(jnp.concatenate([q1, -q0, here, -before, pad], 0))
+    )
+    lhs = jnp.concatenate([a1, a1, a2, a2, a1, a3], 0).astype(bf16)
+    G = mm(lhs, stacked(jnp.concatenate([right, left, q1, q0, pad], 0)), 0, 0)
     un = u[...] - rr[...] * G
     un = jnp.where((rows_of(un.shape) == 0) & (lanes_of(un.shape) == 0), level, un)
     qs = (qh[...], ql[...])
-    return (dot3(qs, dot3(un, qs), 0, 0),)
+    half = split(dot3(un, qs))
+    step = n // 4
+    for part in range(4):
+        cols = slice(part * step, (part + 1) * step)
+        yield dot3((qs[0][:, cols], qs[1][:, cols]), half, 0, 0)
+
+
+def run_field(members, *args):
+    n = args[-1].shape[1]
+    place = lambda: (lax.axis_index("row"), lax.axis_index("col"))
+    if DIRECT:
+        return jnp.concatenate(list(stage_field(*place(), members, *args)), 0)
+
+    def kernel(*refs):
+        field, rows, sem = refs[len(args) :]
+        copies = []
+        for part, value in enumerate(stage_field(*place(), members, *refs[: len(args)])):
+            step = value.shape[0]
+            span = slice(part * step, (part + 1) * step)
+            rows[span, :] = value
+            copies.append(pltpu.make_async_copy(rows.at[span], field.at[span], sem.at[part]))
+            copies[-1].start()
+        for copy in copies:
+            copy.wait()
+
+    vmem = pl.BlockSpec(memory_space=pltpu.VMEM)
+    return pl.pallas_call(
+        kernel,
+        out_shape=jax.ShapeDtypeStruct((n, n), f32),
+        in_specs=[vmem] * len(args),
+        out_specs=pl.BlockSpec(memory_space=pltpu.HBM),
+        scratch_shapes=[pltpu.VMEM((n, n), f32), pltpu.SemaphoreType.DMA((4,))],
+        compiler_params=pltpu.CompilerParams(vmem_limit_bytes=VMEM_LIMIT),
+        name="stage_field",
+    )(*args)
 
 
 def packed(rows):
@@ -467,20 +522,16 @@
         n = grad_x.shape[0]
         t = {k: jnp.asarray(v) for k, v in build_tables(n, members).items()}
         sent, near = jax.ShapeDtypeStruct, pltpu.VMEM
-        edges, u, kept = run_local(members, {**t, "x": grad_x, "y": grad_y}, t["vec"])
+        edges, u, kept = run_local(members, {**t, "x": grad_x, "y": grad_y})
         strip = exchange(edges, "col")
-        names = LATER[:-2] + ("vec",) + LATER[-2:]
-        kept["vec"] = t["vec"]
         share, keep = run_stage(
             stage_strip, members, [sent((members, 4, n + 128), f32), near((8, n), f32)],
-            strip, kept["q1"], kept["q2"], *(kept[name] for name in names),
+            strip, kept["vec"], kept["q1"], kept["q2"], *(kept[name] for name in WAVES["y"]),
         )
         share = exchange(share, "row")
-        (field,) = run_stage(
-            stage_field, members, [sent((n, n), f32)],
-            share, keep, u, kept["q1"], kept["q2"], kept["r"], t["vec"],
+        return run_field(
+            members, share, keep, u, kept["q1"], kept["q2"], kept["r"], kept["vec"]
         )
-        return field
 
     return body
 

time: 51.6 us -> 49.8 us (0.965)
  Pallas kernels: 16.9 us -> 15.8 us
  local copies, waits for them, and re-layouts: 0.72 us -> 0 us
    pallas_call x2 -> x1, Pallas kernels: 10 us -> 5.62 us  [run_stage(): pl.pallas_call(kernel, out_shape=outs, in_specs=[vmem] * len(args), out_s...]
    pallas_call x0 -> x1, Pallas kernels: none -> 2.85 us  [run_field(): pl.pallas_call(kernel, out_shape=jax.ShapeDtypeStruct((n, n), f32), in_sp...]
    unnamed x2 -> x0, local copies, waits for them, and re-layouts: 0.72 us -> none
where the time goes in v5:
time: 49.8 us; the launch traced here: 49.5 us
  blocking collectives  33.7 us (68%)
  Pallas kernels  15.8 us (32%)
    all_to_all x2, blocking collectives, exchange(): return lax.all_to_all(values, axis, split_axis=0, concat_axis=0, tiled=True)  33.7 us
    pallas_call x1, Pallas kernels, run_local(): pl.pallas_call(kernel, out_shape=[jax.ShapeDtypeStruct((members, 4, n), f...  7.3 us
    pallas_call x1, Pallas kernels, run_stage(): pl.pallas_call(kernel, out_shape=outs, in_specs=[vmem] * len(args), out_s...  5.62 us
    pallas_call x1, Pallas kernels, run_field(): pl.pallas_call(kernel, out_shape=jax.ShapeDtypeStruct((n, n), f32), in_sp...  2.85 us

profile of v5, /device:TPU:1, one launch (start us, length us, event | category | flops | bytes accessed | tf_op | source)
XLA Modules:
  0.0 49.5 jit_solution(10198916585144682616)
XLA Ops:
  0.0 7.3 %stage_local.1 = (f32[16,4,512]{2,1,0:T(4,128)S(1)}, f32[512,512]{1,0:T(8,128)S(1)}, f32[8,512]{1,0:T(8,128)S(1)}, bf16[512,512]{1,0:T(8,128)(2,1)S(1)}, bf16[51...) custom-call(f32[8,512]{1,0:T(8,128)} %constant.49.clone.refs_0_, ...), custom_call_target="tpu_custom_call" | custom-call | tf_op jit(solution)/shard_map/stage_local/pallas_call | solution.py:306
  7.3 17.4 %all_to_all.10.refs_0_ = f32[16,4,512]{2,1,0:T(4,128)S(1)} all-to-all(f32[16,4,512]{2,1,0:T(4,128)S(1)} %get-tuple-element.31), channel_id=1, replica_groups=mesh['row'=16,'col'=16] {'col'}, dimensions={0} | all-to-all | bytes 262144 | tf_op jit(solution)/shard_map/all_to_all | solution.py:517
  24.7 5.6 %stage_strip.1 = (f32[16,4,640]{2,1,0:T(4,128)S(1)}, f32[8,512]{1,0:T(8,128)S(1)}) custom-call(f32[16,4,512]{2,1,0:T(4,128)S(1)} %all_to_all.10.refs_0_, f32[8,512]{1,0:T(8,128)S(1)} %get-tuple-element.32.refs_1_.refs_6_, bf16[512,512]{1,0:T(8,128)(2,1)S(1)} %get-tuple-element.33.refs_2_.refs_3_, bf16[512,512]{1,0:T(8,128)(2,1)S(1)} %get-tuple-element.34.refs_3_.refs_4_, ...), custom_call_target="tpu_custom_call" | custom-call | tf_op jit(solution)/shard_map/stage_strip/pallas_call | solution.py:506
  30.3 16.4 %all_to_all.11.refs_0_ = f32[16,4,640]{2,1,0:T(4,128)S(1)} all-to-all(f32[16,4,640]{2,1,0:T(4,128)S(1)} %get-tuple-element.53), channel_id=1, replica_groups=mesh['row'=16,'col'=16] {'row'}, dimensions={0} | all-to-all | bytes 327680 | tf_op jit(solution)/shard_map/all_to_all | solution.py:517
  46.7 2.8 %stage_field.1 = f32[512,512]{1,0:T(8,128)} custom-call(f32[16,4,640]{2,1,0:T(4,128)S(1)} %all_to_all.11.refs_0_, f32[8,512]{1,0:T(8,128)S(1)} %get-tuple-element.54.refs_1_, f32[512,512]{1,0:T(8,128)S(1)} %get-tuple-element.55.refs_2_, bf16[512,512]{1,0:T(8,128)(2,1)S(1)} %get-tuple-element.33.refs_2_.refs_3_, ...), custom_call_target="tpu_custom_call" | custom-call | tf_op jit(solution)/shard_map/stage_field/pallas_call | solution.py:472

commit v6 on v5

--- a/solution.py
+++ b/solution.py
@@ -126,14 +126,20 @@
         stacked = stack_pieces(small)
         kmats[row : row + small.shape[0], : stacked.shape[1]] = stacked
         row += small.shape[0]
-    out = dict(r=r, vec=vec, couple=glob[2], dens=dens, acs=acs, mats=mats, minv=minv)
+    q1, q2, q3 = pieces_of(q, 3)
+    s1, s2 = pieces_of(sp, 2)
+    v1, v2 = pieces_of(vec, 2)
+    out = dict(
+        vec=vec, r=r, col=np.repeat(q0[:, None], min(n, 128), 1), mats=mats,
+        thin=np.concatenate([dens, glob[2]], 0),
+        long=np.concatenate([minv.reshape(-1, n), acs], 0),
+    )
     out = {name: np.asarray(value, np.float32) for name, value in out.items()}
-    out["kmats"] = kmats
-    for name, value, count in (
-        ("q", q, 3), ("s", sp, 2), ("r", r, 3), ("t", turn, 3), ("b", sb, 2), ("w", wbd, 3)
-    ):
-        for i, piece in enumerate(pieces_of(value, count)):
-            out[f"{name}{i + 1}"] = piece
+    out.update(
+        q1=q1, q2=q2, s1=s1, s2=s2, v=np.concatenate([v1, v2], 0), kmats=kmats,
+        w=np.concatenate(pieces_of(wbd, 3), 0), turn=np.concatenate(pieces_of(turn, 3), 0),
+        wide=np.concatenate([q3] + pieces_of(r, 3) + pieces_of(sb, 2), 0),
+    )
     return out
 
 
@@ -224,7 +230,7 @@
     tail = couple * al[M - 1 :]
     for p in range(M - 1):
         wp = w[p : p + 1] + tail if p == M - 2 else w[p : p + 1]
-        H = H + minv[p] * wp
+        H = H + minv[M * p : M * (p + 1), :] * wp
     Hz = dotk(kmats[0:M, :], jnp.concatenate([al[:, :L], source], 0))
     mean = dotk(kmats[M : 2 * M, :], jnp.concatenate([al[:, :L], t0[:, :L], Hz], 0))
     lane = lanes_of((M, L))
@@ -239,35 +245,56 @@
 
 
 def stage_local(r, c, M, need):
-    vec = need("vec")
-    n = vec.shape[1]
+    q1 = need("q1")
+    n = q1.shape[0]
+    half = n // 2
     L = min(n, 128)
-    qs = (need("q1"), need("q2"))
-    m1 = dot3(need("x"), qs, 1, 1)
+    pieces, sums = [], []
+    for name in ("x0", "x1"):
+        pieces.append(split(need(name)))
+        sums.append(mm(pieces[-1][0], q1, 1, 1))
+    q2 = need("q2")
+    m1 = jnp.concatenate(
+        [p + (mm(xh, q2, 1, 1) + mm(xl, q1, 1, 1)) for p, (xh, xl) in zip(sums, pieces)], 0
+    )
+    qs = (q1, q2)
+    n2 = dot3(qs, need("y"))
     ss = (need("s1"), need("s2"))
-    gys = split(need("y"))
-    m2 = dot3(gys, ss, 1, 1)
-    slab = (gys[0][:, n - L :], gys[1][:, n - L :])
-    gyl = dot3(slab, qs, 0, 1)[L - 1 :]
-    f = dot3(ss, m1) + dot3(qs, m2)
+    f = dot3(ss, m1) + dot3(n2, ss, 1, 1)
+    gyl = n2[:, n - L :].T[L - 1 :]
     u = -f * need("r")
-    us = split(u)
-    tk = dot3(vec, us, 1, 1)
-    tl = dot3(vec, us, 1, 0)
+    uh, ul = split(u)
+    v = need("v")
+    p = mm(v, uh, 1, 1)
+    tk = p[:8] + (p[8:] + mm(v, ul, 1, 1)[:8])
+    col = need("col")
+    groups = []
+    for rows in (slice(0, half), slice(half, n)):
+        groups.append(
+            jnp.concatenate(
+                [
+                    jnp.sum(u[rows, a : a + L] * col[rows], 0, keepdims=True)
+                    for a in range(0, n, L)
+                ],
+                1,
+            )
+        )
+    low, high = groups[0] + groups[1], groups[0] - groups[1]
     alpha = gyl + jnp.where(c < M - 1, tk[1:2], 0.0)
-    beta = m1[n - 1 :] + jnp.where(r < M - 1, tl[1:2], 0.0)
-    return to_peers([alpha, tk[0:1], beta, tl[0:1]], M), u
-
-
-WAVES = {None: ("vec", "q1", "x", "q2"), "x": ("s1", "s2", "y", "r")}
-WAVES["y"] = ("q3", "r1", "r2", "r3", "t1", "t2", "t3", "b1", "b2", "w1", "w2", "w3")
-WAVES["y"] += ("dens", "couple", "minv", "acs", "mats", "kmats")
-NAMES = WAVES[None] + WAVES["x"] + WAVES["y"]
-KEPT = ("vec", "q1", "q2", "r") + WAVES["y"]
+    beta = m1[n - 1 :] + jnp.where(r < M - 1, high, 0.0)
+    return to_peers([alpha, tk[0:1], beta, low], M), u
+
+
+WAVES = {None: ("q1", "x0", "x1", "q2"), "x0": ("y", "s1", "s2"), "y": ("r", "v", "col")}
+WAVES["s2"] = ("vec", "wide", "turn", "w", "thin", "long", "mats", "kmats")
+NAMES = WAVES[None] + WAVES["x0"] + WAVES["y"] + WAVES["s2"]
+KEPT = ("q1", "q2", "r") + WAVES["s2"]
 
 
 def run_local(members, arrays):
-    n = arrays["vec"].shape[1]
+    n = arrays["q1"].shape[1]
+    arrays["x0"], arrays["x1"] = arrays["x"][: n // 2], arrays["x"][n // 2 :]
+    shapes = {name: (arrays[name].shape, arrays[name].dtype) for name in NAMES}
     if DIRECT:
         edges, u = stage_local(
             lax.axis_index("row"), lax.axis_index("col"), members, arrays.__getitem__
@@ -280,8 +307,12 @@
         here = dict(zip(KEPT, refs[count + 2 :]))
         here.update(zip((k for k in NAMES if k not in KEPT), refs[count + 2 + len(KEPT) :]))
         sem = refs[-1]
+        def part_of(name, source):
+            pick_half = {"x0": pl.ds(0, n // 2), "x1": pl.ds(n // 2, n // 2)}
+            return source.at[pick_half[name]] if name in pick_half else source
+
         copies = {
-            name: pltpu.make_async_copy(source, here[name], sem.at[i])
+            name: pltpu.make_async_copy(part_of(name, source), here[name], sem.at[i])
             for i, (name, source) in enumerate(zip(NAMES, refs))
         }
 
@@ -298,11 +329,12 @@
         edges[...], u[...] = stage_local(
             lax.axis_index("row"), lax.axis_index("col"), members, need
         )
-        for name in WAVES["y"]:
+        for name in WAVES["s2"]:
             copies[name].wait()
 
+    operands = [name if name not in ("x0", "x1") else "x" for name in NAMES]
     far, vmem, near = pl.BlockSpec(memory_space=pltpu.HBM), pl.BlockSpec(memory_space=pltpu.VMEM), pltpu.VMEM
-    shape = {name: near(arrays[name].shape, arrays[name].dtype) for name in NAMES}
+    shape = {name: near(*shapes[name]) for name in NAMES}
     edges, u, *tables = pl.pallas_call(
         kernel,
         out_shape=[jax.ShapeDtypeStruct((members, 4, n), f32), near((n, n), f32)]
@@ -313,7 +345,7 @@
         + [pltpu.SemaphoreType.DMA((len(NAMES),))],
         compiler_params=pltpu.CompilerParams(vmem_limit_bytes=VMEM_LIMIT),
         name="stage_local",
-    )(*(pltpu.with_memory_space_constraint(arrays[name], pltpu.HBM) for name in NAMES))
+    )(*(pltpu.with_memory_space_constraint(arrays[name], pltpu.HBM) for name in operands))
     return edges, u, dict(zip(KEPT, tables))
 
 
@@ -321,23 +353,23 @@
     return jnp.sum(jnp.where(lanes_of(values.shape) == index, values, 0.0), 1, keepdims=True)
 
 
-def stage_strip(
-    r, c, M, ag, vec, q1, q2, q3, r1, r2, r3, t1, t2, t3, b1, b2, w1, w2, w3,
-    dens, gcouple, minv, acs, mats, kmats,
-):
+def stage_strip(r, c, M, ag, q1, q2, vec, wide, turn, w, thin, long, mats, kmats):
+    n = q1.shape[0]
+    half = n // 2
+    r1, r2, r3 = (wide[a * n : (a + 1) * n, :] for a in range(1, 4))
+    b1, b2 = wide[4 * n : 4 * n + half, :], wide[4 * n + half : 5 * n, :]
+    acs = long[M * M : M * M + 4 * M, :]
     al, t0, be, ta0 = (ag[:, a, :] for a in range(4))
     vec, mats = vec[...], mats[...]
-    n = al.shape[1]
-    half = n // 2
     v0, v1, couple = vec[0:1], vec[1:2], vec[4:5]
     L = min(n, 128)
     qq = 1.0 / math.sqrt(n)
     zero = jnp.zeros((M, L), f32)
     sa, stt = mats[:M, :M], mats[:M, M : 2 * M]
 
-    H, mean = edge_solve(al, t0, couple, zero, minv, kmats, True)
-    rs = (r1[...], r2[...])
-    Z = dot6(jnp.concatenate([H * v0, H * v1], 0), rs + (r3[...],))
+    H, mean = edge_solve(al, t0, couple, zero, long, kmats, True)
+    rs = (r1, r2)
+    Z = dot6(jnp.concatenate([H * v0, H * v1], 0), rs + (r3,))
     add0 = v0 * below(Z[:M]) - v1 * Z[:M]
     add1 = v0 * below(Z[M:]) - v1 * Z[M:]
     flat = jnp.where(lanes_of((M, n)) == 0, mean * qq, 0.0)
@@ -345,14 +377,14 @@
     tau1 = be + jnp.where(r < M - 1, add1 + flat, 0.0)
 
     qs = (q1[...], q2[...])
-    y = dot6(jnp.concatenate([tau1, tau0], 0), qs + (q3[...],))
+    y = dot6(jnp.concatenate([tau1, tau0], 0), qs + (wide[:n, :],))
     ca, sna = acs[0 : 2 * M, :], acs[2 * M : 4 * M, :]
     g = dotk(kmats[4 * M : 8 * M, :], jnp.concatenate([y[:M], y[M:]], 1))
     turned = []
     for side in range(2):
         C, S = (g[k * 2 * M : (k + 1) * 2 * M, side * n : (side + 1) * n] for k in range(2))
         turned.append(jnp.concatenate([C * ca - S * sna, -(C * sna + S * ca)], 1))
-    T = dot6(jnp.concatenate(turned, 0), (t1[...], t2[...], t3[...]))
+    T = dot6(jnp.concatenate(turned, 0), tuple(turn[2 * n * a : 2 * n * (a + 1), :] for a in range(3)))
     shape = (2 * M, half)
     zeroth = lanes_of(shape) == 0
     origin = (rows_of(shape) == 0) & zeroth
@@ -368,17 +400,18 @@
     lift = dotk(kmats[M : 2 * M, :], jnp.concatenate([alz, t0z, Hz], 0))
     g0 = jnp.where(rows_of((M, L)) == M - 1, Hz, dotk(kmats[2 * M : 3 * M, :], Hz))
     up, down = lane_pick(sa, r), lane_pick(stt, r)
-    T1c = jnp.where(r == M - 1, T1 * gcouple[...], T1)
+    T1c = jnp.where(r == M - 1, T1 * thin[2 * M * (M - 1) :, :], T1)
     modes = []
     for m in range(M - 1):
-        value = (up[m : m + 1] * T1c + down[m : m + 1] * T0) * dens[2 * M * m : 2 * M * (m + 1), :]
+        value = (up[m : m + 1] * T1c + down[m : m + 1] * T0) * thin[2 * M * m : 2 * M * (m + 1), :]
         modes.append(jnp.where(origin, g0[m : m + 1, :1] * root, value))
     modes.append(jnp.where(r == M - 1, T1, 0.0) * scale)
     modes = split(jnp.concatenate(modes, 0))
     XC = dot3(modes, (qs[0][:half], qs[1][:half]))
-    XS = dot3(modes, (b1[...], b2[...]))
-    ws = (w1[...], w2[...], w3[...])
-    group = w1.shape[1] // (4 * M)
+    XS = dot3(modes, (b1, b2))
+    third = w.shape[0] // 3
+    ws = tuple(w[third * a : third * (a + 1), :] for a in range(3))
+    group = w.shape[1] // (4 * M)
     lines = []
     for first in range(0, M, group):
         rots = []
@@ -391,7 +424,8 @@
 
     first = lanes_of((1, n)) == 0
     cols = []
-    for k1, cc in ((minv[c], c), (minv[jnp.maximum(c - 1, 0)], c - 1)):
+    for cc in (c, c - 1):
+        k1 = long[pl.ds(pl.multiple_of(jnp.maximum(cc, 0) * M, M), M), :]
         k1 = jnp.where(cc < 0, 0.0, k1)
         cols.append((k1, -below(k1), lane_pick(mats[M : 2 * M, :M], cc) * (-1.0 / qq)))
     ka, kt = lane_pick(mats[2 * M : 3 * M, :M], c), lane_pick(mats[3 * M : 4 * M, :M], c)
@@ -526,7 +560,7 @@
         strip = exchange(edges, "col")
         share, keep = run_stage(
             stage_strip, members, [sent((members, 4, n + 128), f32), near((8, n), f32)],
-            strip, kept["vec"], kept["q1"], kept["q2"], *(kept[name] for name in WAVES["y"]),
+            strip, kept["q1"], kept["q2"], *(kept[name] for name in WAVES["s2"]),
         )
         share = exchange(share, "row")
         return run_field(

time: 49.8 us -> 48.8 us (0.980)
  Pallas kernels: 15.8 us -> 14.8 us
    pallas_call x1, Pallas kernels: 7.3 us -> 6.35 us  [run_local(): pl.pallas_call(kernel, out_shape=[jax.ShapeDtypeStruct((members, 4, n), f...]
where the time goes in v6:
time: 48.8 us; the launch traced here: 48.6 us
  blocking collectives  33.7 us (69%)
  Pallas kernels  14.8 us (30%)
    all_to_all x2, blocking collectives, exchange(): return lax.all_to_all(values, axis, split_axis=0, concat_axis=0, tiled=True)  33.7 us
    pallas_call x1, Pallas kernels, run_local(): pl.pallas_call(kernel, out_shape=[jax.ShapeDtypeStruct((members, 4, n), f...  6.35 us
    pallas_call x1, Pallas kernels, run_stage(): pl.pallas_call(kernel, out_shape=outs, in_specs=[vmem] * len(args), out_s...  5.62 us
    pallas_call x1, Pallas kernels, run_field(): pl.pallas_call(kernel, out_shape=jax.ShapeDtypeStruct((n, n), f32), in_sp...  2.85 us

profile of v6, /device:TPU:1, one launch (start us, length us, event | category | flops | bytes accessed | tf_op | source)
XLA Modules:
  0.0 48.6 jit_solution(9041050047096771269)
XLA Ops:
  0.0 6.3 %stage_local.1 = (f32[16,4,512]{2,1,0:T(4,128)S(1)}, f32[512,512]{1,0:T(8,128)S(1)}, bf16[512,512]{1,0:T(8,128)(2,1)S(1)}, bf16[512,512]{1,0:T(8,128)(2,1)S(1)},...) custom-call(bf16[512,512]{1,0:T(8,128)(2,1)} %constant.36.clone.refs, ...), custom_call_target="tpu_custom_call" | custom-call | tf_op jit(solution)/shard_map/stage_local/pallas_call | solution.py:338
  6.4 17.4 %all_to_all.10.refs_0_ = f32[16,4,512]{2,1,0:T(4,128)S(1)} all-to-all(f32[16,4,512]{2,1,0:T(4,128)S(1)} %get-tuple-element.20), channel_id=1, replica_groups=mesh['row'=16,'col'=16] {'col'}, dimensions={0} | all-to-all | bytes 262144 | tf_op jit(solution)/shard_map/all_to_all | solution.py:551
  23.8 5.6 %stage_strip.1 = (f32[16,4,640]{2,1,0:T(4,128)S(1)}, f32[8,512]{1,0:T(8,128)S(1)}) custom-call(f32[16,4,512]{2,1,0:T(4,128)S(1)} %all_to_all.10.refs_0_, bf16[512,512]{1,0:T(8,128)(2,1)S(1)} %get-tuple-element.21.refs_1_.refs_3_, bf16[512,512]{1,0:T(8,128)(2,1)S(1)} %get-tuple-element.22.refs_2_.refs_4_, f32[8,512]{1,0:T(8,128)S(1)} %get-tuple-element.23.refs_3_.refs_6_, ...), custom_call_target="tpu_custom_call" | custom-call | tf_op jit(solution)/shard_map/stage_strip/pallas_call | solution.py:540
  29.4 16.3 %all_to_all.11.refs_0_ = f32[16,4,640]{2,1,0:T(4,128)S(1)} all-to-all(f32[16,4,640]{2,1,0:T(4,128)S(1)} %get-tuple-element.31), channel_id=1, replica_groups=mesh['row'=16,'col'=16] {'row'}, dimensions={0} | all-to-all | bytes 327680 | tf_op jit(solution)/shard_map/all_to_all | solution.py:551
  45.7 2.8 %stage_field.1 = f32[512,512]{1,0:T(8,128)} custom-call(f32[16,4,640]{2,1,0:T(4,128)S(1)} %all_to_all.11.refs_0_, f32[8,512]{1,0:T(8,128)S(1)} %get-tuple-element.32.refs_1_, f32[512,512]{1,0:T(8,128)S(1)} %get-tuple-element.33.refs_2_, bf16[512,512]{1,0:T(8,128)(2,1)S(1)} %get-tuple-element.21.refs_1_.refs_3_, ...), custom_call_target="tpu_custom_call" | custom-call | tf_op jit(solution)/shard_map/stage_field/pallas_call | solution.py:506

commit v7 on v6

--- a/solution.py
+++ b/solution.py
@@ -152,10 +152,16 @@
     return lax.dot_general(a, b, (((ca,), (cb,)), ((), ())), preferred_element_type=f32)
 
 
+def dot3s(a, b, ca=1, cb=0):
+    ah, al = a if isinstance(a, tuple) else split(a)
+    bh, bl = b if isinstance(b, tuple) else split(b)
+    return mm(ah, bh, ca, cb) + (mm(ah, bl, ca, cb) + mm(al, bh, ca, cb))
+
+
 def dot3(a, b, ca=1, cb=0):
     ah, al = a if isinstance(a, tuple) else split(a)
     bh, bl = b if isinstance(b, tuple) else split(b)
-    return mm(ah, bh, ca, cb) + (mm(ah, bl, ca, cb) + mm(al, bh, ca, cb))
+    return mm(jnp.concatenate([ah, ah, al], ca), jnp.concatenate([bh, bl, bh], cb), ca, cb)
 
 
 def split3(a):
@@ -244,30 +250,25 @@
     return jnp.broadcast_to(one[None], (members,) + one.shape)
 
 
-def stage_local(r, c, M, need):
-    q1 = need("q1")
-    n = q1.shape[0]
+def stage_local(r, c, M, wait, get):
+    wait("q1", "x0", "x1", "q2")
+    m1 = dot3(
+        jnp.concatenate([get("x0"), get("x1")], 0), (get("q1"), get("q2")), 1, 1
+    )
+    wait("y", "s1", "s2", "r", "v", "col")
+    n = m1.shape[0]
     half = n // 2
     L = min(n, 128)
-    pieces, sums = [], []
-    for name in ("x0", "x1"):
-        pieces.append(split(need(name)))
-        sums.append(mm(pieces[-1][0], q1, 1, 1))
-    q2 = need("q2")
-    m1 = jnp.concatenate(
-        [p + (mm(xh, q2, 1, 1) + mm(xl, q1, 1, 1)) for p, (xh, xl) in zip(sums, pieces)], 0
-    )
-    qs = (q1, q2)
-    n2 = dot3(qs, need("y"))
-    ss = (need("s1"), need("s2"))
+    n2 = dot3((get("q1"), get("q2")), get("y"))
+    ss = (get("s1"), get("s2"))
     f = dot3(ss, m1) + dot3(n2, ss, 1, 1)
     gyl = n2[:, n - L :].T[L - 1 :]
-    u = -f * need("r")
+    u = -f * get("r")
     uh, ul = split(u)
-    v = need("v")
+    v = get("v")
     p = mm(v, uh, 1, 1)
     tk = p[:8] + (p[8:] + mm(v, ul, 1, 1)[:8])
-    col = need("col")
+    col = get("col")
     groups = []
     for rows in (slice(0, half), slice(half, n)):
         groups.append(
@@ -285,9 +286,9 @@
     return to_peers([alpha, tk[0:1], beta, low], M), u
 
 
-WAVES = {None: ("q1", "x0", "x1", "q2"), "x0": ("y", "s1", "s2"), "y": ("r", "v", "col")}
+WAVES = {None: ("q1", "x0", "x1", "q2"), "x0": ("y", "s1", "s2", "r", "v", "col")}
 WAVES["s2"] = ("vec", "wide", "turn", "w", "thin", "long", "mats", "kmats")
-NAMES = WAVES[None] + WAVES["x0"] + WAVES["y"] + WAVES["s2"]
+NAMES = WAVES[None] + WAVES["x0"] + WAVES["s2"]
 KEPT = ("q1", "q2", "r") + WAVES["s2"]
 
 
@@ -297,7 +298,8 @@
     shapes = {name: (arrays[name].shape, arrays[name].dtype) for name in NAMES}
     if DIRECT:
         edges, u = stage_local(
-            lax.axis_index("row"), lax.axis_index("col"), members, arrays.__getitem__
+            lax.axis_index("row"), lax.axis_index("col"), members, lambda *names: None,
+            arrays.__getitem__,
         )
         return edges, u, {name: arrays[name] for name in KEPT}
 
@@ -320,17 +322,19 @@
             for name in WAVES.get(wave, ()):
                 copies[name].start()
 
-        def need(name):
-            copies[name].wait()
-            release(name)
+        def wait(*names):
+            for name in names:
+                copies[name].wait()
+                release(name)
+
+        def get(name):
             return here[name][...]
 
         release(None)
         edges[...], u[...] = stage_local(
-            lax.axis_index("row"), lax.axis_index("col"), members, need
+            lax.axis_index("row"), lax.axis_index("col"), members, wait, get
         )
-        for name in WAVES["s2"]:
-            copies[name].wait()
+        wait(*WAVES["s2"])
 
     operands = [name if name not in ("x0", "x1") else "x" for name in NAMES]
     far, vmem, near = pl.BlockSpec(memory_space=pltpu.HBM), pl.BlockSpec(memory_space=pltpu.VMEM), pltpu.VMEM
@@ -407,8 +411,8 @@
         modes.append(jnp.where(origin, g0[m : m + 1, :1] * root, value))
     modes.append(jnp.where(r == M - 1, T1, 0.0) * scale)
     modes = split(jnp.concatenate(modes, 0))
-    XC = dot3(modes, (qs[0][:half], qs[1][:half]))
-    XS = dot3(modes, (b1, b2))
+    XC = dot3s(modes, (qs[0][:half], qs[1][:half]))
+    XS = dot3s(modes, (b1, b2))
     third = w.shape[0] // 3
     ws = tuple(w[third * a : third * (a + 1), :] for a in range(3))
     group = w.shape[1] // (4 * M)
@@ -420,7 +424,8 @@
             rots += [ca * xc - sna * xs, sna * xc + ca * xs]
         lines.append(dotl(ws, jnp.concatenate(rots, 0)))
     hx = doths(jnp.concatenate(lines, 0), qs)
-    Y0, Y1 = dot3(hx * v0, rs), dot3(hx * v1, rs)
+    Y = dot3(jnp.concatenate([hx * v0, hx * v1], 0), rs)
+    Y0, Y1 = Y[: M * M], Y[M * M :]
 
     first = lanes_of((1, n)) == 0
     cols = []

time: 48.8 us -> 48.7 us (level)
  no operation moved by 1% of the time
where the time goes in v7:
time: 48.7 us; the launch traced here: 48.5 us
  blocking collectives  33.7 us (69%)
  Pallas kernels  14.8 us (30%)
    all_to_all x2, blocking collectives, exchange(): return lax.all_to_all(values, axis, split_axis=0, concat_axis=0, tiled=True)  33.7 us
    pallas_call x1, Pallas kernels, run_local(): pl.pallas_call(kernel, out_shape=[jax.ShapeDtypeStruct((members, 4, n), f...  6.31 us
    pallas_call x1, Pallas kernels, run_stage(): pl.pallas_call(kernel, out_shape=outs, in_specs=[vmem] * len(args), out_s...  5.62 us
    pallas_call x1, Pallas kernels, run_field(): pl.pallas_call(kernel, out_shape=jax.ShapeDtypeStruct((n, n), f32), in_sp...  2.85 us

profile of v7, /device:TPU:1, one launch (start us, length us, event | category | flops | bytes accessed | tf_op | source)
XLA Modules:
  0.0 48.5 jit_solution(16047982061786093016)
XLA Ops:
  0.0 6.3 %stage_local.1 = (f32[16,4,512]{2,1,0:T(4,128)S(1)}, f32[512,512]{1,0:T(8,128)S(1)}, bf16[512,512]{1,0:T(8,128)(2,1)S(1)}, bf16[512,512]{1,0:T(8,128)(2,1)S(1)},...) custom-call(bf16[512,512]{1,0:T(8,128)(2,1)} %constant.36.clone.refs, ...), custom_call_target="tpu_custom_call" | custom-call | tf_op jit(solution)/shard_map/stage_local/pallas_call | solution.py:342
  6.3 17.4 %all_to_all.10.refs_0_ = f32[16,4,512]{2,1,0:T(4,128)S(1)} all-to-all(f32[16,4,512]{2,1,0:T(4,128)S(1)} %get-tuple-element.20), channel_id=1, replica_groups=mesh['row'=16,'col'=16] {'col'}, dimensions={0} | all-to-all | bytes 262144 | tf_op jit(solution)/shard_map/all_to_all | solution.py:556
  23.7 5.6 %stage_strip.1 = (f32[16,4,640]{2,1,0:T(4,128)S(1)}, f32[8,512]{1,0:T(8,128)S(1)}) custom-call(f32[16,4,512]{2,1,0:T(4,128)S(1)} %all_to_all.10.refs_0_, bf16[512,512]{1,0:T(8,128)(2,1)S(1)} %get-tuple-element.21.refs_1_.refs_3_, bf16[512,512]{1,0:T(8,128)(2,1)S(1)} %get-tuple-element.22.refs_2_.refs_4_, f32[8,512]{1,0:T(8,128)S(1)} %get-tuple-element.23.refs_3_.refs_6_, ...), custom_call_target="tpu_custom_call" | custom-call | tf_op jit(solution)/shard_map/stage_strip/pallas_call | solution.py:545
  29.4 16.3 %all_to_all.11.refs_0_ = f32[16,4,640]{2,1,0:T(4,128)S(1)} all-to-all(f32[16,4,640]{2,1,0:T(4,128)S(1)} %get-tuple-element.31), channel_id=1, replica_groups=mesh['row'=16,'col'=16] {'row'}, dimensions={0} | all-to-all | bytes 327680 | tf_op jit(solution)/shard_map/all_to_all | solution.py:556
  45.7 2.8 %stage_field.1 = f32[512,512]{1,0:T(8,128)} custom-call(f32[16,4,640]{2,1,0:T(4,128)S(1)} %all_to_all.11.refs_0_, f32[8,512]{1,0:T(8,128)S(1)} %get-tuple-element.32.refs_1_, f32[512,512]{1,0:T(8,128)S(1)} %get-tuple-element.33.refs_2_, bf16[512,512]{1,0:T(8,128)(2,1)S(1)} %get-tuple-element.21.refs_1_.refs_3_, ...), custom_call_target="tpu_custom_call" | custom-call | tf_op jit(solution)/shard_map/stage_field/pallas_call | solution.py:511

commit v8 on v7

--- a/solution.py
+++ b/solution.py
@@ -55,16 +55,22 @@
     lead, e, couple = edge_tables(n, members, np.pi * k / (2 * n))
     vec = np.zeros((8, n))
     vec[0], vec[1], vec[2], vec[3], vec[4] = q0, q1, lead, e, couple
-    m = np.arange(half)
-    cls = np.arange(2 * members)
-    kap = cls[:, None] + 2 * members * m[None]
+    lane = np.arange(half)
+    other = np.where(lane == 0, half, lane)
+    d = np.arange(members)
+    kap = np.concatenate(
+        [
+            d[:, None] + 2 * members * lane[None],
+            2 * members * other[None] - np.where(d == 0, members, d)[:, None],
+        ]
+    )
     glob = np.stack(edge_tables(n, members, np.pi * kap / (2 * total)))
     bend = 1 + glob[1] ** 2 - 2 * glob[1] * np.cos(np.pi * np.arange(1, members) / members)[:, None, None]
     size = np.full((2 * members, half), 1 / np.sqrt(members))
-    size[1:, 0] *= np.sqrt(2)
+    size[1:members, 0] *= np.sqrt(2)
     dens = (glob[0] * size / bend).reshape(-1, half)
     j = 2 * np.arange(n) + 1
-    sb = np.sqrt(2 / n) * np.sin(np.pi * m[:, None] * j[None] / n)
+    sb = np.sqrt(2 / n) * np.sin(np.pi * other[:, None] * j[None] / n)
     turn = np.concatenate([q[:half].T, sb.T], 0)
     sp = np.sqrt(2 / n) * s[:, None] * np.sin(np.pi * k[:, None] * (np.arange(n)[None] + 1) / n)
     sp[:, n - 1] = 0
@@ -73,13 +79,15 @@
     den[0, 0] = 1
     r = 1 / den
     r[0, 0] = 0
-    ang = np.pi * cls[:, None] * j[None] / (2 * total)
-    acs = np.concatenate([np.cos(ang), np.sin(ang)], 0)
+    ang = np.pi * np.arange(members + 1)[:, None] * j[None] / (2 * total)
+    ca, sa = np.cos(ang), np.sin(ang)
+    swap = np.concatenate([sa[members:], ca[1:members]], 0)
+    acs = np.concatenate([ca[:members], sa[:members], swap, np.repeat(ca[members:], members, 0)], 0)
     p = np.arange(members)
-    wang = np.pi * cls[:, None] * p[None] / members
+    wang = np.pi * np.arange(members + 1)[:, None] * p[None] / members
     wc, ws = np.cos(wang), np.sin(wang)
-    wfwd = np.concatenate([wc, ws], 0)
-    winv = np.concatenate([wc.T, -ws.T], 1)
+    wfwd = np.concatenate([wc[:members], wc[members:], ws[1:members]], 0)
+    winv = np.concatenate([wc[:members], wc[members:], -ws[1:members]], 0).T
     M = members
     t = np.arange(1, M)
     st = np.sqrt(2 / M) * np.sin(np.pi * np.outer(t, t) / M)
@@ -109,7 +117,7 @@
     kh = acc @ (keep @ (-(1 + 2 * a0) * np.eye(M) + b0 * up + b0 * up.T))
     s2x = s2.copy()
     s2x[M - 1, M - 1] = 1
-    per = min(M, n // (2 * M), 256 // (4 * M))
+    per = min(M, 256 // (2 * M))
     wbd = np.kron(np.eye(per), winv)
     minv = np.zeros((M, M, n))
     lean = lead / (1 + e * e - 2 * e * np.cos(np.pi * t / M)[:, None])
@@ -255,11 +263,12 @@
     m1 = dot3(
         jnp.concatenate([get("x0"), get("x1")], 0), (get("q1"), get("q2")), 1, 1
     )
-    wait("y", "s1", "s2", "r", "v", "col")
+    wait("y")
     n = m1.shape[0]
     half = n // 2
     L = min(n, 128)
     n2 = dot3((get("q1"), get("q2")), get("y"))
+    wait("s1", "s2", "r", "v", "col")
     ss = (get("s1"), get("s2"))
     f = dot3(ss, m1) + dot3(n2, ss, 1, 1)
     gyl = n2[:, n - L :].T[L - 1 :]
@@ -286,10 +295,10 @@
     return to_peers([alpha, tk[0:1], beta, low], M), u
 
 
-WAVES = {None: ("q1", "x0", "x1", "q2"), "x0": ("y", "s1", "s2", "r", "v", "col")}
-WAVES["s2"] = ("vec", "wide", "turn", "w", "thin", "long", "mats", "kmats")
-NAMES = WAVES[None] + WAVES["x0"] + WAVES["s2"]
-KEPT = ("q1", "q2", "r") + WAVES["s2"]
+WAVES = {None: ("q1", "x0", "x1", "q2"), "q1": ("y",), "x0": ("s1", "s2"), "x1": ("r", "v", "col")}
+WAVES["y"] = ("vec", "wide", "turn", "w", "thin", "long", "mats", "kmats")
+NAMES = sum(WAVES.values(), ())
+KEPT = ("q1", "q2", "r") + WAVES["y"]
 
 
 def run_local(members, arrays):
@@ -334,7 +343,7 @@
         edges[...], u[...] = stage_local(
             lax.axis_index("row"), lax.axis_index("col"), members, wait, get
         )
-        wait(*WAVES["s2"])
+        wait(*WAVES["y"])
 
     operands = [name if name not in ("x0", "x1") else "x" for name in NAMES]
     far, vmem, near = pl.BlockSpec(memory_space=pltpu.HBM), pl.BlockSpec(memory_space=pltpu.VMEM), pltpu.VMEM
@@ -382,19 +391,35 @@
 
     qs = (q1[...], q2[...])
     y = dot6(jnp.concatenate([tau1, tau0], 0), qs + (wide[:n, :],))
-    ca, sna = acs[0 : 2 * M, :], acs[2 * M : 4 * M, :]
-    g = dotk(kmats[4 * M : 8 * M, :], jnp.concatenate([y[:M], y[M:]], 1))
-    turned = []
+    ca, sna, swap, c16 = (acs[a * M : (a + 1) * M, :] for a in range(4))
+    c16 = c16[:1]
+    g = dotk(kmats[4 * M : 6 * M, :], jnp.concatenate([y[:M], y[M:]], 1))
+    xs, ys, extra = [], [], []
     for side in range(2):
-        C, S = (g[k * 2 * M : (k + 1) * 2 * M, side * n : (side + 1) * n] for k in range(2))
-        turned.append(jnp.concatenate([C * ca - S * sna, -(C * sna + S * ca)], 1))
-    T = dot6(jnp.concatenate(turned, 0), tuple(turn[2 * n * a : 2 * n * (a + 1), :] for a in range(3)))
+        C, S = (g[k * M : (k + 1) * M, side * n : (side + 1) * n] for k in range(2))
+        xs.append(C * ca - S * sna)
+        ys.append(C * sna + S * swap)
+        extra.append(S[:1] * c16)
+    xs += extra + [jnp.zeros((M - 2, n), f32)]
+    cosines = tuple(turn[2 * n * a : 2 * n * a + n, :] for a in range(3))
+    sines = tuple(turn[2 * n * a + n : 2 * n * (a + 1), :] for a in range(3))
+    xcos = dot6(jnp.concatenate(xs, 0), cosines)
+    ysin = dot6(jnp.concatenate(ys, 0), sines)
+    pair = (M, half)
+    left_lane, top_row = lanes_of(pair) == 0, rows_of(pair) == 0
     shape = (2 * M, half)
-    zeroth = lanes_of(shape) == 0
-    origin = (rows_of(shape) == 0) & zeroth
+    origin = (rows_of(shape) == 0) & (lanes_of(shape) == 0)
     root = 1.0 / math.sqrt(M)
-    scale = jnp.where(zeroth & (rows_of(shape) > 0), root * math.sqrt(2.0), root)
-    T1, T0 = T[: 2 * M] * scale, T[2 * M :] * scale
+    wider = (lanes_of(shape) == 0) & (rows_of(shape) > 0) & (rows_of(shape) < M)
+    scale = jnp.where(wider, root * math.sqrt(2.0), root)
+    ends = []
+    for side in range(2):
+        xc, yb = xcos[side * M : (side + 1) * M], ysin[side * M : (side + 1) * M]
+        plus = xc - jnp.where(left_lane | top_row, 0.0, yb)
+        alone = jnp.where(top_row, xcos[2 * M + side : 2 * M + side + 1], xc)
+        minus = jnp.where(left_lane, 0.0, alone) + yb
+        ends.append(jnp.concatenate([plus, minus], 0) * scale)
+    T1, T0 = ends
 
     own = rows_of((M, L)) == r
     alz = jnp.where(own, T1[:1, :1], 0.0)
@@ -410,18 +435,25 @@
         value = (up[m : m + 1] * T1c + down[m : m + 1] * T0) * thin[2 * M * m : 2 * M * (m + 1), :]
         modes.append(jnp.where(origin, g0[m : m + 1, :1] * root, value))
     modes.append(jnp.where(r == M - 1, T1, 0.0) * scale)
-    modes = split(jnp.concatenate(modes, 0))
-    XC = dot3s(modes, (qs[0][:half], qs[1][:half]))
-    XS = dot3s(modes, (b1, b2))
+    sums, gaps, single = [], [], []
+    for value in modes:
+        gp, gm = value[:M], value[M:]
+        sums.append(gp + jnp.where(left_lane | top_row, 0.0, gm))
+        gaps.append(jnp.where(top_row, gm, jnp.where(left_lane, 0.0, gp) - gm))
+        single.append(jnp.where(left_lane[:1], 0.0, gm[:1]))
+    XC = dot3s(split(jnp.concatenate(sums + single, 0)), (qs[0][:half], qs[1][:half]))
+    XS = dot3s(split(jnp.concatenate(gaps, 0)), (b1, b2))
     third = w.shape[0] // 3
     ws = tuple(w[third * a : third * (a + 1), :] for a in range(3))
-    group = w.shape[1] // (4 * M)
+    group = w.shape[1] // (2 * M)
     lines = []
+    top_line = rows_of((M, n)) == 0
     for first in range(0, M, group):
         rots = []
         for m in range(first, first + group):
-            xc, xs = XC[2 * M * m : 2 * M * (m + 1)], XS[2 * M * m : 2 * M * (m + 1)]
-            rots += [ca * xc - sna * xs, sna * xc + ca * xs]
+            xc, xs = XC[M * m : M * (m + 1)], XS[M * m : M * (m + 1)]
+            alone = jnp.where(top_line, c16 * XC[M * M + m : M * M + m + 1], 0.0)
+            rots += [ca * xc - sna * xs, sna * xc + swap * xs + alone]
         lines.append(dotl(ws, jnp.concatenate(rots, 0)))
     hx = doths(jnp.concatenate(lines, 0), qs)
     Y = dot3(jnp.concatenate([hx * v0, hx * v1], 0), rs)
@@ -565,7 +597,7 @@
         strip = exchange(edges, "col")
         share, keep = run_stage(
             stage_strip, members, [sent((members, 4, n + 128), f32), near((8, n), f32)],
-            strip, kept["q1"], kept["q2"], *(kept[name] for name in WAVES["s2"]),
+            strip, kept["q1"], kept["q2"], *(kept[name] for name in WAVES["y"]),
         )
         share = exchange(share, "row")
         return run_field(

time: 48.7 us -> 47.7 us (0.979)
  Pallas kernels: 14.8 us -> 13.7 us
    pallas_call x1, Pallas kernels: 5.62 us -> 4.81 us  [run_stage(): pl.pallas_call(kernel, out_shape=outs, in_specs=[vmem] * len(args), out_s...]
where the time goes in v8:
time: 47.7 us; the launch traced here: 47.5 us
  blocking collectives  33.7 us (71%)
  Pallas kernels  13.7 us (29%)
    all_to_all x2, blocking collectives, exchange(): return lax.all_to_all(values, axis, split_axis=0, concat_axis=0, tiled=True)  33.7 us
    pallas_call x1, Pallas kernels, run_local(): pl.pallas_call(kernel, out_shape=[jax.ShapeDtypeStruct((members, 4, n), f...  6.06 us
    pallas_call x1, Pallas kernels, run_stage(): pl.pallas_call(kernel, out_shape=outs, in_specs=[vmem] * len(args), out_s...  4.81 us
    pallas_call x1, Pallas kernels, run_field(): pl.pallas_call(kernel, out_shape=jax.ShapeDtypeStruct((n, n), f32), in_sp...  2.85 us

profile of v8, /device:TPU:1, one launch (start us, length us, event | category | flops | bytes accessed | tf_op | source)
XLA Modules:
  0.0 47.5 jit_solution(17633086329383501512)
XLA Ops:
  0.0 6.1 %stage_local.1 = (f32[16,4,512]{2,1,0:T(4,128)S(1)}, f32[512,512]{1,0:T(8,128)S(1)}, bf16[512,512]{1,0:T(8,128)(2,1)S(1)}, bf16[512,512]{1,0:T(8,128)(2,1)S(1)},...) custom-call(bf16[512,512]{1,0:T(8,128)(2,1)} %constant.36.clone.refs, ...), custom_call_target="tpu_custom_call" | custom-call | tf_op jit(solution)/shard_map/stage_local/pallas_call | solution.py:351
  6.1 17.4 %all_to_all.10.refs_0_ = f32[16,4,512]{2,1,0:T(4,128)S(1)} all-to-all(f32[16,4,512]{2,1,0:T(4,128)S(1)} %get-tuple-element.20), channel_id=1, replica_groups=mesh['row'=16,'col'=16] {'col'}, dimensions={0} | all-to-all | bytes 262144 | tf_op jit(solution)/shard_map/all_to_all | solution.py:588
  23.4 4.8 %stage_strip.1 = (f32[16,4,640]{2,1,0:T(4,128)S(1)}, f32[8,512]{1,0:T(8,128)S(1)}) custom-call(f32[16,4,512]{2,1,0:T(4,128)S(1)} %all_to_all.10.refs_0_, bf16[512,512]{1,0:T(8,128)(2,1)S(1)} %get-tuple-element.21.refs_1_.refs_3_, bf16[512,512]{1,0:T(8,128)(2,1)S(1)} %get-tuple-element.22.refs_2_.refs_4_, f32[8,512]{1,0:T(8,128)S(1)} %get-tuple-element.23.refs_3_.refs_6_, ...), custom_call_target="tpu_custom_call" | custom-call | tf_op jit(solution)/shard_map/stage_strip/pallas_call | solution.py:577
  28.3 16.4 %all_to_all.11.refs_0_ = f32[16,4,640]{2,1,0:T(4,128)S(1)} all-to-all(f32[16,4,640]{2,1,0:T(4,128)S(1)} %get-tuple-element.31), channel_id=1, replica_groups=mesh['row'=16,'col'=16] {'row'}, dimensions={0} | all-to-all | bytes 327680 | tf_op jit(solution)/shard_map/all_to_all | solution.py:588
  44.6 2.8 %stage_field.1 = f32[512,512]{1,0:T(8,128)} custom-call(f32[16,4,640]{2,1,0:T(4,128)S(1)} %all_to_all.11.refs_0_, f32[8,512]{1,0:T(8,128)S(1)} %get-tuple-element.32.refs_1_, f32[512,512]{1,0:T(8,128)S(1)} %get-tuple-element.33.refs_2_, bf16[512,512]{1,0:T(8,128)(2,1)S(1)} %get-tuple-element.21.refs_1_.refs_3_, ...), custom_call_target="tpu_custom_call" | custom-call | tf_op jit(solution)/shard_map/stage_field/pallas_call | solution.py:543

commit v9 on v8

--- a/solution.py
+++ b/solution.py
@@ -128,6 +128,10 @@
     mats[2 * M : 3 * M, :M] = ka.T * qq
     mats[3 * M : 4 * M, :M] = kt.T * qq
     mats[4 * M : 5 * M, :M] = (kh @ t1).T
+    step = (pp[:, None] >= pp[None]).astype(float)
+    blocks = (ka, kt, s2x @ step, kh @ step, s2x @ frac, kh @ frac, frac)
+    for a, block in enumerate(blocks):
+        mats[5 * M : 6 * M, a * M : a * M + block.shape[1]] = block
     kmats = np.zeros((8 * M, 384), jnp.bfloat16)
     row = 0
     for small in (hmat, np.concatenate([ka, kt, kh], 1), s2, s2x, wfwd):
@@ -235,7 +239,7 @@
     return mm(a[:, : 6 * b.shape[0]], stacked(b), 1, 0)
 
 
-def edge_solve(al, t0, couple, source, minv, kmats, special):
+def edge_solve(al, t0, couple, minv, mats, kmats):
     M, n = al.shape
     L = min(n, 128)
     last = rows_of((M, n)) == M - 1
@@ -245,12 +249,12 @@
     for p in range(M - 1):
         wp = w[p : p + 1] + tail if p == M - 2 else w[p : p + 1]
         H = H + minv[M * p : M * (p + 1), :] * wp
-    Hz = dotk(kmats[0:M, :], jnp.concatenate([al[:, :L], source], 0))
+    Hz = mats[5 * M : 6 * M, 6 * M : 6 * M + 1] * al[M - 1 :, :L]
     mean = dotk(kmats[M : 2 * M, :], jnp.concatenate([al[:, :L], t0[:, :L], Hz], 0))
     lane = lanes_of((M, L))
-    first = jnp.where((lane == 0) & special, Hz, H[:, :L])
+    first = jnp.where(lane == 0, Hz, H[:, :L])
     H = first if n == L else jnp.concatenate([first, H[:, L:]], 1)
-    return H, jnp.where(special, mean[:, :1], 0.0)
+    return H, mean[:, :1]
 
 
 def to_peers(rows, members):
@@ -263,12 +267,11 @@
     m1 = dot3(
         jnp.concatenate([get("x0"), get("x1")], 0), (get("q1"), get("q2")), 1, 1
     )
-    wait("y")
+    wait("y", "s1", "s2", "r", "v", "col")
     n = m1.shape[0]
     half = n // 2
     L = min(n, 128)
     n2 = dot3((get("q1"), get("q2")), get("y"))
-    wait("s1", "s2", "r", "v", "col")
     ss = (get("s1"), get("s2"))
     f = dot3(ss, m1) + dot3(n2, ss, 1, 1)
     gyl = n2[:, n - L :].T[L - 1 :]
@@ -295,7 +298,7 @@
     return to_peers([alpha, tk[0:1], beta, low], M), u
 
 
-WAVES = {None: ("q1", "x0", "x1", "q2"), "q1": ("y",), "x0": ("s1", "s2"), "x1": ("r", "v", "col")}
+WAVES = {None: ("q1", "x0", "x1", "q2", "y", "s1", "s2", "r", "v", "col")}
 WAVES["y"] = ("vec", "wide", "turn", "w", "thin", "long", "mats", "kmats")
 NAMES = sum(WAVES.values(), ())
 KEPT = ("q1", "q2", "r") + WAVES["y"]
@@ -377,10 +380,9 @@
     v0, v1, couple = vec[0:1], vec[1:2], vec[4:5]
     L = min(n, 128)
     qq = 1.0 / math.sqrt(n)
-    zero = jnp.zeros((M, L), f32)
     sa, stt = mats[:M, :M], mats[:M, M : 2 * M]
 
-    H, mean = edge_solve(al, t0, couple, zero, long, kmats, True)
+    H, mean = edge_solve(al, t0, couple, long, mats, kmats)
     rs = (r1, r2)
     Z = dot6(jnp.concatenate([H * v0, H * v1], 0), rs + (r3,))
     add0 = v0 * below(Z[:M]) - v1 * Z[:M]
@@ -421,13 +423,13 @@
         ends.append(jnp.concatenate([plus, minus], 0) * scale)
     T1, T0 = ends
 
-    own = rows_of((M, L)) == r
-    alz = jnp.where(own, T1[:1, :1], 0.0)
-    t0z = jnp.where(own, T0[:1, :1], 0.0)
-    src = jnp.where(own, al[M - 1 :, :1] * (1.0 / math.sqrt(M)), 0.0)
-    Hz = dotk(kmats[0:M, :], jnp.concatenate([alz, src], 0))
-    lift = dotk(kmats[M : 2 * M, :], jnp.concatenate([alz, t0z, Hz], 0))
-    g0 = jnp.where(rows_of((M, L)) == M - 1, Hz, dotk(kmats[2 * M : 3 * M, :], Hz))
+    edge = mats[5 * M : 6 * M, :]
+    src = al[M - 1 :, :1] * (1.0 / math.sqrt(M))
+    a15 = jnp.where(r == M - 1, T1[:1, :1], 0.0)
+    kac, ktc, gstep, hstep = (lane_pick(edge[:, a * M : (a + 1) * M], r) for a in range(4))
+    gfrac, hfrac = edge[:, 4 * M : 4 * M + 1], edge[:, 5 * M : 5 * M + 1]
+    lift = kac * T1[:1, :1] + ktc * T0[:1, :1] + hfrac * (a15 + src) - hstep * src
+    g0 = gfrac * (a15 + src) - gstep * src
     up, down = lane_pick(sa, r), lane_pick(stt, r)
     T1c = jnp.where(r == M - 1, T1 * thin[2 * M * (M - 1) :, :], T1)
     modes = []

time: 47.7 us -> 47 us (0.985)
  Pallas kernels: 13.7 us -> 13.1 us
where the time goes in v9:
time: 47 us; the launch traced here: 46.8 us
  blocking collectives  33.7 us (72%)
  Pallas kernels  13.1 us (28%)
    all_to_all x2, blocking collectives, exchange(): return lax.all_to_all(values, axis, split_axis=0, concat_axis=0, tiled=True)  33.7 us
    pallas_call x1, Pallas kernels, run_local(): pl.pallas_call(kernel, out_shape=[jax.ShapeDtypeStruct((members, 4, n), f...  5.65 us
    pallas_call x1, Pallas kernels, run_stage(): pl.pallas_call(kernel, out_shape=outs, in_specs=[vmem] * len(args), out_s...  4.57 us
    pallas_call x1, Pallas kernels, run_field(): pl.pallas_call(kernel, out_shape=jax.ShapeDtypeStruct((n, n), f32), in_sp...  2.85 us

profile of v9, /device:TPU:1, one launch (start us, length us, event | category | flops | bytes accessed | tf_op | source)
XLA Modules:
  0.0 46.8 jit_solution(2933364253252553714)
XLA Ops:
  0.0 5.7 %stage_local.1 = (f32[16,4,512]{2,1,0:T(4,128)S(1)}, f32[512,512]{1,0:T(8,128)S(1)}, bf16[512,512]{1,0:T(8,128)(2,1)S(1)}, bf16[512,512]{1,0:T(8,128)(2,1)S(1)},...) custom-call(bf16[512,512]{1,0:T(8,128)(2,1)} %constant.36.clone.refs, ...), custom_call_target="tpu_custom_call" | custom-call | tf_op jit(solution)/shard_map/stage_local/pallas_call | solution.py:354
  5.7 17.4 %all_to_all.10.refs_0_ = f32[16,4,512]{2,1,0:T(4,128)S(1)} all-to-all(f32[16,4,512]{2,1,0:T(4,128)S(1)} %get-tuple-element.20), channel_id=1, replica_groups=mesh['row'=16,'col'=16] {'col'}, dimensions={0} | all-to-all | bytes 262144 | tf_op jit(solution)/shard_map/all_to_all | solution.py:590
  23.0 4.6 %stage_strip.1 = (f32[16,4,640]{2,1,0:T(4,128)S(1)}, f32[8,512]{1,0:T(8,128)S(1)}) custom-call(f32[16,4,512]{2,1,0:T(4,128)S(1)} %all_to_all.10.refs_0_, bf16[512,512]{1,0:T(8,128)(2,1)S(1)} %get-tuple-element.21.refs_1_.refs_3_, bf16[512,512]{1,0:T(8,128)(2,1)S(1)} %get-tuple-element.22.refs_2_.refs_4_, f32[8,512]{1,0:T(8,128)S(1)} %get-tuple-element.23.refs_3_.refs_6_, ...), custom_call_target="tpu_custom_call" | custom-call | tf_op jit(solution)/shard_map/stage_strip/pallas_call | solution.py:579
  27.6 16.4 %all_to_all.11.refs_0_ = f32[16,4,640]{2,1,0:T(4,128)S(1)} all-to-all(f32[16,4,640]{2,1,0:T(4,128)S(1)} %get-tuple-element.31), channel_id=1, replica_groups=mesh['row'=16,'col'=16] {'row'}, dimensions={0} | all-to-all | bytes 327680 | tf_op jit(solution)/shard_map/all_to_all | solution.py:590
  44.0 2.8 %stage_field.1 = f32[512,512]{1,0:T(8,128)} custom-call(f32[16,4,640]{2,1,0:T(4,128)S(1)} %all_to_all.11.refs_0_, f32[8,512]{1,0:T(8,128)S(1)} %get-tuple-element.32.refs_1_, f32[512,512]{1,0:T(8,128)S(1)} %get-tuple-element.33.refs_2_, bf16[512,512]{1,0:T(8,128)(2,1)S(1)} %get-tuple-element.21.refs_1_.refs_3_, ...), custom_call_target="tpu_custom_call" | custom-call | tf_op jit(solution)/shard_map/stage_field/pallas_call | solution.py:545

commit v10 on v9

--- a/solution.py
+++ b/solution.py
@@ -443,8 +443,8 @@
         sums.append(gp + jnp.where(left_lane | top_row, 0.0, gm))
         gaps.append(jnp.where(top_row, gm, jnp.where(left_lane, 0.0, gp) - gm))
         single.append(jnp.where(left_lane[:1], 0.0, gm[:1]))
-    XC = dot3s(split(jnp.concatenate(sums + single, 0)), (qs[0][:half], qs[1][:half]))
-    XS = dot3s(split(jnp.concatenate(gaps, 0)), (b1, b2))
+    XC = dot3(split(jnp.concatenate(sums + single, 0)), (qs[0][:half], qs[1][:half]))
+    XS = dot3(split(jnp.concatenate(gaps, 0)), (b1, b2))
     third = w.shape[0] // 3
     ws = tuple(w[third * a : third * (a + 1), :] for a in range(3))
     group = w.shape[1] // (2 * M)
@@ -458,8 +458,12 @@
             rots += [ca * xc - sna * xs, sna * xc + swap * xs + alone]
         lines.append(dotl(ws, jnp.concatenate(rots, 0)))
     hx = doths(jnp.concatenate(lines, 0), qs)
-    Y = dot3(jnp.concatenate([hx * v0, hx * v1], 0), rs)
-    Y0, Y1 = Y[: M * M], Y[M * M :]
+    Y0, Y1 = [], []
+    for rows in (slice(0, M * M // 2), slice(M * M // 2, M * M)):
+        Y = dot3(jnp.concatenate([hx[rows] * v0, hx[rows] * v1], 0), rs)
+        Y0.append(Y[: M * M // 2])
+        Y1.append(Y[M * M // 2 :])
+    Y0, Y1 = jnp.concatenate(Y0, 0), jnp.concatenate(Y1, 0)
 
     first = lanes_of((1, n)) == 0
     cols = []

time: 47 us -> 46.9 us (level)
  no operation moved by 1% of the time
where the time goes in v10:
time: 46.9 us; the launch traced here: 46.7 us
  blocking collectives  33.7 us (72%)
  Pallas kernels  13 us (28%)
    all_to_all x2, blocking collectives, exchange(): return lax.all_to_all(values, axis, split_axis=0, concat_axis=0, tiled=True)  33.7 us
    pallas_call x1, Pallas kernels, run_local(): pl.pallas_call(kernel, out_shape=[jax.ShapeDtypeStruct((members, 4, n), f...  5.65 us
    pallas_call x1, Pallas kernels, run_stage(): pl.pallas_call(kernel, out_shape=outs, in_specs=[vmem] * len(args), out_s...  4.47 us
    pallas_call x1, Pallas kernels, run_field(): pl.pallas_call(kernel, out_shape=jax.ShapeDtypeStruct((n, n), f32), in_sp...  2.85 us

profile of v10, /device:TPU:1, one launch (start us, length us, event | category | flops | bytes accessed | tf_op | source)
XLA Modules:
  0.0 46.7 jit_solution(4437602784112474527)
XLA Ops:
  0.0 5.7 %stage_local.1 = (f32[16,4,512]{2,1,0:T(4,128)S(1)}, f32[512,512]{1,0:T(8,128)S(1)}, bf16[512,512]{1,0:T(8,128)(2,1)S(1)}, bf16[512,512]{1,0:T(8,128)(2,1)S(1)},...) custom-call(bf16[512,512]{1,0:T(8,128)(2,1)} %constant.36.clone.refs, ...), custom_call_target="tpu_custom_call" | custom-call | tf_op jit(solution)/shard_map/stage_local/pallas_call | solution.py:354
  5.7 17.4 %all_to_all.10.refs_0_ = f32[16,4,512]{2,1,0:T(4,128)S(1)} all-to-all(f32[16,4,512]{2,1,0:T(4,128)S(1)} %get-tuple-element.20), channel_id=1, replica_groups=mesh['row'=16,'col'=16] {'col'}, dimensions={0} | all-to-all | bytes 262144 | tf_op jit(solution)/shard_map/all_to_all | solution.py:594
  23.0 4.5 %stage_strip.1 = (f32[16,4,640]{2,1,0:T(4,128)S(1)}, f32[8,512]{1,0:T(8,128)S(1)}) custom-call(f32[16,4,512]{2,1,0:T(4,128)S(1)} %all_to_all.10.refs_0_, bf16[512,512]{1,0:T(8,128)(2,1)S(1)} %get-tuple-element.21.refs_1_.refs_3_, bf16[512,512]{1,0:T(8,128)(2,1)S(1)} %get-tuple-element.22.refs_2_.refs_4_, f32[8,512]{1,0:T(8,128)S(1)} %get-tuple-element.23.refs_3_.refs_6_, ...), custom_call_target="tpu_custom_call" | custom-call | tf_op jit(solution)/shard_map/stage_strip/pallas_call | solution.py:583
  27.5 16.4 %all_to_all.11.refs_0_ = f32[16,4,640]{2,1,0:T(4,128)S(1)} all-to-all(f32[16,4,640]{2,1,0:T(4,128)S(1)} %get-tuple-element.31), channel_id=1, replica_groups=mesh['row'=16,'col'=16] {'row'}, dimensions={0} | all-to-all | bytes 327680 | tf_op jit(solution)/shard_map/all_to_all | solution.py:594
  43.9 2.8 %stage_field.1 = f32[512,512]{1,0:T(8,128)} custom-call(f32[16,4,640]{2,1,0:T(4,128)S(1)} %all_to_all.11.refs_0_, f32[8,512]{1,0:T(8,128)S(1)} %get-tuple-element.32.refs_1_, f32[512,512]{1,0:T(8,128)S(1)} %get-tuple-element.33.refs_2_, bf16[512,512]{1,0:T(8,128)(2,1)S(1)} %get-tuple-element.21.refs_1_.refs_3_, ...), custom_call_target="tpu_custom_call" | custom-call | tf_op jit(solution)/shard_map/stage_field/pallas_call | solution.py:549

commit v11 on v10

--- a/solution.py
+++ b/solution.py
@@ -501,6 +501,9 @@
     return share, jnp.concatenate(keep + [jnp.zeros((5, n), f32)], 0)
 
 
+CUTS = (0, 6, 8)
+
+
 def stage_field(r, c, M, share, keep, u, qh, ql, rr, vec):
     keep, vec = keep[...], vec[...]
     n = vec.shape[1]
@@ -521,9 +524,8 @@
     un = jnp.where((rows_of(un.shape) == 0) & (lanes_of(un.shape) == 0), level, un)
     qs = (qh[...], ql[...])
     half = split(dot3(un, qs))
-    step = n // 4
-    for part in range(4):
-        cols = slice(part * step, (part + 1) * step)
+    for first, last in zip(CUTS, CUTS[1:]):
+        cols = slice(first * n // 8, last * n // 8)
         yield dot3((qs[0][:, cols], qs[1][:, cols]), half, 0, 0)
 
 
@@ -537,8 +539,7 @@
         field, rows, sem = refs[len(args) :]
         copies = []
         for part, value in enumerate(stage_field(*place(), members, *refs[: len(args)])):
-            step = value.shape[0]
-            span = slice(part * step, (part + 1) * step)
+            span = slice(CUTS[part] * n // 8, CUTS[part + 1] * n // 8)
             rows[span, :] = value
             copies.append(pltpu.make_async_copy(rows.at[span], field.at[span], sem.at[part]))
             copies[-1].start()
@@ -551,7 +552,7 @@
         out_shape=jax.ShapeDtypeStruct((n, n), f32),
         in_specs=[vmem] * len(args),
         out_specs=pl.BlockSpec(memory_space=pltpu.HBM),
-        scratch_shapes=[pltpu.VMEM((n, n), f32), pltpu.SemaphoreType.DMA((4,))],
+        scratch_shapes=[pltpu.VMEM((n, n), f32), pltpu.SemaphoreType.DMA((len(CUTS) - 1,))],
         compiler_params=pltpu.CompilerParams(vmem_limit_bytes=VMEM_LIMIT),
         name="stage_field",
     )(*args)

time: 46.9 us -> 46.9 us (level)
  no operation moved by 1% of the time
where the time goes in v11:
time: 46.9 us; the launch traced here: 46.7 us
  blocking collectives  33.7 us (72%)
  Pallas kernels  13 us (28%)
    all_to_all x2, blocking collectives, exchange(): return lax.all_to_all(values, axis, split_axis=0, concat_axis=0, tiled=True)  33.7 us
    pallas_call x1, Pallas kernels, run_local(): pl.pallas_call(kernel, out_shape=[jax.ShapeDtypeStruct((members, 4, n), f...  5.65 us
    pallas_call x1, Pallas kernels, run_stage(): pl.pallas_call(kernel, out_shape=outs, in_specs=[vmem] * len(args), out_s...  4.47 us
    pallas_call x1, Pallas kernels, run_field(): pl.pallas_call(kernel, out_shape=jax.ShapeDtypeStruct((n, n), f32), in_sp...  2.83 us

profile of v11, /device:TPU:1, one launch (start us, length us, event | category | flops | bytes accessed | tf_op | source)
XLA Modules:
  0.0 46.7 jit_solution(1463344528299306648)
XLA Ops:
  0.0 5.7 %stage_local.1 = (f32[16,4,512]{2,1,0:T(4,128)S(1)}, f32[512,512]{1,0:T(8,128)S(1)}, bf16[512,512]{1,0:T(8,128)(2,1)S(1)}, bf16[512,512]{1,0:T(8,128)(2,1)S(1)},...) custom-call(bf16[512,512]{1,0:T(8,128)(2,1)} %constant.36.clone.refs, ...), custom_call_target="tpu_custom_call" | custom-call | tf_op jit(solution)/shard_map/stage_local/pallas_call | solution.py:354
  5.7 17.4 %all_to_all.10.refs_0_ = f32[16,4,512]{2,1,0:T(4,128)S(1)} all-to-all(f32[16,4,512]{2,1,0:T(4,128)S(1)} %get-tuple-element.20), channel_id=1, replica_groups=mesh['row'=16,'col'=16] {'col'}, dimensions={0} | all-to-all | bytes 262144 | tf_op jit(solution)/shard_map/all_to_all | solution.py:595
  23.0 4.5 %stage_strip.1 = (f32[16,4,640]{2,1,0:T(4,128)S(1)}, f32[8,512]{1,0:T(8,128)S(1)}) custom-call(f32[16,4,512]{2,1,0:T(4,128)S(1)} %all_to_all.10.refs_0_, bf16[512,512]{1,0:T(8,128)(2,1)S(1)} %get-tuple-element.21.refs_1_.refs_3_, bf16[512,512]{1,0:T(8,128)(2,1)S(1)} %get-tuple-element.22.refs_2_.refs_4_, f32[8,512]{1,0:T(8,128)S(1)} %get-tuple-element.23.refs_3_.refs_6_, ...), custom_call_target="tpu_custom_call" | custom-call | tf_op jit(solution)/shard_map/stage_strip/pallas_call | solution.py:584
  27.5 16.4 %all_to_all.11.refs_0_ = f32[16,4,640]{2,1,0:T(4,128)S(1)} all-to-all(f32[16,4,640]{2,1,0:T(4,128)S(1)} %get-tuple-element.31), channel_id=1, replica_groups=mesh['row'=16,'col'=16] {'row'}, dimensions={0} | all-to-all | bytes 327680 | tf_op jit(solution)/shard_map/all_to_all | solution.py:595
  43.9 2.8 %stage_field.1 = f32[512,512]{1,0:T(8,128)} custom-call(f32[16,4,640]{2,1,0:T(4,128)S(1)} %all_to_all.11.refs_0_, f32[8,512]{1,0:T(8,128)S(1)} %get-tuple-element.32.refs_1_, f32[512,512]{1,0:T(8,128)S(1)} %get-tuple-element.33.refs_2_, bf16[512,512]{1,0:T(8,128)(2,1)S(1)} %get-tuple-element.21.refs_1_.refs_3_, ...), custom_call_target="tpu_custom_call" | custom-call | tf_op jit(solution)/shard_map/stage_field/pallas_call | solution.py:550

commit v12 on v11

--- a/solution.py
+++ b/solution.py
@@ -273,7 +273,12 @@
     L = min(n, 128)
     n2 = dot3((get("q1"), get("q2")), get("y"))
     ss = (get("s1"), get("s2"))
-    f = dot3(ss, m1) + dot3(n2, ss, 1, 1)
+    m1s, n2s = split(m1), split(n2)
+    st = tuple(piece.T for piece in ss)
+    f = dot3(
+        tuple(jnp.concatenate([a, b], 1) for a, b in zip(ss, n2s)),
+        tuple(jnp.concatenate([a, b], 0) for a, b in zip(m1s, st)),
+    )
     gyl = n2[:, n - L :].T[L - 1 :]
     u = -f * get("r")
     uh, ul = split(u)

time: 46.9 us -> 46.9 us (level)
  no operation moved by 1% of the time
where the time goes in v12:
time: 46.9 us; the launch traced here: 46.7 us
  blocking collectives  33.7 us (72%)
  Pallas kernels  13 us (28%)
    all_to_all x2, blocking collectives, exchange(): return lax.all_to_all(values, axis, split_axis=0, concat_axis=0, tiled=True)  33.7 us
    pallas_call x1, Pallas kernels, run_local(): pl.pallas_call(kernel, out_shape=[jax.ShapeDtypeStruct((members, 4, n), f...  5.65 us
    pallas_call x1, Pallas kernels, run_stage(): pl.pallas_call(kernel, out_shape=outs, in_specs=[vmem] * len(args), out_s...  4.48 us
    pallas_call x1, Pallas kernels, run_field(): pl.pallas_call(kernel, out_shape=jax.ShapeDtypeStruct((n, n), f32), in_sp...  2.83 us

profile of v12, /device:TPU:1, one launch (start us, length us, event | category | flops | bytes accessed | tf_op | source)
XLA Modules:
  0.0 46.7 jit_solution(11102174578529450342)
XLA Ops:
  0.0 5.7 %stage_local.1 = (f32[16,4,512]{2,1,0:T(4,128)S(1)}, f32[512,512]{1,0:T(8,128)S(1)}, bf16[512,512]{1,0:T(8,128)(2,1)S(1)}, bf16[512,512]{1,0:T(8,128)(2,1)S(1)},...) custom-call(bf16[512,512]{1,0:T(8,128)(2,1)} %constant.36.clone.refs, ...), custom_call_target="tpu_custom_call" | custom-call | tf_op jit(solution)/shard_map/stage_local/pallas_call | solution.py:359
  5.7 17.4 %all_to_all.10.refs_0_ = f32[16,4,512]{2,1,0:T(4,128)S(1)} all-to-all(f32[16,4,512]{2,1,0:T(4,128)S(1)} %get-tuple-element.20), channel_id=1, replica_groups=mesh['row'=16,'col'=16] {'col'}, dimensions={0} | all-to-all | bytes 262144 | tf_op jit(solution)/shard_map/all_to_all | solution.py:600
  23.0 4.5 %stage_strip.1 = (f32[16,4,640]{2,1,0:T(4,128)S(1)}, f32[8,512]{1,0:T(8,128)S(1)}) custom-call(f32[16,4,512]{2,1,0:T(4,128)S(1)} %all_to_all.10.refs_0_, bf16[512,512]{1,0:T(8,128)(2,1)S(1)} %get-tuple-element.21.refs_1_.refs_3_, bf16[512,512]{1,0:T(8,128)(2,1)S(1)} %get-tuple-element.22.refs_2_.refs_4_, f32[8,512]{1,0:T(8,128)S(1)} %get-tuple-element.23.refs_3_.refs_6_, ...), custom_call_target="tpu_custom_call" | custom-call | tf_op jit(solution)/shard_map/stage_strip/pallas_call | solution.py:589
  27.5 16.4 %all_to_all.11.refs_0_ = f32[16,4,640]{2,1,0:T(4,128)S(1)} all-to-all(f32[16,4,640]{2,1,0:T(4,128)S(1)} %get-tuple-element.31), channel_id=1, replica_groups=mesh['row'=16,'col'=16] {'row'}, dimensions={0} | all-to-all | bytes 327680 | tf_op jit(solution)/shard_map/all_to_all | solution.py:600
  43.9 2.8 %stage_field.1 = f32[512,512]{1,0:T(8,128)} custom-call(f32[16,4,640]{2,1,0:T(4,128)S(1)} %all_to_all.11.refs_0_, f32[8,512]{1,0:T(8,128)S(1)} %get-tuple-element.32.refs_1_, f32[512,512]{1,0:T(8,128)S(1)} %get-tuple-element.33.refs_2_, bf16[512,512]{1,0:T(8,128)(2,1)S(1)} %get-tuple-element.21.refs_1_.refs_3_, ...), custom_call_target="tpu_custom_call" | custom-call | tf_op jit(solution)/shard_map/stage_field/pallas_call | solution.py:555
